TPU v7x, 32 devices: a whole 2x2x4 slice. The times are simulated.
32 devices in a mesh: mkt: 8 (over z, x), grp: 4 (over y, core).
Axes of the slice: x: 2, y: 2, z: 4, core: 2. Of those that a mesh axis runs over, the one named last changes fastest.
Arguments:
- mean_utility: float32 [512, 64], P(('mkt', 'grp')), may hold values from -5 to -1
- market_share: float32 [512, 64], P(('mkt', 'grp')), may hold values from 0.001 to 0.02
- product_traits: float32 [512, 64, 5], P(('mkt', 'grp')), may hold values from -1 to 1
- taste_draws: float32 [512, 5, 1024], P(('mkt', 'grp')), may hold values from -4 to 4
- taste_scale: float32 [5], replicated, may hold values from 0.3 to 1
- type_weight: float32 [512, 1024], P(('mkt', 'grp')), may hold values from 0.1 to 1
- market_size: float32 [512], P(('mkt', 'grp')), may hold values from 0.05 to 3
- product_firm: int32 [512, 64], P(('mkt', 'grp')), may hold values from 0 to 511, all different within a row
- firm_order: int32 [512], replicated, may hold values from 0 to 511, each once
- loyalty: float32 [512, 1024], P(('mkt', 'grp')), may hold values from -1 to 1
- firm_share: float32 [512, 1024], replicated, may hold values from 2e-05 to 0.15
Outputs:
- utility_out: float32 [512, 64], P(('mkt', 'grp'))
- loyalty_out: float32 [512, 1024], P(('mkt', 'grp'))
Inputs may be any that keep to these rules, and one draw needn't show every extreme that they name: `product_firm`: in each market the 64 products belong to 64 different firms, and every firm sells in some market. `firm_order`: each firm appears once.
All inputs are finite; a program needn't handle non-finite values.
Results may differ from a plain program's by a relative error of at most 0.0001.
Values sent between devices are 32-bit elements; how exact they have to be, the bound alone decides.
No kernel may reach another device: no remote copies, remote signals or barrier semaphores. Data moves between devices by JAX's collectives and lax.ppermute only.
A program may use at most 64 MiB of HBM per device.

v0:
```python
import jax
import jax.numpy as jnp
from jax import lax
from jax.sharding import PartitionSpec as P

ITERS = 3


clip_target = 0.5
norm_eps = 1e-06


def inverse_order(firm_order):
    count = firm_order.shape[0]
    return jnp.zeros((count,), jnp.int32).at[firm_order].set(jnp.arange(count, dtype=jnp.int32))


def market_terms(mean_now, taste, type_weight, mass, row_ids, table):
    expu = jnp.exp(mean_now[:, :, None] + taste + jnp.take(table, row_ids, axis=0))
    choice_prob = expu / (1.0 + jnp.sum(expu, axis=1, keepdims=True))
    weighted_sum = jnp.einsum(
        "mjr,mr->mj", choice_prob, type_weight, precision=lax.Precision.HIGHEST
    )
    weighted = choice_prob * mass[:, None, :]
    firm_count = table.shape[0]
    onehot = (
        jnp.arange(firm_count, dtype=jnp.int32)[:, None] == row_ids.reshape(-1)[None, :]
    ).astype(jnp.float32)
    partial_value = jnp.dot(
        onehot,
        weighted.reshape(-1, weighted.shape[2]),
        precision=lax.Precision.HIGHEST,
        preferred_element_type=jnp.float32,
    )
    return (weighted_sum, partial_value)


def local(
    mean_utility,
    market_share,
    product_traits,
    taste_draws,
    taste_scale,
    type_weight,
    market_size,
    product_firm,
    firm_order,
    loyalty,
    firm_share,
):
    firm_count = firm_share.shape[0]
    draw_count = firm_share.shape[1]
    owned_count = loyalty.shape[0]
    devices = lax.axis_size(("mkt", "grp"))
    inverse = inverse_order(firm_order)
    owner_rows = jnp.take(inverse, product_firm, axis=0)
    owned = loyalty
    my_firms = lax.dynamic_slice_in_dim(
        firm_order, lax.axis_index(("mkt", "grp")) * owned_count, owned_count
    )
    taste = jnp.einsum(
        "mjk,mkr->mjr", product_traits * taste_scale, taste_draws, precision=lax.Precision.HIGHEST
    )
    weight_total = jnp.sum(type_weight, axis=1)
    mass = market_size[:, None] * type_weight
    type_mass = lax.psum(jnp.sum(mass, axis=0), ("mkt", "grp"))
    log_observed = jnp.log(market_share)
    mean_now = mean_utility
    my_share = jnp.log(jnp.take(firm_share, my_firms, axis=0))
    for step in range(ITERS):
        table = lax.all_gather(owned, ("mkt", "grp"), axis=0, tiled=True)
        weighted_sum, by_owner = market_terms(mean_now, taste, type_weight, mass, owner_rows, table)
        predicted = weighted_sum / weight_total[:, None]
        blocks = by_owner.reshape(devices, owned_count, draw_count)
        received = lax.all_to_all(blocks, ("mkt", "grp"), split_axis=0, concat_axis=0, tiled=True)
        own_totals = jnp.sum(received, axis=0)
        gap = my_share - jnp.log(own_totals / type_mass[None, :])
        squares = lax.psum(jnp.sum(gap * gap), ("mkt", "grp"))
        clip = jnp.minimum(
            1.0, clip_target / jnp.sqrt(squares / (firm_count * draw_count) + norm_eps)
        )
        owned = owned + clip * gap
        mean_now = mean_now + log_observed - jnp.log(predicted)
    return (mean_now, owned)


def solution(mesh):
    placed = (
        P(("mkt", "grp"), None),
        P(("mkt", "grp"), None),
        P(("mkt", "grp"), None, None),
        P(("mkt", "grp"), None, None),
        P(),
        P(("mkt", "grp"), None),
        P(("mkt", "grp")),
        P(("mkt", "grp"), None),
        P(),
        P(("mkt", "grp"), None),
        P(),
    )
    return jax.shard_map(
        local,
        mesh=mesh,
        in_specs=placed,
        out_specs=(P(("mkt", "grp"), None), P(("mkt", "grp"), None)),
        check_vma=False,
    )
```

profile of v0, /device:TPU:0, one launch (start us, length us, event | category | flops | bytes accessed | tf_op | source)
XLA Modules:
  0.0 555.0 jit_solution(14951167932557971051)
XLA Ops:
  7.2 0.7 all-gather.4.cloned.1.call-update
  7.9 0.7 compare_select_fusion.1
  8.7 0.7 compare_select_fusion.2
  9.4 2.4 scatter_custom_fusion
  11.9 6.9 %gather_fusion = s32[1024]{0:T(1024)S(1)} fusion(s32[512]{0:T(512)S(1)} %scatter_custom_fusion, s32[1024]{0:T(1024)S(1)} %broadcast_clamp_fusion.1), kind=kCustom, calls=%fused_computation.3 | custom fusion | bytes 12288 | tf_op jit(solution)/shard_map/jit(_take)/gather | solution.py:56
  19.1 50.8 %all-gather.4.cloned.1.call-done = f32[512,1024]{1,0:T(8,128)} async-done(((f32[16,1024]{1,0:T(8,128)}), f32[512,1024]{1,0:T(8,128)}) %all-gather.4.cloned.1.call-update) | async-done | bytes 2097168 | tf_op jit(solution)/shard_map/all_gather | solution.py:71
  69.9 8.0 %gather_fusion.2 = f32[1024,1024]{1,0:T(8,128)} fusion(f32[512,1024]{1,0:T(8,128)} %all-gather.4.cloned.1.call-done, s32[1024]{0:T(1024)S(1)} %broadcast_clamp_fusion), kind=kCustom, calls=%fused_computation.clone | custom fusion | bytes 8392704 | tf_op jit(solution)/shard_map/jit(_take)/gather | solution.py:19
  77.9 7.5 %fusion.31 = (f32[16,1024]{1,0:T(8,128)S(1)}, f32[16,64,1024]{2,1,0:T(8,128)S(1)}, f32[16,64,1024]{2,1,0:T(8,128)}) fusion(f32[16,64,1024]{2,1,0:T(8,128)} %bitcast.24, pred[16,64]{1,0:T(8,128)(4,1)S(1)} %get-tuple-element.19, f32[16,64]{1,0:T(8,128)S(1)} %copy-done.11, f32[16,5,1024]{2,0,1:T(8,128)S(1)} %copy-done.4, ...), kind=kOutput, calls=%fused_computation.73 | convolution fusion | flops 67092480 | bytes 13001728 | tf_op jit(solution)/shard_map/mjk,mkr->mjr/dot_general | solution.py:61
  85.4 0.1 fusion.30
  85.6 1.0 broadcast_multiply_fusion.2
  86.5 1.3 copy-done.1
  87.8 5.0 fusion.7
  92.8 3.6 all-to-all-start
  96.5 0.8 compare_and_fusion.1
  97.3 0.6 gather_fusion.1
  97.9 67.7 %psum.28 = f32[1024]{0:T(1024)S(1)} all-reduce(f32[1024]{0:T(1024)S(1)} %get-tuple-element.15), channel_id=1, replica_groups=mesh['mkt'=8,'grp'=4] {'mkt','grp'}, use_global_device_ids=true, to_apply=%region_5.7 | all-reduce | flops 1024 | bytes 8192 | tf_op jit(solution)/shard_map/psum | solution.py:66
  165.5 1.7 reduce_sum.101
  167.2 0.7 multiply_reduce_fusion.2
  167.9 38.4 %psum.29 = f32[]{:T(128)} all-reduce(f32[]{:T(128)} %get-tuple-element.11), channel_id=1, replica_groups=mesh['mkt'=8,'grp'=4] {'mkt','grp'}, use_global_device_ids=true, to_apply=%region_7.9 | all-reduce | flops 1 | bytes 8 | tf_op jit(solution)/shard_map/psum | solution.py:78
  207.0 0.6 multiply_add_fusion.2
  207.7 0.2 all-gather.8.cloned.1.call-start
  208.0 5.5 fusion.9
  213.6 52.0 %all-gather.6.cloned.1.call-done = f32[512,1024]{1,0:T(8,128)} async-done(((f32[16,1024]{1,0:T(8,128)}), f32[512,1024]{1,0:T(8,128)}) %all-gather.6.cloned.1.call-update) | async-done | bytes 2097168 | tf_op jit(solution)/shard_map/all_gather | solution.py:71
  265.6 8.0 %gather_fusion.3 = f32[1024,1024]{1,0:T(8,128)} fusion(f32[512,1024]{1,0:T(8,128)} %all-gather.6.cloned.1.call-done, s32[1024]{0:T(1024)S(1)} %broadcast_clamp_fusion), kind=kCustom, calls=%fused_computation.1.clone | custom fusion | bytes 8392704 | tf_op jit(solution)/shard_map/jit(_take)/gather | solution.py:19
  273.6 4.0 fusion.28
  277.7 1.0 broadcast_multiply_fusion.1
  278.7 1.3 copy-done.2
  280.0 3.7 fusion.5
  283.7 52.0 %all_to_all.15 = f32[32,16,1024]{2,1,0:T(8,128)} all-to-all(f32[32,16,1024]{2,1,0:T(8,128)S(1)} %fusion.5), channel_id=1, replica_groups=mesh['mkt'=8,'grp'=4] {'mkt','grp'}, dimensions={0} | all-to-all | bytes 4194304 | tf_op jit(solution)/shard_map/all_to_all | solution.py:75
  335.8 1.7 reduce_sum.105
  337.5 0.7 multiply_reduce_fusion.1
  338.2 38.9 %psum.30 = f32[]{:T(128)} all-reduce(f32[]{:T(128)} %get-tuple-element.7), channel_id=1, replica_groups=mesh['mkt'=8,'grp'=4] {'mkt','grp'}, use_global_device_ids=true, to_apply=%region_11.13 | all-reduce | flops 1 | bytes 8 | tf_op jit(solution)/shard_map/psum | solution.py:78
  377.8 0.6 multiply_add_fusion.1
  378.5 5.5 fusion.10
  384.1 50.7 %all-gather.8.cloned.1.call-done = f32[512,1024]{1,0:T(8,128)} async-done(((f32[16,1024]{1,0:T(8,128)}), f32[512,1024]{1,0:T(8,128)}) %all-gather.8.cloned.1.call-update) | async-done | bytes 2097168 | tf_op jit(solution)/shard_map/all_gather | solution.py:71
  434.8 8.0 %gather_fusion.4 = f32[1024,1024]{1,0:T(8,128)} fusion(f32[512,1024]{1,0:T(8,128)} %all-gather.8.cloned.1.call-done, s32[1024]{0:T(1024)S(1)} %broadcast_clamp_fusion), kind=kCustom, calls=%fused_computation.2.clone | custom fusion | bytes 8392704 | tf_op jit(solution)/shard_map/jit(_take)/gather | solution.py:19
  442.8 4.1 fusion.26
  446.9 1.0 broadcast_multiply_fusion
  447.9 1.3 copy-done.3
  449.2 5.0 fusion.3
  454.2 3.6 all-to-all-start.2
  457.8 5.5 fusion.11
  463.4 0.7 log_subtract_fusion.3
  464.1 42.4 %all-to-all-done.2 = f32[32,16,1024]{2,1,0:T(8,128)} async-done(((f32[32,16,1024]{2,1,0:T(8,128)}), f32[32,16,1024]{2,1,0:T(8,128)}, u32[]{:S(2)}, u32[]{:S(2)}) %all-to-all-start.2) | async-done | bytes 2097184 | tf_op jit(solution)/shard_map/all_to_all | solution.py:75
  506.5 1.7 reduce_sum.108
  508.2 0.8 multiply_reduce_fusion
  509.0 38.3 %psum.31 = f32[]{:T(128)} all-reduce(f32[]{:T(128)} %get-tuple-element.3), channel_id=1, replica_groups=mesh['mkt'=8,'grp'=4] {'mkt','grp'}, use_global_device_ids=true, to_apply=%region_15.17 | all-reduce | flops 1 | bytes 8 | tf_op jit(solution)/shard_map/psum | solution.py:78
  547.9 0.6 multiply_add_fusion
  (48 shorter events, 0.8 us)
Async XLA Ops:
  7.2 90.1 %copy-start = (f32[512,1024]{1,0:T(8,128)S(1)}, f32[512,1024]{1,0:T(8,128)}, u32[]{:S(2)}) copy-start(f32[512,1024]{1,0:T(8,128)} %param.23) | copy-start | bytes 6291460
  7.2 62.7 %all-gather.4.cloned.1.call-start = ((), (), s32[]{:S(2)}) async-start(), calls=%async_computation.3 | async-start | bytes 2162688 | tf_op jit(solution)/shard_map/all_gather | solution.py:71
  11.8 7.0 %copy-start.12 = (s32[16,64]{1,0:T(8,128)S(1)}, s32[16,64]{1,0:T(8,128)}, u32[]{:S(2)}) copy-start(s32[16,64]{1,0:T(8,128)} %param.20) | copy-start | bytes 12292
  11.8 7.1 %copy-start.10 = (f32[16,64,5]{1,0,2:T(8,128)S(1)}, f32[16,64,5]{1,0,2:T(8,128)}, u32[]{:S(2)}) copy-start(f32[16,64,5]{1,0,2:T(8,128)} %param.15) | copy-start | bytes 61444
  11.9 7.1 %copy-start.13 = (f32[5]{0:T(128)S(1)}, f32[5]{0:T(128)}, u32[]{:S(2)}) copy-start(f32[5]{0:T(128)} %param.17) | copy-start | bytes 64
  19.1 58.8 %copy-start.4 = (f32[16,5,1024]{2,0,1:T(8,128)S(1)}, f32[16,5,1024]{2,0,1:T(8,128)}, u32[]{:S(2)}) copy-start(f32[16,5,1024]{2,0,1:T(8,128)} %param.16) | copy-start | bytes 983044
  19.1 58.8 %copy-start.11 = (f32[16,64]{1,0:T(8,128)S(1)}, f32[16,64]{1,0:T(8,128)}, u32[]{:S(2)}) copy-start(f32[16,64]{1,0:T(8,128)} %param.13) | copy-start | bytes 12292
  77.9 7.5 %copy-start.9 = (f32[16,1024]{1,0:T(8,128)S(1)}, f32[16,1024]{1,0:T(8,128)}, u32[]{:S(2)}) copy-start(f32[16,1024]{1,0:T(8,128)} %param.18) | copy-start | bytes 196612
  77.9 7.5 %copy-start.14 = (f32[16]{0:T(128)S(1)}, f32[16]{0:T(128)}, u32[]{:S(2)}) copy-start(f32[16]{0:T(128)} %param.19) | copy-start | bytes 196
  85.4 2.4 copy-start.1
  92.8 114.2 %copy-start.7 = (f32[16,1024]{1,0:T(8,128)S(1)}, f32[16,1024]{1,0:T(8,128)}, u32[]{:S(2)}) copy-start(f32[16,1024]{1,0:T(8,128)} %param.22) | copy-start | bytes 196612
  92.8 72.7 %all-to-all-start = ((f32[32,16,1024]{2,1,0:T(8,128)}), f32[32,16,1024]{2,1,0:T(8,128)}, u32[]{:S(2)}, u32[]{:S(2)}) async-start(f32[32,16,1024]{2,1,0:T(8,128)} %fusion.7), calls=%async_computation | async-start | bytes 4194304 | tf_op jit(solution)/shard_map/all_to_all | solution.py:75
  96.4 169.2 %all-gather.6.cloned.1.call-start = ((), (), s32[]{:S(2)}) async-start(), calls=%async_computation.4 | async-start | bytes 2162688 | tf_op jit(solution)/shard_map/all_gather | solution.py:71
  207.7 227.1 %all-gather.8.cloned.1.call-start = ((), (), s32[]{:S(2)}) async-start(), calls=%async_computation.5 | async-start | bytes 2162688 | tf_op jit(solution)/shard_map/all_gather | solution.py:71
  207.9 5.5 copy-start.8
  277.7 2.3 copy-start.2
  283.7 94.1 %copy-start.6 = (f32[16,1024]{1,0:T(8,128)S(1)}, f32[16,1024]{1,0:T(8,128)}, u32[]{:S(2)}) copy-start(f32[16,1024]{1,0:T(8,128)} %multiply_add_fusion.2) | copy-start | bytes 196612
  446.9 2.3 copy-start.3
  454.2 52.3 %all-to-all-start.2 = ((f32[32,16,1024]{2,1,0:T(8,128)}), f32[32,16,1024]{2,1,0:T(8,128)}, u32[]{:S(2)}, u32[]{:S(2)}) async-start(f32[32,16,1024]{2,1,0:T(8,128)} %fusion.3), calls=%async_computation.2 | async-start | bytes 4194304 | tf_op jit(solution)/shard_map/all_to_all | solution.py:75
  457.8 90.0 %copy-start.5 = (f32[16,1024]{1,0:T(8,128)S(1)}, f32[16,1024]{1,0:T(8,128)}, u32[]{:S(2)}) copy-start(f32[16,1024]{1,0:T(8,128)} %multiply_add_fusion.1) | copy-start | bytes 196612
Sparse Core Ops, SparseCore 0:
  10.8 58.9 all-gather.3
  207.8 57.7 all-gather.5
  378.6 56.1 all-gather.7
where the time goes:
time: 557 us; the launch traced here: 555 us
  blocking collectives  235 us (42%)
  waiting for transfers between devices  197 us (35%)
  local copies, waits for them, and re-layouts  38.1 us (7%)
  matrix products  37.9 us (7%)
  other arithmetic  23.5 us (4%)
  between operations  16 us (3%)
  starting transfers between devices  7.5 us (1%)
    all_gather x3, waiting for transfers between devices, local(): table = lax.all_gather(owned, ('mkt', 'grp'), axis=0, tiled=True)  154 us
    psum x3, blocking collectives, local(): squares = lax.psum(jnp.sum(gap * gap), ('mkt', 'grp'))  116 us
    psum x1, blocking collectives, local(): type_mass = lax.psum(jnp.sum(mass, axis=0), ('mkt', 'grp'))  67.7 us
    all_to_all x1, blocking collectives, local(): lax.all_to_all(blocks, ('mkt', 'grp'), split_axis=0, concat_axis=0, tiled...  52 us
    all_to_all x2, waiting for transfers between devices, local(): lax.all_to_all(blocks, ('mkt', 'grp'), split_axis=0, concat_axis=0, tiled...  42.4 us
    gather x3, local copies, waits for them, and re-layouts, market_terms(): jnp.take(table, row_ids, axis=0)  24 us
    dot_general x3, matrix products, market_terms(): jnp.einsum('mjr,mr->mj', choice_prob, type_weight, precision=lax.Precisio...  16.6 us
    dot_general x3, matrix products, market_terms(): jnp.dot(onehot, weighted.reshape(-1, weighted.shape[2]), precision=lax.Pr...  13.8 us
  transfers between devices with their start and end apart: 5, of which 4 were waited for; matrix products, arithmetic and copies ran while one was open for 5% of the time, Pallas kernels for 0%

commit v1 on v0

v1 whole, which is shorter than its diff:
```python
import functools

import jax
import jax.numpy as jnp
from jax import lax
from jax.experimental import pallas as pl
from jax.experimental.pallas import tpu as pltpu
from jax.sharding import PartitionSpec as P

ITERS = 3
LANES = 128
clip_target = 0.5
norm_eps = 1e-06
AXES = ("mkt", "grp")
BF = jnp.bfloat16
F32 = jnp.float32


class Plan:
    def __init__(self, devices, own_markets, products, traits, types, firms, own_firms):
        self.D = devices
        self.C = devices // 2
        self.M = own_markets
        self.J = products
        self.K = traits
        self.R = types
        self.F = firms
        self.own = own_firms
        self.RL = types // self.C
        self.hh = LANES // self.RL
        self.ii = own_markets // self.hh
        self.h = LANES // products
        self.i8 = own_markets // self.h
        self.g = self.i8 // self.ii
        self.ML = own_markets * self.C
        self.G = self.g * LANES
        self.FP = firms // self.hh
        self.ownp = -(-own_firms // self.hh) * self.hh
        self.oi = self.ownp // self.hh
        self.OR = self.C * self.oi
        self.s_draws = 0
        self.s_mass = self.s_draws + traits * self.ii
        self.s_traits = self.s_mass + self.ii
        self.s_firms = self.s_traits + traits * self.i8
        self.s_mean = self.s_firms + self.i8
        self.s_loy = self.s_mean + self.i8
        self.S = self.s_loy + self.oi
        self.S2 = self.i8 + 1
        self.S3 = self.i8 + 2 * self.oi + 1
        self.groups = [[2 * c + k for c in range(self.C)] for k in range(2)]
        self.swap = [(d, d ^ 1) for d in range(devices)]
        self.NR = max(LANES, 2 * self.RL)


VM = pl.BlockSpec(memory_space=pltpu.VMEM)


def call(kernel, outs, args, scratch=(), alias=None, vmem=48):
    return pl.pallas_call(
        kernel,
        out_shape=outs,
        in_specs=[VM] * len(args),
        out_specs=jax.tree.map(lambda _: VM, outs),
        scratch_shapes=list(scratch),
        input_output_aliases=alias or {},
        compiler_params=pltpu.CompilerParams(vmem_limit_bytes=vmem * 2**20),
    )(*args)


def sds(shape, dtype=F32):
    return jax.ShapeDtypeStruct(shape, dtype)


def block_mask(p, rows, b):
    lane = lax.broadcasted_iota(jnp.int32, (rows, LANES), 1)
    return lane // p.RL == b


def fold(p, x):
    total = x
    for b in range(1, p.hh):
        total = total + pltpu.roll(x, b * p.RL, 1)
    return total


def split3(x):
    a = x.astype(BF)
    rest = x - a.astype(F32)
    b = rest.astype(BF)
    c = (rest - b.astype(F32)).astype(BF)
    return a, b, c


def dot(a, b):
    return jnp.dot(a, b, preferred_element_type=F32)


def natural(p, src, dst, step, offset):
    for gi in range(p.g):
        for c in range(p.C):
            at = (gi * p.C + c) * p.ii
            dst[at : at + p.ii, :] = src[c * step + offset + gi * p.ii : c * step + offset + (gi + 1) * p.ii, :]


def turn(p, nat, store):
    for gi in range(p.g):
        turned = nat[gi * LANES : (gi + 1) * LANES, :].T
        for q in range(p.h):
            store(q * p.g + gi, turned[q * p.J : (q + 1) * p.J, :])


def firm_row(p, firms_t, j):
    return jnp.concatenate([firms_t[b, pl.ds(j, 1), :] for b in range(p.hh)], axis=1)


def pack_kernel(p, draws, mass, traits, firms, mean, loyalty, out):
    def by_type(x, section, rows, count):
        for t in range(p.R // LANES):
            tile = x[:, t * LANES : (t + 1) * LANES]
            for b in range(p.hh):
                c = t * p.hh + b
                value = None
                for q in range(p.hh):
                    shift = ((q - b) * p.RL) % LANES
                    moved = pltpu.roll(tile, shift, 1) if shift else tile
                    piece = moved[q * rows : (q + 1) * rows, :]
                    value = piece if value is None else jnp.where(block_mask(p, rows, q), piece, value)
                out[c * p.S + section : c * p.S + section + rows, :] = value

    for k in range(p.K):
        by_type(draws[k], p.s_draws + k * p.ii, p.ii, p.M)
    by_type(mass[...], p.s_mass, p.ii, p.M)
    by_type(loyalty[...], p.s_loy, p.oi, p.ownp)

    def copied(x, section):
        value = jnp.concatenate([x[q * p.i8 : (q + 1) * p.i8, :] for q in range(p.h)], axis=1)
        for c in range(p.C):
            out[c * p.S + section : c * p.S + section + p.i8, :] = value

    for k in range(p.K):
        copied(traits[k], p.s_traits + k * p.i8)
    copied(firms[...], p.s_firms)
    copied(mean[...], p.s_mean)


def prep_kernel(p, recv, taste, firms_t, mean_t, mass_t, mass_row, loy, nat, draws_t, traits_t):
    def typed(section, store):
        for c in range(p.C):
            nat[c * p.ii : (c + 1) * p.ii, :] = recv[c * p.S + section : c * p.S + section + p.ii, :]
        flat = nat[0:LANES, :]
        turned = flat.T
        for b in range(p.hh):
            store(b, turned[b * p.RL : (b + 1) * p.RL, :])
        return flat

    def put_mass(b, value):
        mass_t[:, b * LANES : (b + 1) * LANES] = value

    flat = typed(p.s_mass, put_mass)
    row = jnp.sum(flat, axis=0, keepdims=True)
    mass_row[...] = jnp.broadcast_to(fold(p, jnp.broadcast_to(row, (8, LANES))), (8, LANES))
    for k in range(p.K):

        def put_draws(b, value):
            draws_t[k, :, b * LANES : (b + 1) * LANES] = value

        typed(p.s_draws + k * p.ii, put_draws)

    def product(section, store):
        natural(p, recv, nat, p.S, section)
        turn(p, nat, store)

    def put_firms(b, value):
        firms_t[b] = value.astype(jnp.int32)

    def put_mean(b, value):
        mean_t[b] = value

    product(p.s_firms, put_firms)
    product(p.s_mean, put_mean)
    for k in range(p.K):

        def put_traits(b, value):
            traits_t[k, b] = value

        product(p.s_traits + k * p.i8, put_traits)
    for c in range(p.C):
        loy[c * p.oi : (c + 1) * p.oi, :] = recv[c * p.S + p.s_loy : c * p.S + p.s_loy + p.oi, :]

    def body(j, _):
        for b in range(p.hh):
            at = slice(b * LANES, (b + 1) * LANES)
            value = None
            for k in range(p.K):
                term = traits_t[k, b, pl.ds(j, 1), :] * draws_t[k, :, at]
                value = term if value is None else value + term
            taste[j, :, at] = value
        return 0

    lax.fori_loop(0, p.J, body, 0)


def table_kernel(p, mine, other, order, table):
    firm = lax.broadcasted_iota(jnp.int32, (p.F, p.OR), 0)
    total = jnp.zeros((p.F, LANES), F32)
    for s, ref in enumerate((mine, other)):
        pieces = split3(ref[...])
        for b in range(p.hh):
            hot = (firm == order[s * p.hh + b : s * p.hh + b + 1, :]).astype(BF)
            found = dot(hot, pieces[0]) + dot(hot, pieces[1]) + dot(hot, pieces[2])
            total = total + jnp.where(block_mask(p, p.F, b), found, 0.0)
    pack_table(p, fold(p, total), table)


def pack_table(p, full, out):
    value = full[0 : p.FP, :]
    for b in range(1, p.hh):
        value = jnp.where(block_mask(p, p.FP, b), full[b * p.FP : (b + 1) * p.FP, :], value)
    out[...] = value


def gather_kernel(p, packed, firms_t, out, tab):
    pieces = split3(packed[...].T)
    for b in range(p.hh):
        for q in range(3):
            tab[b, q * p.RL : (q + 1) * p.RL, :] = pieces[q][b * p.RL : (b + 1) * p.RL, :]

    def body(j, _):
        row = firm_row(p, firms_t, j)
        total = None
        for b in range(p.hh):
            firm = lax.broadcasted_iota(jnp.int32, (p.FP, p.ML), 0)
            hot = (firm == row - b * p.FP).astype(BF)
            term = dot(tab[b], hot)
            total = term if total is None else total + term
        out[j] = total[0 : p.RL] + total[p.RL : 2 * p.RL] + total[2 * p.RL : 3 * p.RL]
        return 0

    lax.fori_loop(0, p.J, body, 0, unroll=2)


def choice_body(p, utility_of, mass_t, parts, pred, expu, pred_t, base):
    for b in range(p.hh):
        at = slice(b * LANES, (b + 1) * LANES)

        def first(j, total):
            e = jnp.exp(utility_of(j, b, at))
            expu[j] = e
            return total + e

        total = lax.fori_loop(0, p.J, first, jnp.zeros((p.RL, LANES), F32), unroll=4)
        scale = mass_t[:, at] / (1.0 + total)

        def second(j, _):
            value = expu[j] * scale
            hi = value.astype(BF)
            parts[j, 0 : p.RL, at] = hi
            parts[j, p.RL : 2 * p.RL, at] = (value - hi.astype(F32)).astype(BF)
            if p.NR > 2 * p.RL:
                parts[j, 2 * p.RL :, at] = jnp.zeros((p.NR - 2 * p.RL, LANES), BF)
            pred_t[b, pl.ds(j, 1), :] = jnp.sum(value, axis=0, keepdims=True)
            return 0

        lax.fori_loop(0, p.J, second, 0, unroll=4)
    for gi in range(p.g):
        flat = jnp.concatenate([pred_t[q * p.g + gi] for q in range(p.h)], axis=0).T
        for c in range(p.C):
            pred[c * p.i8 + gi * p.ii : c * p.i8 + (gi + 1) * p.ii, :] = flat[c * p.ii : (c + 1) * p.ii, :]


def choice_first_kernel(p, taste, found, mean_t, mass_t, base, parts, pred, expu, pred_t):
    def utility_of(j, b, at):
        value = taste[j, :, at] + found[j, :, at]
        base[j, :, at] = value
        return value + mean_t[b, pl.ds(j, 1), :]

    choice_body(p, utility_of, mass_t, parts, pred, expu, pred_t, base)


def clip_of(p, squares):
    return jnp.minimum(1.0, clip_target / jnp.sqrt(squares / (p.F * p.R) + norm_eps))


def choice_next_kernel(p, base_in, found, recv, mass_t, base, parts, pred, clip, expu, pred_t, nat):
    natural(p, recv, nat, p.S2, 0)
    squares = recv[p.i8 : p.i8 + 1, :]
    for c in range(1, p.C):
        squares = squares + recv[c * p.S2 + p.i8 : c * p.S2 + p.i8 + 1, :]
    factor = clip_of(p, squares)
    clip[...] = jnp.broadcast_to(factor, (8, LANES))

    def put_mean(b, value):
        pred_t[b] = value

    turn(p, nat, put_mean)

    def utility_of(j, b, at):
        value = base_in[j, :, at] + factor * found[j, :, at]
        base[j, :, at] = value
        return value + pred_t[b, pl.ds(j, 1), :]

    choice_body(p, utility_of, mass_t, parts, pred, expu, pred_t, base)


def scatter_kernel(p, parts, firms_t, mass_row, out, acc):
    acc[...] = jnp.zeros_like(acc)
    firm = lax.broadcasted_iota(jnp.int32, (p.F, p.ML), 0)

    def body(j, _):
        value = None
        for u in range(2):
            hot = (firm == firm_row(p, firms_t, 2 * j + u)).astype(BF)
            term = lax.dot_general(hot, parts[2 * j + u], (((1,), (1,)), ((), ())), preferred_element_type=F32)
            value = term if value is None else value + term
        acc[...] += value
        return 0

    lax.fori_loop(0, p.J // 2, body, 0)
    pack_table(p, fold(p, acc[...]), out.at[0 : p.FP])
    out[p.FP : p.FP + 8, :] = mass_row[...]


def gap_of(p, mine, other, share):
    mass = mine[p.FP : p.FP + 1, :] + other[p.FP : p.FP + 1, :]
    totals = mine[0 : p.FP, :] + other[0 : p.FP, :]
    return jnp.log(share[...]) - jnp.log(totals / mass)


def squares_row(gap):
    rows = jnp.sum(gap * gap, axis=0, keepdims=True)
    return jnp.broadcast_to(jnp.sum(rows, axis=1, keepdims=True), (8, LANES))


def gap_kernel(p, mine, other, share, gap, squares):
    value = gap_of(p, mine, other, share)
    gap[...] = value
    squares[...] = squares_row(value)


def chunk_sum(p, recv, step, rows):
    total = recv[0:rows, :]
    for c in range(1, p.C):
        total = total + recv[c * step : c * step + rows, :]
    return total


def mean_kernel(p, recv, mean, log_share, mass_total, squares, mean_out, send):
    predicted = chunk_sum(p, recv, p.i8, p.i8) / mass_total[...]
    value = mean[...] + log_share[...] - jnp.log(predicted)
    mean_out[...] = value
    for c in range(p.C):
        send[c * p.S2 : c * p.S2 + p.i8, :] = value
        send[c * p.S2 + p.i8 : (c + 1) * p.S2, :] = squares[0:1, :]


def final_kernel(p, mine, other, share, table, gap0, gap1, clips, order, pred, send):
    gap = gap_of(p, mine, other, share)
    squares = squares_row(gap)
    base = table[...] + clips[0:1, :] * gap0[...] + clips[8:9, :] * gap1[...]
    rows = p.OR
    for n, value in enumerate((base, gap)):
        pieces = split3(value)
        picked = jnp.zeros((rows, LANES), F32)
        for o in range(p.hh):
            column = order[:, o : o + 1]
            total = jnp.zeros((rows, LANES), F32)
            for b in range(p.hh):
                firm = lax.broadcasted_iota(jnp.int32, (rows, p.FP), 1) + b * p.FP
                hot = (firm == column).astype(BF)
                found = dot(hot, pieces[0]) + dot(hot, pieces[1]) + dot(hot, pieces[2])
                total = total + jnp.where(block_mask(p, rows, b), found, 0.0)
            picked = jnp.where(block_mask(p, rows, o), fold(p, total), picked)
        at = p.i8 + n * p.oi
        for c in range(p.C):
            send[c * p.S3 + at : c * p.S3 + at + p.oi, :] = picked[c * p.oi : (c + 1) * p.oi, :]
    for c in range(p.C):
        send[c * p.S3 : c * p.S3 + p.i8, :] = pred[c * p.i8 : (c + 1) * p.i8, :]
        send[(c + 1) * p.S3 - 1 : (c + 1) * p.S3, :] = squares[0:1, :]


def out_kernel(p, recv, mean, log_share, mass_total, mean_out, loyalty_out):
    predicted = chunk_sum(p, recv, p.S3, p.i8) / mass_total[...]
    mean_out[...] = mean[...] + log_share[...] - jnp.log(predicted)
    squares = recv[p.S3 - 1 : p.S3, :]
    for c in range(1, p.C):
        squares = squares + recv[(c + 1) * p.S3 - 1 : (c + 1) * p.S3, :]
    clip = clip_of(p, squares)
    for t in range(p.R // LANES):
        values = []
        for b in range(p.hh):
            at = (t * p.hh + b) * p.S3 + p.i8
            values.append(recv[at : at + p.oi, :] + clip * recv[at + p.oi : at + 2 * p.oi, :])
        for o in range(p.hh):
            row = None
            for b in range(p.hh):
                shift = ((b - o) * p.RL) % LANES
                moved = pltpu.roll(values[b], shift, 1) if shift else values[b]
                row = moved if row is None else jnp.where(block_mask(p, p.oi, b), moved, row)
            loyalty_out[o * p.oi : (o + 1) * p.oi, t * LANES : (t + 1) * LANES] = row


def local(
    mean_utility,
    market_share,
    product_traits,
    taste_draws,
    taste_scale,
    type_weight,
    market_size,
    product_firm,
    firm_order,
    loyalty,
    firm_share,
):
    p = Plan(
        lax.axis_size(AXES),
        mean_utility.shape[0],
        mean_utility.shape[1],
        taste_scale.shape[0],
        firm_share.shape[1],
        firm_share.shape[0],
        loyalty.shape[0],
    )
    index = lax.axis_index(AXES)
    half, place = index % 2, index // 2

    def exchange(x):
        return lax.all_to_all(x, AXES, split_axis=0, concat_axis=0, tiled=True, axis_index_groups=p.groups)

    def swap(x):
        return lax.ppermute(x, AXES, p.swap)

    def kernel(fn, *args, **kwargs):
        return functools.partial(fn, p, *args, **kwargs)

    def packed_products(x):
        return x.reshape(p.h, p.i8, p.J).transpose(1, 0, 2).reshape(p.i8, LANES)

    mass = market_size[:, None] * type_weight
    mass_total = packed_products(jnp.broadcast_to(jnp.sum(mass, axis=1)[:, None], mean_utility.shape))
    log_share = packed_products(jnp.log(market_share))
    mean = packed_products(mean_utility)
    share = lax.dynamic_slice_in_dim(firm_share, place * p.RL, p.RL, axis=1)
    share = share.reshape(p.hh, p.FP, p.RL).transpose(1, 0, 2).reshape(p.FP, LANES)
    order = firm_order.reshape(p.C, 2, p.own)
    order = jnp.pad(order, ((0, 0), (0, 0), (0, p.ownp - p.own)), constant_values=-1)
    order = order.reshape(p.C, 2, p.hh, p.oi).transpose(1, 2, 0, 3).reshape(2, p.hh, p.OR)
    order_mine = lax.dynamic_index_in_dim(order, half, 0, keepdims=False)
    order_other = lax.dynamic_index_in_dim(order, 1 - half, 0, keepdims=False)
    order_rows = jnp.concatenate([order_mine, order_other], axis=0)
    order_columns = order_mine.T

    send = call(
        kernel(pack_kernel),
        sds((p.C * p.S, LANES)),
        (
            taste_draws.transpose(1, 0, 2),
            mass,
            product_traits.transpose(2, 0, 1) * taste_scale[:, None, None],
            product_firm.astype(F32),
            mean_utility,
            jnp.pad(loyalty, ((0, p.ownp - p.own), (0, 0))),
        ),
    )
    recv = exchange(send)
    taste, firms_t, mean_t, mass_t, mass_row, loy = call(
        kernel(prep_kernel),
        (
            sds((p.J, p.RL, p.ML)),
            sds((p.hh, p.J, LANES), jnp.int32),
            sds((p.hh, p.J, LANES)),
            sds((p.RL, p.ML)),
            sds((8, LANES)),
            sds((p.OR, LANES)),
        ),
        (recv,),
        scratch=(
            pltpu.VMEM((p.G, LANES), F32),
            pltpu.VMEM((p.K, p.RL, p.ML), F32),
            pltpu.VMEM((p.K, p.hh, p.J, LANES), F32),
        ),
    )
    table = call(kernel(table_kernel), sds((p.FP, LANES)), (loy, swap(loy), order_rows))

    def gather(packed):
        return call(
            kernel(gather_kernel),
            sds((p.J, p.RL, p.ML)),
            (packed, firms_t),
            scratch=(pltpu.VMEM((p.hh, 3 * p.RL, p.FP), BF),),
        )

    choice_outs = (
        sds((p.J, p.RL, p.ML)),
        sds((p.J, p.NR, p.ML), BF),
        sds((p.C * p.i8, LANES)),
    )
    choice_scratch = (pltpu.VMEM((p.J, p.RL, LANES), F32), pltpu.VMEM((p.hh, p.J, LANES), F32))
    found = gather(table)
    base, parts, pred = call(
        kernel(choice_first_kernel), choice_outs, (taste, found, mean_t, mass_t), scratch=choice_scratch, alias={0: 0}
    )
    gaps, clips = [], []
    for step in range(ITERS):
        last = step == ITERS - 1
        totals = call(
            kernel(scatter_kernel),
            sds((p.FP + 8, LANES)),
            (parts, firms_t, mass_row),
            scratch=(pltpu.VMEM((p.F, p.NR), F32),),
        )
        other = swap(totals)
        if last:
            break
        gap, squares = call(kernel(gap_kernel), (sds((p.FP, LANES)), sds((8, LANES))), (totals, other, share))
        gaps.append(gap)
        mean, send = call(
            kernel(mean_kernel),
            (sds((p.i8, LANES)), sds((p.C * p.S2, LANES))),
            (exchange(pred), mean, log_share, mass_total, squares),
        )
        recv = exchange(send)
        found = gather(gap)
        base, parts, pred, clip = call(
            kernel(choice_next_kernel),
            choice_outs + (sds((8, LANES)),),
            (base, found, recv, mass_t),
            scratch=choice_scratch + (pltpu.VMEM((p.G, LANES), F32),),
            alias={0: 0},
        )
        clips.append(clip)
    send = call(
        kernel(final_kernel),
        sds((p.C * p.S3, LANES)),
        (totals, other, share, table, gaps[0], gaps[1], jnp.concatenate(clips, axis=0), order_columns, pred),
    )
    mean_out, loyalty_out = call(
        kernel(out_kernel),
        (sds((p.i8, LANES)), sds((p.ownp, p.R))),
        (exchange(send), mean, log_share, mass_total),
    )
    mean_out = mean_out.reshape(p.i8, p.h, p.J).transpose(1, 0, 2).reshape(p.M, p.J)
    return (mean_out, loyalty_out[0 : p.own])


def solution(mesh):
    both = ("mkt", "grp")
    placed = (
        P(both, None),
        P(both, None),
        P(both, None, None),
        P(both, None, None),
        P(),
        P(both, None),
        P(both),
        P(both, None),
        P(),
        P(both, None),
        P(),
    )
    return jax.shard_map(
        local,
        mesh=mesh,
        in_specs=placed,
        out_specs=(P(both, None), P(both, None)),
        check_vma=False,
    )
```

time: 557 us -> 199 us (0.36)
  blocking collectives: 235 us -> 16.9 us
  waiting for transfers between devices: 197 us -> 30.5 us
  Pallas kernels: 0 us -> 86 us
  matrix products: 37.9 us -> 0 us
  starting transfers between devices: 7.5 us -> 31.6 us
  other arithmetic: 23.5 us -> 2.74 us
  between operations: 16 us -> 1.01 us
  local copies, waits for them, and re-layouts: 38.1 us -> 29 us
    psum x4 -> x0, blocking collectives: 183 us -> none  [the longest x3 116 us: local(): squares = lax.psum(jnp.sum(gap * gap), ('mkt', 'grp'))]
    all_gather x3 -> x0, waiting for transfers between devices: 154 us -> none  [local(): table = lax.all_gather(owned, ('mkt', 'grp'), axis=0, tiled=True)]
    pallas_call x0 -> x18, Pallas kernels: none -> 86 us  [call(): pl.pallas_call(kernel, out_shape=outs, in_specs=[VM] * len(args), out_spe...]
    dot_general x7 -> x0, matrix products: 37.9 us -> none  [the longest x3 16.6 us: market_terms(): jnp.einsum('mjr,mr->mj', choice_prob, type_weight, precision=lax.Precisio...]
    all_to_all x1, blocking collectives: 52 us -> 16.9 us  [exchange(): lax.all_to_all(x, AXES, split_axis=0, concat_axis=0, tiled=True, axis_ind...]
    gather x6 -> x0, local copies, waits for them, and re-layouts: 31.6 us -> none  [the longest x3 24 us: market_terms(): jnp.take(table, row_ids, axis=0)]
    all_to_all x2 -> x5, starting transfers between devices: 7.2 us -> 31.3 us  [exchange(): lax.all_to_all(x, AXES, split_axis=0, concat_axis=0, tiled=True, axis_ind...]
    unnamed x30 -> x32, local copies, waits for them, and re-layouts: 3.92 us -> 24.3 us
  transfers between devices with their start and end apart: 5 -> 9, of which waited for: 4 -> 5; matrix products, arithmetic and copies ran while one was open for 5% -> 1% of each run, Pallas kernels for 0% -> 16%
where the time goes in v1:
time: 199 us; the launch traced here: 198 us
  Pallas kernels  86 us (43%)
  starting transfers between devices  31.6 us (16%)
  waiting for transfers between devices  30.5 us (15%)
  local copies, waits for them, and re-layouts  29 us (15%)
  blocking collectives  16.9 us (8%)
  other arithmetic  2.74 us (1%)
    pallas_call x18, Pallas kernels, call(): pl.pallas_call(kernel, out_shape=outs, in_specs=[VM] * len(args), out_spe...  86 us
    all_to_all x5, starting transfers between devices, exchange(): lax.all_to_all(x, AXES, split_axis=0, concat_axis=0, tiled=True, axis_ind...  31.3 us
    all_to_all x5, waiting for transfers between devices, exchange(): lax.all_to_all(x, AXES, split_axis=0, concat_axis=0, tiled=True, axis_ind...  27.3 us
    unnamed x32, local copies, waits for them, and re-layouts  24.3 us
    all_to_all x1, blocking collectives, exchange(): lax.all_to_all(x, AXES, split_axis=0, concat_axis=0, tiled=True, axis_ind...  16.9 us
  transfers between devices with their start and end apart: 9, of which 5 were waited for; matrix products, arithmetic and copies ran while one was open for 1% of the time, Pallas kernels for 16%

profile of v1, /device:TPU:0, one launch (start us, length us, event | category | flops | bytes accessed | tf_op | source)
XLA Modules:
  0.0 197.7 jit_solution(1117749493316359341)
XLA Ops:
  0.6 0.8 convert_element_type.3.firms
  1.5 0.9 multiply_bitcast_fusion.traits
  2.3 1.0 fusion
  3.4 1.0 copy-done.12
  4.4 0.8 copy-done.13
  5.2 0.7 copy-done.14
  5.9 0.2 shard_map.122
  6.1 0.9 copy-done.11
  7.0 8.3 %all-to-all-start = ((f32[16,112,128]{2,1,0:T(8,128)}), f32[16,112,128]{2,1,0:T(8,128)S(1)}, u32[]{:S(2)}, u32[]{:S(2)}) async-start(f32[16,112,128]{2,1,0:T(8,128)} %bitcast.36), calls=%async_computation | async-start | bytes 1835008 | tf_op jit(solution)/shard_map/all_to_all | solution.py:428
  15.4 0.8 reshape.60
  16.7 0.7 log_bitcast_fusion
  17.4 20.0 %all-to-all-done = f32[16,112,128]{2,1,0:T(8,128)S(1)} async-done(((f32[16,112,128]{2,1,0:T(8,128)}), f32[16,112,128]{2,1,0:T(8,128)S(1)}, u32[]{:S(2)}, u32[]{:S(2)}) %all-to-all-start) | async-done | bytes 917536 | tf_op jit(solution)/shard_map/all_to_all | solution.py:428
  37.4 2.2 %shard_map.123 = (f32[64,64,256]{2,1,0:T(8,128)S(1)}, s32[2,64,128]{2,1,0:T(8,128)S(1)}, f32[2,64,128]{2,1,0:T(8,128)S(1)}, f32[64,256]{1,0:T(8,128)S(1)}, f32[8,128]{1,0:T(8,128)S(1)}, /*index=5*/f32[128,128]{1,0:T(8,128)S(1)}) custom-call(f32[1792,128]{1,0:T(8,128)S(1)} %bitcast.35), custom_call_target="tpu_custom_call" | custom-call | tf_op jit(solution)/shard_map/pallas_call | solution.py:59
  39.7 1.2 collective-permute-done.other
  40.9 0.6 shard_map.124.packed.table
  41.5 10.3 %shard_map.125.found = f32[64,64,256]{2,1,0:T(8,128)S(1)} custom-call(f32[256,128]{1,0:T(8,128)S(1)} %shard_map.124.packed.table, s32[2,64,128]{2,1,0:T(8,128)S(1)} %get-tuple-element.30.firms_t), custom_call_target="tpu_custom_call" | custom-call | tf_op jit(solution)/shard_map/pallas_call | solution.py:59
  51.9 2.0 copy-done.7
  53.9 6.8 %shard_map.126 = (f32[64,64,256]{2,1,0:T(8,128)S(1)}, bf16[64,128,256]{2,1,0:T(8,128)(2,1)}, f32[128,128]{1,0:T(8,128)}) custom-call(f32[64,64,256]{2,1,0:T(8,128)S(1)} %get-tuple-element.28.taste, f32[64,64,256]{2,1,0:T(8,128)} %copy-done.7, f32[2,64,128]{2,1,0:T(8,128)S(1)} %get-tuple-element.31.mean_t, ...), custom_call_target="tpu_custom_call", output_to_operand_aliasing={{0}: (0, {})} | custom-call | tf_op jit(solution)/shard_map/pallas_call | solution.py:59
  60.7 2.0 copy-done.1
  62.7 5.6 %all-to-all-start.1 = ((f32[16,8,128]{2,1,0:T(8,128)}), f32[16,8,128]{2,1,0:T(8,128)S(1)}, u32[]{:S(2)}, u32[]{:S(2)}) async-start(f32[16,8,128]{2,1,0:T(8,128)} %bitcast.10), calls=%async_computation.1 | async-start | bytes 131072 | tf_op jit(solution)/shard_map/all_to_all | solution.py:428
  68.3 2.2 %copy-done.8 = bf16[64,128,256]{2,1,0:T(8,128)(2,1)S(1)} copy-done((bf16[64,128,256]{2,1,0:T(8,128)(2,1)S(1)}, bf16[64,128,256]{2,1,0:T(8,128)(2,1)}, u32[]{:S(2)}) %copy-start.8) | copy-done | bytes 4194328
  70.5 9.8 %shard_map.127.mine = f32[264,128]{1,0:T(8,128)S(1)} custom-call(bf16[64,128,256]{2,1,0:T(8,128)(2,1)S(1)} %copy-done.8, s32[2,64,128]{2,1,0:T(8,128)S(1)} %get-tuple-element.30.firms_t, f32[8,128]{1,0:T(8,128)S(1)} %get-tuple-element.35.mass_row), custom_call_target="tpu_custom_call" | custom-call | tf_op jit(solution)/shard_map/pallas_call | solution.py:59
  81.0 0.6 collective-permute-done.1.other
  81.9 0.7 all_to_all.48
  82.5 6.9 %all-to-all-start.2 = ((f32[16,9,128]{2,1,0:T(8,128)}), f32[16,9,128]{2,1,0:T(8,128)S(1)}, u32[]{:S(2)}, u32[]{:S(2)}) async-start(f32[16,9,128]{2,1,0:T(8,128)} %all_to_all.48), calls=%async_computation.2 | async-start | bytes 262144 | tf_op jit(solution)/shard_map/all_to_all | solution.py:428
  89.5 10.3 %shard_map.129.found = f32[64,64,256]{2,1,0:T(8,128)S(1)} custom-call(f32[256,128]{1,0:T(8,128)S(1)} %get-tuple-element.36.packed.gap0, s32[2,64,128]{2,1,0:T(8,128)S(1)} %get-tuple-element.30.firms_t), custom_call_target="tpu_custom_call" | custom-call | tf_op jit(solution)/shard_map/pallas_call | solution.py:59
  99.8 2.0 %copy-done.5 = f32[64,64,256]{2,1,0:T(8,128)} copy-done((f32[64,64,256]{2,1,0:T(8,128)}, f32[64,64,256]{2,1,0:T(8,128)S(1)}, u32[]{:S(2)}) %copy-start.5) | copy-done | bytes 4194328
  101.9 2.2 %copy-done.2 = f32[64,64,256]{2,1,0:T(8,128)S(1)} copy-done((f32[64,64,256]{2,1,0:T(8,128)S(1)}, f32[64,64,256]{2,1,0:T(8,128)}, u32[]{:S(2)}) %copy-start.2) | copy-done | bytes 4194328
  104.0 7.0 %shard_map.131 = (f32[64,64,256]{2,1,0:T(8,128)S(1)}, bf16[64,128,256]{2,1,0:T(8,128)(2,1)}, f32[128,128]{1,0:T(8,128)}, f32[8,128]{1,0:T(8,128)S(1)}) custom-call(f32[64,64,256]{2,1,0:T(8,128)S(1)} %copy-done.2, f32[64,64,256]{2,1,0:T(8,128)} %copy-done.5, f32[144,128]{1,0:T(8,128)S(1)} %all_to_all.50.recv, ...), custom_call_target="tpu_custom_call", output_to_operand_aliasing={{0}: (0, {})} | custom-call | tf_op jit(solution)/shard_map/pallas_call | solution.py:59
  111.0 2.0 copy-done.3
  113.0 2.2 %copy-done.10 = bf16[64,128,256]{2,1,0:T(8,128)(2,1)S(1)} copy-done((bf16[64,128,256]{2,1,0:T(8,128)(2,1)S(1)}, bf16[64,128,256]{2,1,0:T(8,128)(2,1)}, u32[]{:S(2)}) %copy-start.10) | copy-done | bytes 4194328
  115.2 9.8 %shard_map.132.mine = f32[264,128]{1,0:T(8,128)S(1)} custom-call(bf16[64,128,256]{2,1,0:T(8,128)(2,1)S(1)} %copy-done.10, s32[2,64,128]{2,1,0:T(8,128)S(1)} %get-tuple-element.30.firms_t, f32[8,128]{1,0:T(8,128)S(1)} %get-tuple-element.35.mass_row), custom_call_target="tpu_custom_call" | custom-call | tf_op jit(solution)/shard_map/pallas_call | solution.py:59
  125.0 6.9 %all-to-all-start.3 = ((f32[16,8,128]{2,1,0:T(8,128)}), f32[16,8,128]{2,1,0:T(8,128)S(1)}, u32[]{:S(2)}, u32[]{:S(2)}) async-start(f32[16,8,128]{2,1,0:T(8,128)} %bitcast.17), calls=%async_computation.3 | async-start | bytes 131072 | tf_op jit(solution)/shard_map/all_to_all | solution.py:428
  132.0 0.2 shard_map.133
  132.1 7.4 %all-to-all-done.3 = f32[16,8,128]{2,1,0:T(8,128)S(1)} async-done(((f32[16,8,128]{2,1,0:T(8,128)}), f32[16,8,128]{2,1,0:T(8,128)S(1)}, u32[]{:S(2)}, u32[]{:S(2)}) %all-to-all-start.3) | async-done | bytes 65568 | tf_op jit(solution)/shard_map/all_to_all | solution.py:428
  139.5 0.7 all_to_all.54
  140.2 3.5 %all-to-all-start.4 = ((f32[16,9,128]{2,1,0:T(8,128)}), f32[16,9,128]{2,1,0:T(8,128)S(1)}, u32[]{:S(2)}, u32[]{:S(2)}) async-start(f32[16,9,128]{2,1,0:T(8,128)} %all_to_all.54), calls=%async_computation.4 | async-start | bytes 262144 | tf_op jit(solution)/shard_map/all_to_all | solution.py:428
  143.7 10.3 %shard_map.134.found = f32[64,64,256]{2,1,0:T(8,128)S(1)} custom-call(f32[256,128]{1,0:T(8,128)S(1)} %get-tuple-element.42.packed.gap1, s32[2,64,128]{2,1,0:T(8,128)S(1)} %get-tuple-element.30.firms_t), custom_call_target="tpu_custom_call" | custom-call | tf_op jit(solution)/shard_map/pallas_call | solution.py:59
  154.1 2.0 %copy-done.6 = f32[64,64,256]{2,1,0:T(8,128)} copy-done((f32[64,64,256]{2,1,0:T(8,128)}, f32[64,64,256]{2,1,0:T(8,128)S(1)}, u32[]{:S(2)}) %copy-start.6) | copy-done | bytes 4194328
  156.1 2.2 %copy-done.4 = f32[64,64,256]{2,1,0:T(8,128)S(1)} copy-done((f32[64,64,256]{2,1,0:T(8,128)S(1)}, f32[64,64,256]{2,1,0:T(8,128)}, u32[]{:S(2)}) %copy-start.4) | copy-done | bytes 4194328
  158.3 6.9 %shard_map.136 = (f32[64,64,256]{2,1,0:T(8,128)S(1)}, bf16[64,128,256]{2,1,0:T(8,128)(2,1)}, f32[128,128]{1,0:T(8,128)S(1)}, f32[8,128]{1,0:T(8,128)S(1)}) custom-call(f32[64,64,256]{2,1,0:T(8,128)S(1)} %copy-done.4, f32[64,64,256]{2,1,0:T(8,128)} %copy-done.6, f32[144,128]{1,0:T(8,128)S(1)} %all_to_all.56.recv, ...), custom_call_target="tpu_custom_call", output_to_operand_aliasing={{0}: (0, {})} | custom-call | tf_op jit(solution)/shard_map/pallas_call | solution.py:59
  165.2 2.2 %copy-done.9 = bf16[64,128,256]{2,1,0:T(8,128)(2,1)S(1)} copy-done((bf16[64,128,256]{2,1,0:T(8,128)(2,1)S(1)}, bf16[64,128,256]{2,1,0:T(8,128)(2,1)}, u32[]{:S(2)}) %copy-start.9) | copy-done | bytes 4194328
  167.4 9.8 %shard_map.137.mine = f32[264,128]{1,0:T(8,128)S(1)} custom-call(bf16[64,128,256]{2,1,0:T(8,128)(2,1)S(1)} %copy-done.9, s32[2,64,128]{2,1,0:T(8,128)S(1)} %get-tuple-element.30.firms_t, f32[8,128]{1,0:T(8,128)S(1)} %get-tuple-element.35.mass_row), custom_call_target="tpu_custom_call" | custom-call | tf_op jit(solution)/shard_map/pallas_call | solution.py:59
  177.3 1.3 collective-permute-done.3.other
  178.6 0.7 shard_map.138
  179.3 16.9 %all_to_all.66 = f32[16,25,128]{2,1,0:T(8,128)S(1)} all-to-all(f32[16,25,128]{2,1,0:T(8,128)S(1)} %all_to_all.57), channel_id=1, replica_groups={{0,2,4,6,8,10,12,14,16,18,20,22,24,26,28,30},{1,3,5,7,9,11,13,15,17,19,..., dimensions={0} | all-to-all | bytes 409600 | tf_op jit(solution)/shard_map/all_to_all | solution.py:428
  196.2 0.8 shard_map.139
  197.1 0.6 copy.60
  (53 shorter events, 1.8 us)
Async XLA Ops:
  0.6 80.0 %copy-start = (f32[512,1024]{1,0:T(8,128)S(1)}, f32[512,1024]{1,0:T(8,128)}, u32[]{:S(2)}) copy-start(f32[512,1024]{1,0:T(8,128)} %param.21) | copy-start | bytes 6291460
  3.4 1.0 copy-start.12
  4.4 0.8 copy-start.13
  5.2 0.7 copy-start.14
  6.1 0.9 copy-start.11
  7.0 30.3 %all-to-all-start = ((f32[16,112,128]{2,1,0:T(8,128)}), f32[16,112,128]{2,1,0:T(8,128)S(1)}, u32[]{:S(2)}, u32[]{:S(2)}) async-start(f32[16,112,128]{2,1,0:T(8,128)} %bitcast.36), calls=%async_computation | async-start | bytes 1835008 | tf_op jit(solution)/shard_map/all_to_all | solution.py:428
  39.6 1.3 collective-permute-start
  51.9 2.0 copy-start.7
  60.7 2.0 copy-start.1
  62.7 17.8 %copy-start.15 = (f32[16,64]{1,0:T(8,128)S(1)}, f32[16,64]{1,0:T(8,128)}, u32[]{:S(2)}) copy-start(f32[16,64]{1,0:T(8,128)} %mean.1) | copy-start | bytes 12292
  62.7 19.2 %all-to-all-start.1 = ((f32[16,8,128]{2,1,0:T(8,128)}), f32[16,8,128]{2,1,0:T(8,128)S(1)}, u32[]{:S(2)}, u32[]{:S(2)}) async-start(f32[16,8,128]{2,1,0:T(8,128)} %bitcast.10), calls=%async_computation.1 | async-start | bytes 131072 | tf_op jit(solution)/shard_map/all_to_all | solution.py:428
  68.3 2.2 %copy-start.8 = (bf16[64,128,256]{2,1,0:T(8,128)(2,1)S(1)}, bf16[64,128,256]{2,1,0:T(8,128)(2,1)}, u32[]{:S(2)}) copy-start(bf16[64,128,256]{2,1,0:T(8,128)(2,1)} %get-tuple-element.34.parts) | copy-start | bytes 12582916
  80.3 1.4 collective-permute-start.1
  82.5 19.3 %all-to-all-start.2 = ((f32[16,9,128]{2,1,0:T(8,128)}), f32[16,9,128]{2,1,0:T(8,128)S(1)}, u32[]{:S(2)}, u32[]{:S(2)}) async-start(f32[16,9,128]{2,1,0:T(8,128)} %all_to_all.48), calls=%async_computation.2 | async-start | bytes 262144 | tf_op jit(solution)/shard_map/all_to_all | solution.py:428
  99.8 2.0 %copy-start.5 = (f32[64,64,256]{2,1,0:T(8,128)}, f32[64,64,256]{2,1,0:T(8,128)S(1)}, u32[]{:S(2)}) copy-start(f32[64,64,256]{2,1,0:T(8,128)S(1)} %shard_map.129.found) | copy-start | bytes 12582916
  101.8 2.2 %copy-start.2 = (f32[64,64,256]{2,1,0:T(8,128)S(1)}, f32[64,64,256]{2,1,0:T(8,128)}, u32[]{:S(2)}) copy-start(f32[64,64,256]{2,1,0:T(8,128)} %copy-done.1) | copy-start | bytes 12582916
  111.0 2.0 copy-start.3
  113.0 2.2 %copy-start.10 = (bf16[64,128,256]{2,1,0:T(8,128)(2,1)S(1)}, bf16[64,128,256]{2,1,0:T(8,128)(2,1)}, u32[]{:S(2)}) copy-start(bf16[64,128,256]{2,1,0:T(8,128)(2,1)} %get-tuple-element.41.parts) | copy-start | bytes 12582916
  124.9 7.0 %collective-permute-start.2 = (f32[264,128]{1,0:T(8,128)S(1)}, f32[264,128]{1,0:T(8,128)S(1)}, u32[]{:S(2)}, u32[]{:S(2)}) collective-permute-start(f32[264,128]{1,0:T(8,128)S(1)} %shard_map.132.mine), channel_id=1, source_target_pairs={{0,1},{1,0},{2,3},{3,2},{4,5},{5,4},{6,7},{7,6},{8,9},{9,8},{10,11... | collective-permute-start | bytes 405512 | tf_op jit(solution)/shard_map/ppermute | solution.py:431
  125.0 14.5 %all-to-all-start.3 = ((f32[16,8,128]{2,1,0:T(8,128)}), f32[16,8,128]{2,1,0:T(8,128)S(1)}, u32[]{:S(2)}, u32[]{:S(2)}) async-start(f32[16,8,128]{2,1,0:T(8,128)} %bitcast.17), calls=%async_computation.3 | async-start | bytes 131072 | tf_op jit(solution)/shard_map/all_to_all | solution.py:428
  140.2 15.9 %all-to-all-start.4 = ((f32[16,9,128]{2,1,0:T(8,128)}), f32[16,9,128]{2,1,0:T(8,128)S(1)}, u32[]{:S(2)}, u32[]{:S(2)}) async-start(f32[16,9,128]{2,1,0:T(8,128)} %all_to_all.54), calls=%async_computation.4 | async-start | bytes 262144 | tf_op jit(solution)/shard_map/all_to_all | solution.py:428
  154.1 2.0 %copy-start.6 = (f32[64,64,256]{2,1,0:T(8,128)}, f32[64,64,256]{2,1,0:T(8,128)S(1)}, u32[]{:S(2)}) copy-start(f32[64,64,256]{2,1,0:T(8,128)S(1)} %shard_map.134.found) | copy-start | bytes 12582916
  156.1 2.2 %copy-start.4 = (f32[64,64,256]{2,1,0:T(8,128)S(1)}, f32[64,64,256]{2,1,0:T(8,128)}, u32[]{:S(2)}) copy-start(f32[64,64,256]{2,1,0:T(8,128)} %copy-done.3) | copy-start | bytes 12582916
  165.2 2.2 %copy-start.9 = (bf16[64,128,256]{2,1,0:T(8,128)(2,1)S(1)}, bf16[64,128,256]{2,1,0:T(8,128)(2,1)}, u32[]{:S(2)}) copy-start(bf16[64,128,256]{2,1,0:T(8,128)(2,1)} %get-tuple-element.47.parts) | copy-start | bytes 12582916
  177.2 1.4 collective-permute-start.3

commit v2 on v0

v2 whole, which is shorter than its diff:
```python
import functools

import jax
import jax.numpy as jnp
from jax import lax
from jax.experimental import pallas as pl
from jax.experimental.pallas import tpu as pltpu
from jax.sharding import PartitionSpec as P

ITERS = 3
LANES = 128
clip_target = 0.5
norm_eps = 1e-06
BF = jnp.bfloat16
F32 = jnp.float32


class Plan:
    def __init__(self, mkt, grp, own_markets, products, traits, types, firms, own_firms):
        self.C, self.Q = mkt, grp
        self.M, self.J, self.K = own_markets, products, traits
        self.R, self.F, self.own = types, firms, own_firms
        self.RL = types // mkt
        self.hh = LANES // self.RL
        self.ii = own_markets // self.hh
        self.h = LANES // products
        self.i8 = own_markets // self.h
        self.top = max(self.hh, self.h)
        self.w = own_markets // self.top
        self.ML = own_markets * mkt
        self.PR = mkt * self.i8
        self.FP = firms // self.hh
        self.HR = self.FP // 2
        self.ownp = -(-own_firms // self.hh) * self.hh
        self.oi = self.ownp // self.hh
        self.u = max(1, 256 // self.ML)
        self.NS = products // self.u
        self.NR = max(LANES, 2 * self.RL)
        self.s_draws = 0
        self.s_mass = self.s_draws + traits * self.ii
        self.s_loy = self.s_mass + self.ii
        self.s_traits = self.s_loy + self.oi
        self.s_firms = self.s_traits + traits * self.i8
        self.s_mean = self.s_firms + self.i8
        self.s_shift = self.s_mean + self.i8
        self.S = -(-(self.s_shift + self.i8) // 8) * 8
        self.PB = self.hh * products
        self.S2 = self.PB + 8
        self.S3 = -(-(self.i8 + 2 * self.oi + 1) // 8) * 8
        self.vmem = 16 if firms * products * self.ML <= 2**22 else 58


VM = pl.BlockSpec(memory_space=pltpu.VMEM)
SM = pl.BlockSpec(memory_space=pltpu.SMEM)
HBM = pl.BlockSpec(memory_space=pltpu.HBM)


def call(p, kernel, outs, args, scratch=(), specs=None, out_specs=None, flops=0):
    return pl.pallas_call(
        functools.partial(kernel, p),
        out_shape=outs,
        in_specs=specs or [VM] * len(args),
        out_specs=out_specs or jax.tree.map(lambda _: VM, outs),
        scratch_shapes=list(scratch),
        compiler_params=pltpu.CompilerParams(vmem_limit_bytes=p.vmem * 2**20),
    )(*args)


def sds(shape, dtype=F32):
    return jax.ShapeDtypeStruct(shape, dtype)


def block_mask(width, rows, b):
    return lax.broadcasted_iota(jnp.int32, (rows, LANES), 1) // width == b


def fold(p, x):
    total = x
    for b in range(1, p.hh):
        total = total + pltpu.roll(x, b * p.RL, 1)
    return total


def split2(x):
    a = x.astype(BF)
    return a, (x - a.astype(F32)).astype(BF)


def split3(x):
    a = x.astype(BF)
    b, c = split2(x - a.astype(F32))
    return a, b, c


def dot(a, b):
    return jnp.dot(a, b, preferred_element_type=F32)


def dot_t(a, b):
    return lax.dot_general(a, b, (((1,), (1,)), ((), ())), preferred_element_type=F32)


def moved(x, shift):
    return pltpu.roll(x, shift % LANES, 1) if shift % LANES else x


def pack_kernel(
    p, scale, size, draws_h, weight_h, loyalty_h, traits_h, firms_h, mean_h, share_h, out_h,
    draws, weight, loyalty, traits, firms, mean, share, out, sems, out_sems,
):
    pairs = (
        (draws_h, draws), (weight_h, weight), (traits_h, traits), (firms_h, firms),
        (mean_h, mean), (share_h, share), (loyalty_h, loyalty),
    )
    copies = [pltpu.make_async_copy(a, b, sems.at[n]) for n, (a, b) in enumerate(pairs)]
    for copy in copies:
        copy.start()
    for copy in copies:
        copy.wait()
    row = lax.broadcasted_iota(jnp.int32, (p.M, LANES), 0)
    column = jnp.zeros((p.M, LANES), F32)
    for m in range(p.M):
        column = jnp.where(row == m, size[m], column)
    mass_total = None
    tiles = []
    for t in range(p.R // LANES):
        tile = weight[:, t * LANES : (t + 1) * LANES] * column
        tiles.append(tile)
        mass_total = tile if mass_total is None else mass_total + tile
    mass_total = jnp.sum(mass_total, axis=1, keepdims=True)

    def by_type(tile_of, c, section, rows):
        tile, b = tile_of(c // p.hh), c % p.hh
        value = tile[0:rows, :] if not b else moved(tile, -b * p.RL)[0:rows, :]
        for q in range(1, p.hh):
            piece = moved(tile, (q - b) * p.RL)[q * rows : (q + 1) * rows, :]
            value = jnp.where(block_mask(p.RL, rows, q), piece, value)
        out[c * p.S + section : c * p.S + section + rows, :] = value

    def packed(x):
        return jnp.concatenate([x[q * p.i8 : (q + 1) * p.i8, :] for q in range(p.h)], axis=1)

    products = [packed(traits[k] * scale[k]) for k in range(p.K)]
    products += [packed(firms[...].astype(F32)), packed(mean[...])]
    products += [packed(jnp.log(share[...]) + jnp.log(mass_total))]
    sends = []
    for c in range(p.C):
        for k in range(p.K):
            by_type(lambda t: draws[k, :, t * LANES : (t + 1) * LANES], c, p.s_draws + k * p.ii, p.ii)
        by_type(lambda t: tiles[t], c, p.s_mass, p.ii)
        by_type(lambda t: loyalty[:, t * LANES : (t + 1) * LANES], c, p.s_loy, p.oi)
        for n, value in enumerate(products):
            at = c * p.S + p.s_traits + n * p.i8
            out[at : at + p.i8, :] = value
        part = pl.ds(c * p.S, p.S)
        copy = pltpu.make_async_copy(out.at[part], out_h.at[part], out_sems.at[c])
        copy.start()
        sends.append(copy)
    for copy in sends:
        copy.wait()


def prep_kernel(p, recv, firms_t, mean_t, shift_t, mass_t, mass_row, loy, draws_t, traits_t, nat):
    ta = p.top // p.hh

    def typed(section, store):
        for a in range(ta):
            for c in range(p.C):
                at = c * p.S + section + a * p.w
                nat[(a * p.C + c) * p.w : (a * p.C + c + 1) * p.w, :] = recv[at : at + p.w, :]
        flat = nat[0:LANES, :]
        turned = flat.T
        for b in range(p.hh):
            store(b, turned[b * p.RL : (b + 1) * p.RL, :])
        return flat

    def put_mass(b, value):
        mass_t[:, b * LANES : (b + 1) * LANES] = value

    flat = typed(p.s_mass, put_mass)
    row = jnp.sum(flat, axis=0, keepdims=True)
    mass_row[...] = fold(p, jnp.broadcast_to(row, (8, LANES)))
    for k in range(p.K):

        def put_draws(b, value):
            draws_t[k, :, b * LANES : (b + 1) * LANES] = value

        typed(p.s_draws + k * p.ii, put_draws)

    tb = p.top // p.h

    def product(section, store):
        for copy in range(max(1, LANES // p.PR)):
            for a in range(tb):
                for c in range(p.C):
                    at = c * p.S + section + a * p.w
                    to = copy * p.PR + (a * p.C + c) * p.w
                    nat[to : to + p.w, :] = recv[at : at + p.w, :]
        if p.PR >= LANES:
            per = p.PR // LANES
            for gi in range(per):
                turned = nat[gi * LANES : (gi + 1) * LANES, :].T
                for q in range(p.h):
                    store(q * per + gi, turned[q * p.J : (q + 1) * p.J, :])
        else:
            per = LANES // p.PR
            turned = nat[0:LANES, :].T
            for b in range(p.hh):
                value = turned[b * per * p.J : (b * per + 1) * p.J, :]
                for s in range(1, per):
                    at = (b * per + s) * p.J
                    value = jnp.where(block_mask(p.PR, p.J, s), turned[at : at + p.J, :], value)
                store(b, value)

    def into(ref):
        def store(b, value):
            ref[b] = value

        return store

    product(p.s_firms, into(firms_t))
    product(p.s_mean, into(mean_t))
    product(p.s_shift, into(shift_t))
    for k in range(p.K):
        product(p.s_traits + k * p.i8, into(traits_t.at[k]))
    loy[...] = jnp.zeros_like(loy)
    for c in range(p.C):
        loy[c * p.oi : (c + 1) * p.oi, :] = recv[c * p.S + p.s_loy : c * p.S + p.s_loy + p.oi, :]


def taste_kernel(p, draws_t, traits_t, firms_t, taste, hot):
    rows = min(p.F, 256)
    firm = lax.broadcasted_iota(jnp.int32, (rows, LANES), 0).astype(F32).astype(BF)

    def body(n, _):
        for v in range(p.u):
            j = n * p.u + v
            for b in range(p.hh):
                at = slice(b * LANES, (b + 1) * LANES)
                value = None
                for k in range(p.K):
                    term = traits_t[k, b, pl.ds(j, 1), :] * draws_t[k, :, at]
                    value = term if value is None else value + term
                taste[j, :, at] = value
                row = firms_t[b, pl.ds(j, 1), :]
                to = slice(v * p.ML + b * LANES, v * p.ML + (b + 1) * LANES)
                for base in range(0, p.F, rows):
                    want = jnp.broadcast_to(row - float(base), (rows, LANES)).astype(BF)
                    hot[n, base : base + rows, to] = jnp.where(firm == want, jnp.ones((), BF), jnp.zeros((), BF))
        return 0

    lax.fori_loop(0, p.NS, body, 0)


def table_kernel(p, place, order, share_h, *refs):
    blocks, (table, share, columns, tile, sem) = refs[:-5], refs[-5:]
    lane = place[0] * p.RL
    start = pl.multiple_of(lane // LANES * LANES, LANES)
    copy = pltpu.make_async_copy(share_h.at[:, pl.ds(start, LANES)], tile, sem)
    copy.start()
    firm = lax.broadcasted_iota(jnp.int32, (p.F, LANES), 0)
    total = jnp.zeros((p.F, LANES), F32)
    blocks = [ref[at : at + LANES, :] for ref in blocks for at in range(0, ref.shape[0], LANES)]
    for s, block in enumerate(blocks):
        pieces = jnp.concatenate(split3(block), axis=1)
        member = place[1] ^ s
        for b in range(p.hh):
            hot = (firm == order[pl.ds(member * p.hh + b, 1), :]).astype(F32).astype(BF)
            found = dot(hot, pieces)
            found = found[:, 0:LANES] + found[:, LANES : 2 * LANES] + found[:, 2 * LANES :]
            if p.hh > 1:
                found = jnp.where(block_mask(p.RL, p.F, b), found, 0.0)
            total = total + found
    pack_table(p, fold(p, total), table)
    for b in range(p.hh):
        row = order[pl.ds(place[1] * p.hh + b, 1), :].astype(F32)
        columns[b] = jnp.broadcast_to(row, (LANES, LANES)).T
    copy.wait()
    if p.hh == 1:
        share[...] = tile[...]
    else:
        for b in range(p.hh):
            part = pltpu.roll(tile[b * p.FP : (b + 1) * p.FP, :], (b * p.RL + LANES - (lane - start)) % LANES, 1)
            mask = block_mask(p.RL, p.FP, b)
            share[...] = part if not b else jnp.where(mask, part, share[...])


def pack_table(p, full, out):
    value = full[0 : p.FP, :]
    for b in range(1, p.hh):
        value = jnp.where(block_mask(p.RL, p.FP, b), full[b * p.FP : (b + 1) * p.FP, :], value)
    out[...] = value


def clip_of(p, squares):
    return jnp.minimum(1.0, clip_target / jnp.sqrt(squares / (p.F * p.R) + norm_eps))


def sum_chunks(p, recv, step, start, rows):
    total = recv[start : start + rows, :]
    for c in range(1, p.C):
        total = total + recv[c * step + start : c * step + start + rows, :]
    return total


def step_body(p, place, table, mean_of, taste, hot, mass_t, mass_row, pred, keep, give, tab, expu, parts, acc):
    turned = table[...].T
    for q, piece in enumerate(split2(turned)):
        for b in range(p.hh):
            tab[b, q * p.RL : (q + 1) * p.RL, :] = piece[b * p.RL : (b + 1) * p.RL, :]

    def gather(n, total):
        if p.hh == 1:
            found = dot(tab[0], hot[n])
        else:
            found = dot(tab[0], hot[n, 0 : p.FP, :])
            for b in range(1, p.hh):
                found = found + dot(tab[b], hot[n, b * p.FP : (b + 1) * p.FP, :])
        found = found[0 : p.RL] + found[p.RL : 2 * p.RL]
        for v in range(p.u):
            j = n * p.u + v
            means = [jnp.broadcast_to(mean_of[b, pl.ds(j, 1), :], (p.RL, LANES)) for b in range(p.hh)]
            means = means[0] if p.hh == 1 else jnp.concatenate(means, axis=1)
            e = jnp.exp(taste[j] + found[:, v * p.ML : (v + 1) * p.ML] + means)
            expu[j] = e
            total = total + e
        return total

    total = lax.fori_loop(0, p.NS, gather, jnp.zeros((p.RL, p.ML), F32), unroll=2)
    scale = mass_t[...] / (1.0 + total)
    acc[...] = jnp.zeros_like(acc)
    if p.NR > 2 * p.RL:
        parts[...] = jnp.zeros_like(parts)
    per = 2

    def scatter(n, _):
        value = None
        for s in range(per):
            for v in range(p.u):
                j = (n * per + s) * p.u + v
                x = expu[j] * scale
                hi, lo = split2(x)
                at = slice(v * p.ML, (v + 1) * p.ML)
                parts[s, 0 : p.RL, at] = hi
                parts[s, p.RL : 2 * p.RL, at] = lo
                row = jnp.sum(x, axis=0, keepdims=True)
                for b in range(p.hh):
                    pred[pl.ds(b * p.J + j, 1), :] = row[:, b * LANES : (b + 1) * LANES]
            term = dot_t(hot[n * per + s], parts[s])
            value = term if value is None else value + term
        acc[...] += value
        return 0

    lax.fori_loop(0, p.NS // per, scatter, 0)
    full = acc[:, 0:LANES]
    for t in range(1, p.NR // LANES):
        full = full + acc[:, t * LANES : (t + 1) * LANES]
    if p.hh == 1:
        acc[:, 0:LANES] = full
    else:
        pack_table(p, fold(p, full), acc.at[0 : p.FP, 0:LANES])
    mine = (place[1] & 1) * p.HR
    keep[0 : p.HR, :] = acc[pl.ds(pl.multiple_of(mine, 8), p.HR), 0:LANES]
    give[0 : p.HR, :] = acc[pl.ds(pl.multiple_of(p.HR - mine, 8), p.HR), 0:LANES]
    keep[p.HR :, :] = mass_row[...]
    give[p.HR :, :] = mass_row[...]


def first_kernel(p, place, table, mean_t, taste, hot, mass_t, mass_row, pred, keep, give, *scratch):
    step_body(p, place, table, mean_t, taste, hot, mass_t, mass_row, pred, keep, give, *scratch)


def next_kernel(
    p, place, recv, gap_mine, gap_other, table_in, mean_in, shift_t, taste, hot, mass_t, mass_row,
    table, mean_t, pred, keep, give, *scratch
):
    clip = clip_of(p, sum_chunks(p, recv, p.S2, p.PB, 1))
    mine = (place[1] & 1) * p.HR
    for ref, start in ((gap_mine, mine), (gap_other, p.HR - mine)):
        at = pl.ds(pl.multiple_of(start, 8), p.HR)
        table[at, :] = table_in[at, :] + clip * ref[0 : p.HR, :]
    for b in range(p.hh):
        total = sum_chunks(p, recv, p.S2, b * p.J, p.J)
        mean_t[b] = mean_in[b] + shift_t[b] - jnp.log(total)
    step_body(p, place, table, mean_t, taste, hot, mass_t, mass_row, pred, keep, give, *scratch)


def add_kernel(p, a, b, out):
    out[...] = a[...] + b[...]


def gap_kernel(p, place, mine, other, share, gap):
    total = mine[...] + other[...]
    at = pl.ds(pl.multiple_of((place[1] & 1) * p.HR, 8), p.HR)
    value = jnp.log(share[at, :]) - jnp.log(total[0 : p.HR, :] / total[p.HR : p.HR + 1, :])
    gap[0 : p.HR, :] = value
    rows = jnp.sum(value * value, axis=0, keepdims=True)
    gap[p.HR :, :] = jnp.broadcast_to(jnp.sum(rows, axis=1, keepdims=True), (8, LANES))


def send_kernel(p, gap_mine, gap_other, pred, send):
    squares = gap_mine[p.HR :, :] + gap_other[p.HR :, :]
    value = pred[...]
    for c in range(p.C):
        send[c * p.S2 : c * p.S2 + p.PB, :] = value
        send[c * p.S2 + p.PB : (c + 1) * p.S2, :] = squares


def final_kernel(p, place, gap_mine, gap_other, table, columns, pred, mean_t, shift_t, send, own, gap, nat, means):
    mine = (place[1] & 1) * p.HR
    for ref, start in ((gap_mine, mine), (gap_other, p.HR - mine)):
        gap[pl.ds(pl.multiple_of(start, 8), p.HR), :] = ref[0 : p.HR, :]
    squares = gap_mine[p.HR : p.HR + 1, :] + gap_other[p.HR : p.HR + 1, :]
    lane = lax.broadcasted_iota(jnp.int32, (LANES, LANES), 1).astype(F32)
    for n, ref in enumerate((table, gap)):
        pieces = jnp.concatenate(split3(ref[...]), axis=1)
        picked = None
        for o in range(p.hh):
            total = None
            for b in range(p.hh):
                wide = -(-p.FP // LANES)
                hot = [columns[o] == lane + float(b * p.FP + t * LANES) for t in range(wide)]
                hot = jnp.concatenate([x.astype(F32).astype(BF) for x in hot], axis=1)[:, 0 : p.FP]
                found = dot(hot, pieces)
                found = found[:, 0:LANES] + found[:, LANES : 2 * LANES] + found[:, 2 * LANES :]
                if p.hh > 1:
                    found = jnp.where(block_mask(p.RL, LANES, b), found, 0.0)
                total = found if total is None else total + found
            total = fold(p, total)
            picked = total if picked is None else jnp.where(block_mask(p.RL, LANES, o), total, picked)
        at = p.i8 + n * p.oi
        for c in range(p.C):
            send[c * p.S3 + at : c * p.S3 + at + p.oi, :] = picked[c * p.oi : (c + 1) * p.oi, :]
    tb = p.top // p.h

    def by_owner(block, store):
        if p.PR >= LANES:
            per = p.PR // LANES
            for gi in range(per):
                tall = [block(q * per + gi) for q in range(p.h)]
                nat[gi * LANES : (gi + 1) * LANES, :] = jnp.concatenate(tall, axis=0).T
        else:
            per = LANES // p.PR
            tall = [moved(block(q // per), -(q % per) * p.PR) for q in range(p.h)]
            nat[0:LANES, :] = jnp.concatenate(tall, axis=0).T
        for c in range(p.C):
            for a in range(tb):
                at = (a * p.C + c) * p.w
                store(c, slice(a * p.w, (a + 1) * p.w), nat[at : at + p.w, :])

    def put_mean(c, at, value):
        means[c, at, :] = value

    def put_pred(c, at, value):
        send[c * p.S3 + at.start : c * p.S3 + at.stop, :] = value

    by_owner(lambda b: mean_t[b] + shift_t[b], put_mean)
    by_owner(lambda b: pred[b * p.J : (b + 1) * p.J, :], put_pred)
    own[...] = means[place[0]]
    for c in range(p.C):
        send[(c + 1) * p.S3 - 1 : (c + 1) * p.S3, :] = squares


def out_kernel(p, recv, own, mean_out, loyalty_out):
    predicted = sum_chunks(p, recv, p.S3, 0, p.i8)
    value = own[...] - jnp.log(predicted)
    for q in range(p.h):
        mean_out[q * p.i8 : (q + 1) * p.i8, :] = moved(value, -q * p.J)[:, 0 : p.J]
    clip = clip_of(p, sum_chunks(p, recv, p.S3, p.S3 - 1, 1))
    for t in range(p.R // LANES):
        values = []
        for b in range(p.hh):
            at = (t * p.hh + b) * p.S3 + p.i8
            values.append(recv[at : at + p.oi, :] + clip * recv[at + p.oi : at + 2 * p.oi, :])
        for o in range(p.hh):
            row = moved(values[0], -o * p.RL)
            for b in range(1, p.hh):
                row = jnp.where(block_mask(p.RL, p.oi, b), moved(values[b], (b - o) * p.RL), row)
            loyalty_out[o * p.oi : (o + 1) * p.oi, t * LANES : (t + 1) * LANES] = row


def local(
    mean_utility,
    market_share,
    product_traits,
    taste_draws,
    taste_scale,
    type_weight,
    market_size,
    product_firm,
    firm_order,
    loyalty,
    firm_share,
):
    p = Plan(
        lax.axis_size("mkt"),
        lax.axis_size("grp"),
        mean_utility.shape[0],
        mean_utility.shape[1],
        taste_scale.shape[0],
        firm_share.shape[1],
        firm_share.shape[0],
        loyalty.shape[0],
    )
    place = jnp.stack([lax.axis_index("mkt"), lax.axis_index("grp")]).astype(jnp.int32)

    def exchange(x):
        return lax.all_to_all(x, "mkt", split_axis=0, concat_axis=0, tiled=True)

    def swap(x, bit):
        return lax.ppermute(x, "grp", [(q, q ^ bit) for q in range(p.Q)])

    order = firm_order.reshape(p.C, p.Q, p.own)
    order = jnp.pad(order, ((0, 0), (0, 0), (0, p.ownp - p.own)), constant_values=-1)
    order = order.reshape(p.C, p.Q, p.hh, p.oi).transpose(1, 2, 0, 3).reshape(p.Q * p.hh, p.C * p.oi)
    order = jnp.pad(order, ((0, 0), (0, LANES - p.C * p.oi)), constant_values=-1)
    if p.ownp > p.own:
        loyalty = jnp.pad(loyalty, ((0, p.ownp - p.own), (0, 0)))

    send = call(
        p,
        pack_kernel,
        sds((p.C * p.S, LANES)),
        (
            taste_scale,
            market_size,
            taste_draws.transpose(1, 0, 2),
            type_weight,
            loyalty,
            product_traits.transpose(2, 0, 1),
            product_firm,
            mean_utility,
            market_share,
        ),
        specs=[SM, SM] + [HBM] * 7,
        out_specs=HBM,
        scratch=(
            pltpu.VMEM((p.K, p.M, p.R), F32),
            pltpu.VMEM((p.M, p.R), F32),
            pltpu.VMEM((p.ownp, p.R), F32),
            pltpu.VMEM((p.K, p.M, p.J), F32),
            pltpu.VMEM((p.M, p.J), jnp.int32),
            pltpu.VMEM((p.M, p.J), F32),
            pltpu.VMEM((p.M, p.J), F32),
            pltpu.VMEM((p.C * p.S, LANES), F32),
            pltpu.SemaphoreType.DMA((7,)),
            pltpu.SemaphoreType.DMA((p.C,)),
        ),
    )
    tiles = sds((p.hh, p.J, LANES))
    firms_t, mean_t, shift_t, mass_t, mass_row, loy, draws_t, traits_t = call(
        p,
        prep_kernel,
        (
            tiles,
            tiles,
            tiles,
            sds((p.RL, p.ML)),
            sds((8, LANES)),
            sds((LANES, LANES)),
            sds((p.K, p.RL, p.ML)),
            sds((p.K, p.hh, p.J, LANES)),
        ),
        (exchange(send),),
        scratch=(pltpu.VMEM((max(LANES, p.PR), LANES), F32),),
    )
    rows = [loy]
    bit = 1
    while bit < p.Q:
        rows.append(swap(rows[0] if bit == 1 else jnp.concatenate(rows, axis=0), bit))
        bit *= 2
    taste, hot = call(
        p,
        taste_kernel,
        (sds((p.J, p.RL, p.ML)), sds((p.NS, p.F, p.u * p.ML), BF)),
        (draws_t, traits_t, firms_t),
    )
    table, share, columns = call(
        p,
        table_kernel,
        (sds((p.FP, LANES)), sds((p.FP, LANES)), sds((p.hh, LANES, LANES))),
        (place, order, firm_share, *rows),
        specs=[SM, VM, HBM] + [VM] * len(rows),
        scratch=(pltpu.VMEM((p.F, LANES), F32), pltpu.SemaphoreType.DMA(())),
    )
    half = sds((p.HR + 8, LANES))
    step_outs = (sds((p.PB, LANES)), half, half)
    step_scratch = (
        pltpu.VMEM((p.hh, 2 * p.RL, p.FP), BF),
        pltpu.VMEM((p.J, p.RL, p.ML), F32),
        pltpu.VMEM((2, p.NR, p.u * p.ML), BF),
        pltpu.VMEM((p.F, p.NR), F32),
    )
    fixed = (taste, hot, mass_t, mass_row)
    for step in range(ITERS):
        if step == 0:
            pred, keep, give = call(
                p,
                first_kernel,
                step_outs,
                (place, table, mean_t, *fixed),
                specs=[SM] + [VM] * 6,
                scratch=step_scratch,
            )
        else:
            table, mean_t, pred, keep, give = call(
                p,
                next_kernel,
                (sds((p.FP, LANES)), tiles) + step_outs,
                (place, recv, gap_mine, gap_other, table, mean_t, shift_t, *fixed),
                specs=[SM] + [VM] * 10,
                scratch=step_scratch,
            )
        mine = call(p, add_kernel, half, (keep, swap(give, 1)))
        bit = 2
        while 2 * bit < p.Q:
            mine = call(p, add_kernel, half, (mine, swap(mine, bit)))
            bit *= 2
        gap_mine = call(p, gap_kernel, half, (place, mine, swap(mine, bit), share), specs=[SM, VM, VM, VM])
        gap_other = swap(gap_mine, 1)
        if step < ITERS - 1:
            recv = exchange(call(p, send_kernel, sds((p.C * p.S2, LANES)), (gap_mine, gap_other, pred)))
    send, own = call(
        p,
        final_kernel,
        (sds((p.C * p.S3, LANES)), sds((p.i8, LANES))),
        (place, gap_mine, gap_other, table, columns, pred, mean_t, shift_t),
        specs=[SM] + [VM] * 7,
        scratch=(
            pltpu.VMEM((p.FP, LANES), F32),
            pltpu.VMEM((max(LANES, p.PR), LANES), F32),
            pltpu.VMEM((p.C, p.i8, LANES), F32),
        ),
    )
    mean_out, loyalty_out = call(
        p, out_kernel, (sds((p.M, p.J)), sds((p.ownp, p.R))), (exchange(send), own)
    )
    return (mean_out, loyalty_out[0 : p.own] if p.ownp > p.own else loyalty_out)


def solution(mesh):
    both = ("mkt", "grp")
    placed = (
        P(both, None),
        P(both, None),
        P(both, None, None),
        P(both, None, None),
        P(),
        P(both, None),
        P(both),
        P(both, None),
        P(),
        P(both, None),
        P(),
    )
    return jax.shard_map(
        local,
        mesh=mesh,
        in_specs=placed,
        out_specs=(P(both, None), P(both, None)),
        check_vma=False,
    )
```

time: 557 us -> 148 us (0.27)
  waiting for transfers between devices: 197 us -> 22 us
  blocking collectives: 235 us -> 64.1 us
  Pallas kernels: 0 us -> 46 us
  matrix products: 37.9 us -> 0 us
  local copies, waits for them, and re-layouts: 38.1 us -> 7.82 us
  other arithmetic: 23.5 us -> 0.08 us
  between operations: 16 us -> 0.78 us
    psum x4 -> x0, blocking collectives: 183 us -> none  [the longest x3 116 us: local(): squares = lax.psum(jnp.sum(gap * gap), ('mkt', 'grp'))]
    all_gather x3 -> x0, waiting for transfers between devices: 154 us -> none  [local(): table = lax.all_gather(owned, ('mkt', 'grp'), axis=0, tiled=True)]
    pallas_call x0 -> x17, Pallas kernels: none -> 46 us  [call(): pl.pallas_call(functools.partial(kernel, p), out_shape=outs, in_specs=spe...]
    all_to_all x2 -> x0, waiting for transfers between devices: 42.4 us -> none  [local(): lax.all_to_all(blocks, ('mkt', 'grp'), split_axis=0, concat_axis=0, tiled...]
    dot_general x7 -> x0, matrix products: 37.9 us -> none  [the longest x3 16.6 us: market_terms(): jnp.einsum('mjr,mr->mj', choice_prob, type_weight, precision=lax.Precisio...]
    gather x6 -> x0, local copies, waits for them, and re-layouts: 31.6 us -> none  [the longest x3 24 us: market_terms(): jnp.take(table, row_ids, axis=0)]
    ppermute x0 -> x11, waiting for transfers between devices: none -> 22 us  [swap(): return lax.ppermute(x, 'grp', [(q, q ^ bit) for q in range(p.Q)])]
    reduce_sum x9 -> x0, other arithmetic: 15.5 us -> none  [the longest x2 8.1 us: market_terms(): choice_prob = expu / (1.0 + jnp.sum(expu, axis=1, keepdims=True))]
  transfers between devices with their start and end apart: 5 -> 11, of which waited for: 4 -> 11; matrix products, arithmetic and copies ran while one was open for 5% -> 1% of each run, Pallas kernels for 0% -> 2%
where the time goes in v2:
time: 148 us; the launch traced here: 147 us
  blocking collectives  64.1 us (43%)
  Pallas kernels  46 us (31%)
  waiting for transfers between devices  22 us (15%)
  local copies, waits for them, and re-layouts  7.82 us (5%)
  starting transfers between devices  6.63 us (4%)
    all_to_all x4, blocking collectives, exchange(): return lax.all_to_all(x, 'mkt', split_axis=0, concat_axis=0, tiled=True)  64.1 us
    pallas_call x17, Pallas kernels, call(): pl.pallas_call(functools.partial(kernel, p), out_shape=outs, in_specs=spe...  46 us
    ppermute x11, waiting for transfers between devices, swap(): return lax.ppermute(x, 'grp', [(q, q ^ bit) for q in range(p.Q)])  22 us
    unnamed x20, local copies, waits for them, and re-layouts  6.97 us
    ppermute x11, starting transfers between devices, swap(): return lax.ppermute(x, 'grp', [(q, q ^ bit) for q in range(p.Q)])  6.63 us
  transfers between devices with their start and end apart: 11, of which 11 were waited for; matrix products, arithmetic and copies ran while one was open for 1% of the time, Pallas kernels for 2%

profile of v2, /device:TPU:0, one launch (start us, length us, event | category | flops | bytes accessed | tf_op | source)
XLA Modules:
  0.0 147.4 jit_solution(14577697569961716112)
XLA Ops:
  0.7 1.1 copy-done.1
  1.8 0.8 copy-done.2
  2.6 0.8 copy-done.3
  3.4 0.8 copy-done.4
  4.2 0.7 copy-done.5
  4.9 0.7 copy-done.6
  5.6 0.7 copy-done.7
  6.3 0.7 copy-done.8
  7.0 0.7 copy-done.9
  7.6 2.1 %shard_map.122 = f32[1408,128]{1,0:T(8,128)S(1)} custom-call(f32[5]{0:T(128)S(1)} %copy-done.8, f32[16]{0:T(128)S(1)} %copy-done.9, f32[5,16,1024]{2,1,0:T(8,128)S(1)} %bitcast.24, f32[16,1024]{1,0:T(8,128)S(1)} %copy-done.2, f32[16,1024]{1,0:T(8,128)S(1)} %copy-done.3, f32[5,16,64]{2,1,0:T(8,128)S(1)} %bitcast.26, s32[16,64]{1,0:T(8,128)S(1)} %copy-done.5, ...), custom_call_target="tpu_custom_call" | custom-call | tf_op jit(solution)/shard_map/pallas_call | solution.py:59
  9.8 25.9 %all_to_all.44 = f32[8,176,128]{2,1,0:T(8,128)S(1)} all-to-all(f32[8,176,128]{2,1,0:T(8,128)S(1)} %bitcast.18), channel_id=1, replica_groups=mesh['mkt'=8,'grp'=4] {'mkt'}, dimensions={0} | all-to-all | bytes 1441792 | tf_op jit(solution)/shard_map/all_to_all | solution.py:508
  35.7 0.3 shard_map.123
  36.0 0.1 collective-permute-start
  36.1 1.2 collective-permute-done.refs_1_
  37.3 1.6 %collective-permute-start.1 = (f32[256,128]{1,0:T(8,128)S(1)}, f32[256,128]{1,0:T(8,128)S(1)}, u32[]{:S(2)}, u32[]{:S(2)}) collective-permute-start(f32[256,128]{1,0:T(8,128)S(1)} %pad_maximum_fusion), channel_id=1, source_target_pairs={{0,2},{1,3},{2,0},{3,1},{4,6},{5,7},{6,4},{7,5},{8,10},{9,11},{10,... | collective-permute-start | bytes 393224 | tf_op jit(solution)/shard_map/ppermute | solution.py:511
  38.9 0.8 reshape.20
  39.7 0.1 reshape.21.order
  39.8 0.1 pad_add_fusion.place
  39.8 2.8 %shard_map.125 = (f32[64,128,128]{2,1,0:T(8,128)S(1)}, bf16[32,512,256]{2,1,0:T(8,128)(2,1)S(1)}) custom-call(f32[5,128,128]{2,1,0:T(8,128)S(1)} %get-tuple-element.33.draws_t, f32[5,1,64,128]{3,2,1,0:T(8,128)S(1)} %get-tuple-element.34.traits_t, f32[1,64,128]{2,1,0:T(8,128)S(1)} %get-tuple-element.35.firms_t), custom_call_target="tpu_custom_call" | custom-call | tf_op jit(solution)/shard_map/pallas_call | solution.py:59
  42.6 0.3 collective-permute-done.1.refs_2_
  42.9 1.2 shard_map.124
  44.1 11.9 %shard_map.126 = (f32[64,128]{1,0:T(8,128)S(1)}, f32[264,128]{1,0:T(8,128)S(1)}, f32[264,128]{1,0:T(8,128)S(1)}) custom-call(s32[2]{0:T(128)S(1)} %pad_add_fusion.place, f32[512,128]{1,0:T(8,128)S(1)} %get-tuple-element.31.table.table_in, f32[1,64,128]{2,1,0:T(8,128)S(1)} %get-tuple-element.32.mean_t.mean_in, f32[64,128,128]{2,1,0:T(8,128)S(1)} %get-tuple-element.36.taste, ...), custom_call_target="tpu_custom_call" | custom-call | tf_op jit(solution)/shard_map/pallas_call | solution.py:59
  56.0 0.1 collective-permute-start.2
  56.1 1.3 collective-permute-done.2.b
  57.5 1.6 %collective-permute-start.3 = (f32[264,128]{1,0:T(8,128)S(1)}, f32[264,128]{1,0:T(8,128)S(1)}, u32[]{:S(2)}, u32[]{:S(2)}) collective-permute-start(f32[264,128]{1,0:T(8,128)S(1)} %shard_map.127.mine), channel_id=1, source_target_pairs={{0,2},{1,3},{2,0},{3,1},{4,6},{5,7},{6,4},{7,5},{8,10},{9,11},{10,... | collective-permute-start | bytes 405512 | tf_op jit(solution)/shard_map/ppermute | solution.py:511
  59.1 4.1 %collective-permute-done.3.other = f32[264,128]{1,0:T(8,128)S(1)} collective-permute-done((f32[264,128]{1,0:T(8,128)S(1)}, f32[264,128]{1,0:T(8,128)S(1)}, u32[]{:S(2)}, u32[]{:S(2)}) %collective-permute-start.3) | collective-permute-done | bytes 135200 | tf_op jit(solution)/shard_map/ppermute | solution.py:511
  63.2 0.7 shard_map.128.gap_mine
  63.9 0.0 collective-permute-start.4
  63.9 1.4 collective-permute-done.4.gap_other
  65.3 14.0 %all_to_all.45 = f32[8,72,128]{2,1,0:T(8,128)S(1)} all-to-all(f32[8,72,128]{2,1,0:T(8,128)S(1)} %bitcast.21), channel_id=1, replica_groups=mesh['mkt'=8,'grp'=4] {'mkt'}, dimensions={0} | all-to-all | bytes 589824 | tf_op jit(solution)/shard_map/all_to_all | solution.py:508
  79.2 11.9 %shard_map.130 = (f32[512,128]{1,0:T(8,128)S(1)}, f32[1,64,128]{2,1,0:T(8,128)S(1)}, f32[64,128]{1,0:T(8,128)S(1)}, f32[264,128]{1,0:T(8,128)S(1)}, f32[264,128]{1,0:T(8,128)S(1)}) custom-call(s32[2]{0:T(128)S(1)} %pad_add_fusion.place, f32[576,128]{1,0:T(8,128)S(1)} %bitcast.20, f32[264,128]{1,0:T(8,128)S(1)} %shard_map.128.gap_mine, ...), custom_call_target="tpu_custom_call" | custom-call | tf_op jit(solution)/shard_map/pallas_call | solution.py:59
  91.2 0.1 collective-permute-start.5
  91.3 1.3 collective-permute-done.5.b
  92.6 1.6 %collective-permute-start.6 = (f32[264,128]{1,0:T(8,128)S(1)}, f32[264,128]{1,0:T(8,128)S(1)}, u32[]{:S(2)}, u32[]{:S(2)}) collective-permute-start(f32[264,128]{1,0:T(8,128)S(1)} %shard_map.131.mine), channel_id=1, source_target_pairs={{0,2},{1,3},{2,0},{3,1},{4,6},{5,7},{6,4},{7,5},{8,10},{9,11},{10,... | collective-permute-start | bytes 405512 | tf_op jit(solution)/shard_map/ppermute | solution.py:511
  94.2 4.1 %collective-permute-done.6.other = f32[264,128]{1,0:T(8,128)S(1)} collective-permute-done((f32[264,128]{1,0:T(8,128)S(1)}, f32[264,128]{1,0:T(8,128)S(1)}, u32[]{:S(2)}, u32[]{:S(2)}) %collective-permute-start.6) | collective-permute-done | bytes 135200 | tf_op jit(solution)/shard_map/ppermute | solution.py:511
  98.3 0.7 shard_map.132.gap_mine
  99.0 1.4 collective-permute-done.7.gap_other
  100.4 13.3 %all_to_all.46 = f32[8,72,128]{2,1,0:T(8,128)S(1)} all-to-all(f32[8,72,128]{2,1,0:T(8,128)S(1)} %bitcast.22), channel_id=1, replica_groups=mesh['mkt'=8,'grp'=4] {'mkt'}, dimensions={0} | all-to-all | bytes 589824 | tf_op jit(solution)/shard_map/all_to_all | solution.py:508
  113.7 11.9 %shard_map.134 = (f32[512,128]{1,0:T(8,128)S(1)}, f32[1,64,128]{2,1,0:T(8,128)S(1)}, f32[64,128]{1,0:T(8,128)S(1)}, f32[264,128]{1,0:T(8,128)S(1)}, f32[264,128]{1,0:T(8,128)S(1)}) custom-call(s32[2]{0:T(128)S(1)} %pad_add_fusion.place, f32[576,128]{1,0:T(8,128)S(1)} %bitcast.19, f32[264,128]{1,0:T(8,128)S(1)} %shard_map.132.gap_mine, ...), custom_call_target="tpu_custom_call" | custom-call | tf_op jit(solution)/shard_map/pallas_call | solution.py:59
  125.7 0.1 collective-permute-start.8
  125.8 1.3 collective-permute-done.8.b
  127.1 1.6 %collective-permute-start.9 = (f32[264,128]{1,0:T(8,128)S(1)}, f32[264,128]{1,0:T(8,128)S(1)}, u32[]{:S(2)}, u32[]{:S(2)}) collective-permute-start(f32[264,128]{1,0:T(8,128)S(1)} %shard_map.135.mine), channel_id=1, source_target_pairs={{0,2},{1,3},{2,0},{3,1},{4,6},{5,7},{6,4},{7,5},{8,10},{9,11},{10,... | collective-permute-start | bytes 405512 | tf_op jit(solution)/shard_map/ppermute | solution.py:511
  128.7 4.1 %collective-permute-done.9.other = f32[264,128]{1,0:T(8,128)S(1)} collective-permute-done((f32[264,128]{1,0:T(8,128)S(1)}, f32[264,128]{1,0:T(8,128)S(1)}, u32[]{:S(2)}, u32[]{:S(2)}) %collective-permute-start.9) | collective-permute-done | bytes 135200 | tf_op jit(solution)/shard_map/ppermute | solution.py:511
  132.8 0.7 shard_map.136.gap_mine
  133.5 1.4 collective-permute-done.10.gap_other
  134.9 0.9 shard_map.137
  135.8 10.9 %all_to_all.47 = f32[8,48,128]{2,1,0:T(8,128)S(1)} all-to-all(f32[8,48,128]{2,1,0:T(8,128)S(1)} %bitcast.25), channel_id=1, replica_groups=mesh['mkt'=8,'grp'=4] {'mkt'}, dimensions={0} | all-to-all | bytes 393216 | tf_op jit(solution)/shard_map/all_to_all | solution.py:508
  146.7 0.7 shard_map.138
  (20 shorter events, 0.1 us)
Async XLA Ops:
  0.6 42.3 %copy-start = (f32[512,1024]{1,0:T(8,128)S(1)}, f32[512,1024]{1,0:T(8,128)}, u32[]{:S(2)}) copy-start(f32[512,1024]{1,0:T(8,128)} %share_h.3) | copy-start | bytes 6291460
  0.6 1.1 copy-start.1
  1.8 0.8 copy-start.2
  2.6 0.8 copy-start.3
  3.4 0.8 copy-start.4
  4.2 0.7 copy-start.5
  4.9 0.7 copy-start.6
  5.6 0.7 copy-start.7
  6.3 0.7 copy-start.8
  7.0 0.7 copy-start.9
  36.0 1.3 collective-permute-start
  37.3 5.6 %collective-permute-start.1 = (f32[256,128]{1,0:T(8,128)S(1)}, f32[256,128]{1,0:T(8,128)S(1)}, u32[]{:S(2)}, u32[]{:S(2)}) collective-permute-start(f32[256,128]{1,0:T(8,128)S(1)} %pad_maximum_fusion), channel_id=1, source_target_pairs={{0,2},{1,3},{2,0},{3,1},{4,6},{5,7},{6,4},{7,5},{8,10},{9,11},{10,... | collective-permute-start | bytes 393224 | tf_op jit(solution)/shard_map/ppermute | solution.py:511
  56.0 1.4 collective-permute-start.2
  57.5 5.7 %collective-permute-start.3 = (f32[264,128]{1,0:T(8,128)S(1)}, f32[264,128]{1,0:T(8,128)S(1)}, u32[]{:S(2)}, u32[]{:S(2)}) collective-permute-start(f32[264,128]{1,0:T(8,128)S(1)} %shard_map.127.mine), channel_id=1, source_target_pairs={{0,2},{1,3},{2,0},{3,1},{4,6},{5,7},{6,4},{7,5},{8,10},{9,11},{10,... | collective-permute-start | bytes 405512 | tf_op jit(solution)/shard_map/ppermute | solution.py:511
  63.9 1.4 collective-permute-start.4
  91.2 1.4 collective-permute-start.5
  92.6 5.7 %collective-permute-start.6 = (f32[264,128]{1,0:T(8,128)S(1)}, f32[264,128]{1,0:T(8,128)S(1)}, u32[]{:S(2)}, u32[]{:S(2)}) collective-permute-start(f32[264,128]{1,0:T(8,128)S(1)} %shard_map.131.mine), channel_id=1, source_target_pairs={{0,2},{1,3},{2,0},{3,1},{4,6},{5,7},{6,4},{7,5},{8,10},{9,11},{10,... | collective-permute-start | bytes 405512 | tf_op jit(solution)/shard_map/ppermute | solution.py:511
  99.0 1.4 collective-permute-start.7
  125.7 1.4 collective-permute-start.8
  127.1 5.7 %collective-permute-start.9 = (f32[264,128]{1,0:T(8,128)S(1)}, f32[264,128]{1,0:T(8,128)S(1)}, u32[]{:S(2)}, u32[]{:S(2)}) collective-permute-start(f32[264,128]{1,0:T(8,128)S(1)} %shard_map.135.mine), channel_id=1, source_target_pairs={{0,2},{1,3},{2,0},{3,1},{4,6},{5,7},{6,4},{7,5},{8,10},{9,11},{10,... | collective-permute-start | bytes 405512 | tf_op jit(solution)/shard_map/ppermute | solution.py:511
  133.5 1.4 collective-permute-start.10

commit v3 on v2

--- a/solution.py
+++ b/solution.py
@@ -35,6 +35,7 @@
         self.oi = self.ownp // self.hh
         self.u = max(1, 256 // self.ML)
         self.NS = products // self.u
+        self.per = min(16, self.NS)
         self.NR = max(LANES, 2 * self.RL)
         self.s_draws = 0
         self.s_mass = self.s_draws + traits * self.ii
@@ -55,14 +56,14 @@
 HBM = pl.BlockSpec(memory_space=pltpu.HBM)
 
 
-def call(p, kernel, outs, args, scratch=(), specs=None, out_specs=None, flops=0):
+def call(p, kernel, outs, args, scratch=(), specs=None, out_specs=None, vmem=None):
     return pl.pallas_call(
         functools.partial(kernel, p),
         out_shape=outs,
         in_specs=specs or [VM] * len(args),
         out_specs=out_specs or jax.tree.map(lambda _: VM, outs),
         scratch_shapes=list(scratch),
-        compiler_params=pltpu.CompilerParams(vmem_limit_bytes=p.vmem * 2**20),
+        compiler_params=pltpu.CompilerParams(vmem_limit_bytes=(vmem or p.vmem) * 2**20),
     )(*args)
 
 
@@ -243,18 +244,17 @@
                     value = term if value is None else value + term
                 taste[j, :, at] = value
                 row = firms_t[b, pl.ds(j, 1), :]
-                to = slice(v * p.ML + b * LANES, v * p.ML + (b + 1) * LANES)
                 for base in range(0, p.F, rows):
                     want = jnp.broadcast_to(row - float(base), (rows, LANES)).astype(BF)
-                    hot[n, base : base + rows, to] = jnp.where(firm == want, jnp.ones((), BF), jnp.zeros((), BF))
+                    hot[j, b, base : base + rows, :] = jnp.where(firm == want, jnp.ones((), BF), jnp.zeros((), BF))
         return 0
 
     lax.fori_loop(0, p.NS, body, 0)
 
 
-def table_kernel(p, place, order, share_h, *refs):
+def table_kernel(p, order, share_h, *refs):
     blocks, (table, share, columns, tile, sem) = refs[:-5], refs[-5:]
-    lane = place[0] * p.RL
+    lane = lax.axis_index("mkt") * p.RL
     start = pl.multiple_of(lane // LANES * LANES, LANES)
     copy = pltpu.make_async_copy(share_h.at[:, pl.ds(start, LANES)], tile, sem)
     copy.start()
@@ -263,7 +263,7 @@
     blocks = [ref[at : at + LANES, :] for ref in blocks for at in range(0, ref.shape[0], LANES)]
     for s, block in enumerate(blocks):
         pieces = jnp.concatenate(split3(block), axis=1)
-        member = place[1] ^ s
+        member = lax.axis_index("grp") ^ s
         for b in range(p.hh):
             hot = (firm == order[pl.ds(member * p.hh + b, 1), :]).astype(F32).astype(BF)
             found = dot(hot, pieces)
@@ -273,7 +273,7 @@
             total = total + found
     pack_table(p, fold(p, total), table)
     for b in range(p.hh):
-        row = order[pl.ds(place[1] * p.hh + b, 1), :].astype(F32)
+        row = order[pl.ds(lax.axis_index("grp") * p.hh + b, 1), :].astype(F32)
         columns[b] = jnp.broadcast_to(row, (LANES, LANES)).T
     copy.wait()
     if p.hh == 1:
@@ -303,19 +303,18 @@
     return total
 
 
-def step_body(p, place, table, mean_of, taste, hot, mass_t, mass_row, pred, keep, give, tab, expu, parts, acc):
+def step_body(p, table, mean_of, taste, hot, mass_t, mass_row, pred, keep, give, tab, expu, parts, acc):
     turned = table[...].T
     for q, piece in enumerate(split2(turned)):
-        for b in range(p.hh):
-            tab[b, q * p.RL : (q + 1) * p.RL, :] = piece[b * p.RL : (b + 1) * p.RL, :]
+        for t in range(p.F // LANES):
+            b, at = divmod(t * LANES, p.FP)
+            tab[t, q * p.RL : (q + 1) * p.RL, :] = piece[b * p.RL : (b + 1) * p.RL, at : at + LANES]
+
+    def hot_of(n):
+        return jnp.concatenate([hot[n * p.u + v, b] for v in range(p.u) for b in range(p.hh)], axis=1)
 
     def gather(n, total):
-        if p.hh == 1:
-            found = dot(tab[0], hot[n])
-        else:
-            found = dot(tab[0], hot[n, 0 : p.FP, :])
-            for b in range(1, p.hh):
-                found = found + dot(tab[b], hot[n, b * p.FP : (b + 1) * p.FP, :])
+        found = dot(jnp.concatenate([tab[t] for t in range(p.F // LANES)], axis=1), hot_of(n))
         found = found[0 : p.RL] + found[p.RL : 2 * p.RL]
         for v in range(p.u):
             j = n * p.u + v
@@ -326,12 +325,12 @@
             total = total + e
         return total
 
-    total = lax.fori_loop(0, p.NS, gather, jnp.zeros((p.RL, p.ML), F32), unroll=2)
+    total = lax.fori_loop(0, p.NS, gather, jnp.zeros((p.RL, p.ML), F32), unroll=min(16, p.NS))
     scale = mass_t[...] / (1.0 + total)
     acc[...] = jnp.zeros_like(acc)
     if p.NR > 2 * p.RL:
         parts[...] = jnp.zeros_like(parts)
-    per = 2
+    per = p.per
 
     def scatter(n, _):
         value = None
@@ -340,13 +339,15 @@
                 j = (n * per + s) * p.u + v
                 x = expu[j] * scale
                 hi, lo = split2(x)
-                at = slice(v * p.ML, (v + 1) * p.ML)
-                parts[s, 0 : p.RL, at] = hi
-                parts[s, p.RL : 2 * p.RL, at] = lo
+                for b in range(p.hh):
+                    at = slice(b * LANES, (b + 1) * LANES)
+                    parts[s, v * p.hh + b, 0 : p.RL, :] = hi[:, at]
+                    parts[s, v * p.hh + b, p.RL : 2 * p.RL, :] = lo[:, at]
                 row = jnp.sum(x, axis=0, keepdims=True)
                 for b in range(p.hh):
                     pred[pl.ds(b * p.J + j, 1), :] = row[:, b * LANES : (b + 1) * LANES]
-            term = dot_t(hot[n * per + s], parts[s])
+            right = jnp.concatenate([parts[s, t] for t in range(p.u * p.hh)], axis=1)
+            term = dot_t(hot_of(n * per + s), right)
             value = term if value is None else value + term
         acc[...] += value
         return 0
@@ -359,39 +360,48 @@
         acc[:, 0:LANES] = full
     else:
         pack_table(p, fold(p, full), acc.at[0 : p.FP, 0:LANES])
-    mine = (place[1] & 1) * p.HR
+    mine = (lax.axis_index("grp") & 1) * p.HR
     keep[0 : p.HR, :] = acc[pl.ds(pl.multiple_of(mine, 8), p.HR), 0:LANES]
     give[0 : p.HR, :] = acc[pl.ds(pl.multiple_of(p.HR - mine, 8), p.HR), 0:LANES]
     keep[p.HR :, :] = mass_row[...]
     give[p.HR :, :] = mass_row[...]
 
 
-def first_kernel(p, place, table, mean_t, taste, hot, mass_t, mass_row, pred, keep, give, *scratch):
-    step_body(p, place, table, mean_t, taste, hot, mass_t, mass_row, pred, keep, give, *scratch)
+def step_scratch_of(p):
+    return (
+        pltpu.VMEM((p.F // LANES, 2 * p.RL, LANES), BF),
+        pltpu.VMEM((p.J, p.RL, p.ML), F32),
+        pltpu.VMEM((p.per, p.u * p.hh, p.NR, LANES), BF),
+        pltpu.VMEM((p.F, p.NR), F32),
+    )
+
+
+def first_kernel(p, table, mean_t, taste, hot, mass_t, mass_row, pred, keep, give, *scratch):
+    step_body(p, table, mean_t, taste, hot, mass_t, mass_row, pred, keep, give, *scratch)
 
 
 def next_kernel(
-    p, place, recv, gap_mine, gap_other, table_in, mean_in, shift_t, taste, hot, mass_t, mass_row,
+    p, recv, gap_mine, gap_other, table_in, mean_in, shift_t, taste, hot, mass_t, mass_row,
     table, mean_t, pred, keep, give, *scratch
 ):
     clip = clip_of(p, sum_chunks(p, recv, p.S2, p.PB, 1))
-    mine = (place[1] & 1) * p.HR
+    mine = (lax.axis_index("grp") & 1) * p.HR
     for ref, start in ((gap_mine, mine), (gap_other, p.HR - mine)):
         at = pl.ds(pl.multiple_of(start, 8), p.HR)
         table[at, :] = table_in[at, :] + clip * ref[0 : p.HR, :]
     for b in range(p.hh):
         total = sum_chunks(p, recv, p.S2, b * p.J, p.J)
         mean_t[b] = mean_in[b] + shift_t[b] - jnp.log(total)
-    step_body(p, place, table, mean_t, taste, hot, mass_t, mass_row, pred, keep, give, *scratch)
+    step_body(p, table, mean_t, taste, hot, mass_t, mass_row, pred, keep, give, *scratch)
 
 
 def add_kernel(p, a, b, out):
     out[...] = a[...] + b[...]
 
 
-def gap_kernel(p, place, mine, other, share, gap):
+def gap_kernel(p, mine, other, share, gap):
     total = mine[...] + other[...]
-    at = pl.ds(pl.multiple_of((place[1] & 1) * p.HR, 8), p.HR)
+    at = pl.ds(pl.multiple_of((lax.axis_index("grp") & 1) * p.HR, 8), p.HR)
     value = jnp.log(share[at, :]) - jnp.log(total[0 : p.HR, :] / total[p.HR : p.HR + 1, :])
     gap[0 : p.HR, :] = value
     rows = jnp.sum(value * value, axis=0, keepdims=True)
@@ -406,8 +416,8 @@
         send[c * p.S2 + p.PB : (c + 1) * p.S2, :] = squares
 
 
-def final_kernel(p, place, gap_mine, gap_other, table, columns, pred, mean_t, shift_t, send, own, gap, nat, means):
-    mine = (place[1] & 1) * p.HR
+def final_kernel(p, gap_mine, gap_other, table, columns, pred, mean_t, shift_t, send, own, gap, nat, means):
+    mine = (lax.axis_index("grp") & 1) * p.HR
     for ref, start in ((gap_mine, mine), (gap_other, p.HR - mine)):
         gap[pl.ds(pl.multiple_of(start, 8), p.HR), :] = ref[0 : p.HR, :]
     squares = gap_mine[p.HR : p.HR + 1, :] + gap_other[p.HR : p.HR + 1, :]
@@ -456,7 +466,7 @@
 
     by_owner(lambda b: mean_t[b] + shift_t[b], put_mean)
     by_owner(lambda b: pred[b * p.J : (b + 1) * p.J, :], put_pred)
-    own[...] = means[place[0]]
+    own[...] = means[lax.axis_index("mkt")]
     for c in range(p.C):
         send[(c + 1) * p.S3 - 1 : (c + 1) * p.S3, :] = squares
 
@@ -502,7 +512,6 @@
         firm_share.shape[0],
         loyalty.shape[0],
     )
-    place = jnp.stack([lax.axis_index("mkt"), lax.axis_index("grp")]).astype(jnp.int32)
 
     def exchange(x):
         return lax.all_to_all(x, "mkt", split_axis=0, concat_axis=0, tiled=True)
@@ -532,6 +541,7 @@
             mean_utility,
             market_share,
         ),
+        vmem=60,
         specs=[SM, SM] + [HBM] * 7,
         out_specs=HBM,
         scratch=(
@@ -572,25 +582,20 @@
     taste, hot = call(
         p,
         taste_kernel,
-        (sds((p.J, p.RL, p.ML)), sds((p.NS, p.F, p.u * p.ML), BF)),
+        (sds((p.J, p.RL, p.ML)), sds((p.J, p.hh, p.F, LANES), BF)),
         (draws_t, traits_t, firms_t),
     )
     table, share, columns = call(
         p,
         table_kernel,
         (sds((p.FP, LANES)), sds((p.FP, LANES)), sds((p.hh, LANES, LANES))),
-        (place, order, firm_share, *rows),
-        specs=[SM, VM, HBM] + [VM] * len(rows),
+        (order, firm_share, *rows),
+        specs=[VM, HBM] + [VM] * len(rows),
         scratch=(pltpu.VMEM((p.F, LANES), F32), pltpu.SemaphoreType.DMA(())),
     )
     half = sds((p.HR + 8, LANES))
     step_outs = (sds((p.PB, LANES)), half, half)
-    step_scratch = (
-        pltpu.VMEM((p.hh, 2 * p.RL, p.FP), BF),
-        pltpu.VMEM((p.J, p.RL, p.ML), F32),
-        pltpu.VMEM((2, p.NR, p.u * p.ML), BF),
-        pltpu.VMEM((p.F, p.NR), F32),
-    )
+    step_scratch = step_scratch_of(p)
     fixed = (taste, hot, mass_t, mass_row)
     for step in range(ITERS):
         if step == 0:
@@ -598,8 +603,7 @@
                 p,
                 first_kernel,
                 step_outs,
-                (place, table, mean_t, *fixed),
-                specs=[SM] + [VM] * 6,
+                (table, mean_t, *fixed),
                 scratch=step_scratch,
             )
         else:
@@ -607,8 +611,7 @@
                 p,
                 next_kernel,
                 (sds((p.FP, LANES)), tiles) + step_outs,
-                (place, recv, gap_mine, gap_other, table, mean_t, shift_t, *fixed),
-                specs=[SM] + [VM] * 10,
+                (recv, gap_mine, gap_other, table, mean_t, shift_t, *fixed),
                 scratch=step_scratch,
             )
         mine = call(p, add_kernel, half, (keep, swap(give, 1)))
@@ -616,7 +619,7 @@
         while 2 * bit < p.Q:
             mine = call(p, add_kernel, half, (mine, swap(mine, bit)))
             bit *= 2
-        gap_mine = call(p, gap_kernel, half, (place, mine, swap(mine, bit), share), specs=[SM, VM, VM, VM])
+        gap_mine = call(p, gap_kernel, half, (mine, swap(mine, bit), share))
         gap_other = swap(gap_mine, 1)
         if step < ITERS - 1:
             recv = exchange(call(p, send_kernel, sds((p.C * p.S2, LANES)), (gap_mine, gap_other, pred)))
@@ -624,8 +627,7 @@
         p,
         final_kernel,
         (sds((p.C * p.S3, LANES)), sds((p.i8, LANES))),
-        (place, gap_mine, gap_other, table, columns, pred, mean_t, shift_t),
-        specs=[SM] + [VM] * 7,
+        (gap_mine, gap_other, table, columns, pred, mean_t, shift_t),
         scratch=(
             pltpu.VMEM((p.FP, LANES), F32),
             pltpu.VMEM((max(LANES, p.PR), LANES), F32),

time: 148 us -> 121 us (0.82)
  Pallas kernels: 46 us -> 25.6 us
  local copies, waits for them, and re-layouts: 7.82 us -> 0.85 us
    pallas_call x17, Pallas kernels: 46 us -> 25.6 us  [call(): pl.pallas_call(functools.partial(kernel, p), out_shape=outs, in_specs=spe...]
    unnamed x20 -> x2, local copies, waits for them, and re-layouts: 6.97 us -> 0.01 us
where the time goes in v3:
time: 121 us; the launch traced here: 120 us
  blocking collectives  64.3 us (53%)
  Pallas kernels  25.6 us (21%)
  waiting for transfers between devices  22.1 us (18%)
  starting transfers between devices  6.63 us (5%)
    all_to_all x4, blocking collectives, exchange(): return lax.all_to_all(x, 'mkt', split_axis=0, concat_axis=0, tiled=True)  64.3 us
    pallas_call x17, Pallas kernels, call(): pl.pallas_call(functools.partial(kernel, p), out_shape=outs, in_specs=spe...  25.6 us
    ppermute x11, waiting for transfers between devices, swap(): return lax.ppermute(x, 'grp', [(q, q ^ bit) for q in range(p.Q)])  22.1 us
    ppermute x11, starting transfers between devices, swap(): return lax.ppermute(x, 'grp', [(q, q ^ bit) for q in range(p.Q)])  6.63 us
  transfers between devices with their start and end apart: 11, of which 11 were waited for; matrix products, arithmetic and copies ran while one was open for 1% of the time, Pallas kernels for 2%

profile of v3, /device:TPU:0, one launch (start us, length us, event | category | flops | bytes accessed | tf_op | source)
XLA Modules:
  0.0 120.3 jit_solution(16436702293675312302)
XLA Ops:
  0.6 0.0 copy-start
  0.6 3.0 %shard_map.122 = f32[1408,128]{1,0:T(8,128)} custom-call(f32[5]{0:T(128)} %scale.1, f32[16]{0:T(128)} %size.1, f32[5,16,1024]{2,1,0:T(8,128)} %bitcast.23, f32[16,1024]{1,0:T(8,128)} %weight_h.1, f32[16,1024]{1,0:T(8,128)} %loyalty_h.1, f32[5,16,64]{2,1,0:T(8,128)} %bitcast.25, s32[16,64]{1,0:T(8,128)} %firms_h.1, f32[16,64]{1,0:T(8,128)} %mean_h.1, ...), custom_call_target="tpu_custom_call" | custom-call | tf_op jit(solution)/shard_map/pallas_call | solution.py:60
  3.7 26.1 %all_to_all.44 = f32[8,176,128]{2,1,0:T(8,128)S(1)} all-to-all(f32[8,176,128]{2,1,0:T(8,128)} %bitcast.22), channel_id=1, replica_groups=mesh['mkt'=8,'grp'=4] {'mkt'}, dimensions={0} | all-to-all | bytes 1441792 | tf_op jit(solution)/shard_map/all_to_all | solution.py:517
  29.8 0.3 shard_map.123
  30.1 0.1 collective-permute-start
  30.2 1.2 %collective-permute-done.refs_1_ = f32[128,128]{1,0:T(8,128)S(1)} collective-permute-done((f32[128,128]{1,0:T(8,128)S(1)}, f32[128,128]{1,0:T(8,128)S(1)}, u32[]{:S(2)}, u32[]{:S(2)}) %collective-permute-start) | collective-permute-done | bytes 65568 | tf_op jit(solution)/shard_map/ppermute | solution.py:520
  31.4 1.6 %collective-permute-start.1 = (f32[256,128]{1,0:T(8,128)S(1)}, f32[256,128]{1,0:T(8,128)S(1)}, u32[]{:S(2)}, u32[]{:S(2)}) collective-permute-start(f32[256,128]{1,0:T(8,128)S(1)} %pad_maximum_fusion), channel_id=1, source_target_pairs={{0,2},{1,3},{2,0},{3,1},{4,6},{5,7},{6,4},{7,5},{8,10},{9,11},{10,... | collective-permute-start | bytes 393224 | tf_op jit(solution)/shard_map/ppermute | solution.py:520
  33.0 0.8 reshape.20
  33.8 0.1 reshape.21.order
  33.9 2.8 %shard_map.125 = (f32[64,128,128]{2,1,0:T(8,128)S(1)}, bf16[64,1,512,128]{3,2,1,0:T(8,128)(2,1)S(1)}) custom-call(f32[5,128,128]{2,1,0:T(8,128)S(1)} %get-tuple-element.33.draws_t, f32[5,1,64,128]{3,2,1,0:T(8,128)S(1)} %get-tuple-element.34.traits_t, f32[1,64,128]{2,1,0:T(8,128)S(1)} %get-tuple-element.35.firms_t), custom_call_target="tpu_custom_call" | custom-call | tf_op jit(solution)/shard_map/pallas_call | solution.py:60
  36.6 0.4 collective-permute-done.1.refs_2_
  37.0 0.0 copy-done
  37.0 0.6 shard_map.124
  37.7 5.7 %shard_map.126 = (f32[64,128]{1,0:T(8,128)S(1)}, f32[264,128]{1,0:T(8,128)S(1)}, f32[264,128]{1,0:T(8,128)S(1)}) custom-call(f32[512,128]{1,0:T(8,128)S(1)} %get-tuple-element.31.table.table_in, f32[1,64,128]{2,1,0:T(8,128)S(1)} %get-tuple-element.32.mean_t.mean_in, f32[64,128,128]{2,1,0:T(8,128)S(1)} %get-tuple-element.36.taste, ...), custom_call_target="tpu_custom_call" | custom-call | tf_op jit(solution)/shard_map/pallas_call | solution.py:60
  43.4 0.1 collective-permute-start.2
  43.5 1.3 %collective-permute-done.2.b = f32[264,128]{1,0:T(8,128)S(1)} collective-permute-done((f32[264,128]{1,0:T(8,128)S(1)}, f32[264,128]{1,0:T(8,128)S(1)}, u32[]{:S(2)}, u32[]{:S(2)}) %collective-permute-start.2) | collective-permute-done | bytes 135200 | tf_op jit(solution)/shard_map/ppermute | solution.py:520
  44.9 1.6 %collective-permute-start.3 = (f32[264,128]{1,0:T(8,128)S(1)}, f32[264,128]{1,0:T(8,128)S(1)}, u32[]{:S(2)}, u32[]{:S(2)}) collective-permute-start(f32[264,128]{1,0:T(8,128)S(1)} %shard_map.127.mine), channel_id=1, source_target_pairs={{0,2},{1,3},{2,0},{3,1},{4,6},{5,7},{6,4},{7,5},{8,10},{9,11},{10,... | collective-permute-start | bytes 405512 | tf_op jit(solution)/shard_map/ppermute | solution.py:520
  46.4 4.1 %collective-permute-done.3.other = f32[264,128]{1,0:T(8,128)S(1)} collective-permute-done((f32[264,128]{1,0:T(8,128)S(1)}, f32[264,128]{1,0:T(8,128)S(1)}, u32[]{:S(2)}, u32[]{:S(2)}) %collective-permute-start.3) | collective-permute-done | bytes 135200 | tf_op jit(solution)/shard_map/ppermute | solution.py:520
  50.6 0.2 shard_map.128.gap_mine
  50.7 0.0 collective-permute-start.4
  50.7 1.4 %collective-permute-done.4.gap_other = f32[264,128]{1,0:T(8,128)S(1)} collective-permute-done((f32[264,128]{1,0:T(8,128)S(1)}, f32[264,128]{1,0:T(8,128)S(1)}, u32[]{:S(2)}, u32[]{:S(2)}) %collective-permute-start.4) | collective-permute-done | bytes 135200 | tf_op jit(solution)/shard_map/ppermute | solution.py:520
  52.1 14.0 %all_to_all.45 = f32[8,72,128]{2,1,0:T(8,128)S(1)} all-to-all(f32[8,72,128]{2,1,0:T(8,128)S(1)} %bitcast.18), channel_id=1, replica_groups=mesh['mkt'=8,'grp'=4] {'mkt'}, dimensions={0} | all-to-all | bytes 589824 | tf_op jit(solution)/shard_map/all_to_all | solution.py:517
  66.1 5.8 %shard_map.130 = (f32[512,128]{1,0:T(8,128)S(1)}, f32[1,64,128]{2,1,0:T(8,128)S(1)}, f32[64,128]{1,0:T(8,128)S(1)}, f32[264,128]{1,0:T(8,128)S(1)}, f32[264,128]{1,0:T(8,128)S(1)}) custom-call(f32[576,128]{1,0:T(8,128)S(1)} %bitcast.17, f32[264,128]{1,0:T(8,128)S(1)} %shard_map.128.gap_mine, f32[264,128]{1,0:T(8,128)S(1)} %collective-permute-done.4.gap_other, ...), custom_call_target="tpu_custom_call" | custom-call | tf_op jit(solution)/shard_map/pallas_call | solution.py:60
  71.9 0.1 collective-permute-start.5
  71.9 1.3 %collective-permute-done.5.b = f32[264,128]{1,0:T(8,128)S(1)} collective-permute-done((f32[264,128]{1,0:T(8,128)S(1)}, f32[264,128]{1,0:T(8,128)S(1)}, u32[]{:S(2)}, u32[]{:S(2)}) %collective-permute-start.5) | collective-permute-done | bytes 135200 | tf_op jit(solution)/shard_map/ppermute | solution.py:520
  73.3 1.6 %collective-permute-start.6 = (f32[264,128]{1,0:T(8,128)S(1)}, f32[264,128]{1,0:T(8,128)S(1)}, u32[]{:S(2)}, u32[]{:S(2)}) collective-permute-start(f32[264,128]{1,0:T(8,128)S(1)} %shard_map.131.mine), channel_id=1, source_target_pairs={{0,2},{1,3},{2,0},{3,1},{4,6},{5,7},{6,4},{7,5},{8,10},{9,11},{10,... | collective-permute-start | bytes 405512 | tf_op jit(solution)/shard_map/ppermute | solution.py:520
  74.9 4.1 %collective-permute-done.6.other = f32[264,128]{1,0:T(8,128)S(1)} collective-permute-done((f32[264,128]{1,0:T(8,128)S(1)}, f32[264,128]{1,0:T(8,128)S(1)}, u32[]{:S(2)}, u32[]{:S(2)}) %collective-permute-start.6) | collective-permute-done | bytes 135200 | tf_op jit(solution)/shard_map/ppermute | solution.py:520
  79.0 0.2 shard_map.132.gap_mine
  79.2 0.0 collective-permute-start.7
  79.2 1.4 %collective-permute-done.7.gap_other = f32[264,128]{1,0:T(8,128)S(1)} collective-permute-done((f32[264,128]{1,0:T(8,128)S(1)}, f32[264,128]{1,0:T(8,128)S(1)}, u32[]{:S(2)}, u32[]{:S(2)}) %collective-permute-start.7) | collective-permute-done | bytes 135200 | tf_op jit(solution)/shard_map/ppermute | solution.py:520
  80.6 13.3 %all_to_all.46 = f32[8,72,128]{2,1,0:T(8,128)S(1)} all-to-all(f32[8,72,128]{2,1,0:T(8,128)S(1)} %bitcast.19), channel_id=1, replica_groups=mesh['mkt'=8,'grp'=4] {'mkt'}, dimensions={0} | all-to-all | bytes 589824 | tf_op jit(solution)/shard_map/all_to_all | solution.py:517
  93.9 5.8 %shard_map.134 = (f32[512,128]{1,0:T(8,128)S(1)}, f32[1,64,128]{2,1,0:T(8,128)S(1)}, f32[64,128]{1,0:T(8,128)S(1)}, f32[264,128]{1,0:T(8,128)S(1)}, f32[264,128]{1,0:T(8,128)S(1)}) custom-call(f32[576,128]{1,0:T(8,128)S(1)} %bitcast.16, f32[264,128]{1,0:T(8,128)S(1)} %shard_map.132.gap_mine, f32[264,128]{1,0:T(8,128)S(1)} %collective-permute-done.7.gap_other, ...), custom_call_target="tpu_custom_call" | custom-call | tf_op jit(solution)/shard_map/pallas_call | solution.py:60
  99.7 0.1 collective-permute-start.8
  99.7 1.3 %collective-permute-done.8.b = f32[264,128]{1,0:T(8,128)S(1)} collective-permute-done((f32[264,128]{1,0:T(8,128)S(1)}, f32[264,128]{1,0:T(8,128)S(1)}, u32[]{:S(2)}, u32[]{:S(2)}) %collective-permute-start.8) | collective-permute-done | bytes 135200 | tf_op jit(solution)/shard_map/ppermute | solution.py:520
  101.1 1.6 %collective-permute-start.9 = (f32[264,128]{1,0:T(8,128)S(1)}, f32[264,128]{1,0:T(8,128)S(1)}, u32[]{:S(2)}, u32[]{:S(2)}) collective-permute-start(f32[264,128]{1,0:T(8,128)S(1)} %shard_map.135.mine), channel_id=1, source_target_pairs={{0,2},{1,3},{2,0},{3,1},{4,6},{5,7},{6,4},{7,5},{8,10},{9,11},{10,... | collective-permute-start | bytes 405512 | tf_op jit(solution)/shard_map/ppermute | solution.py:520
  102.7 4.1 %collective-permute-done.9.other = f32[264,128]{1,0:T(8,128)S(1)} collective-permute-done((f32[264,128]{1,0:T(8,128)S(1)}, f32[264,128]{1,0:T(8,128)S(1)}, u32[]{:S(2)}, u32[]{:S(2)}) %collective-permute-start.9) | collective-permute-done | bytes 135200 | tf_op jit(solution)/shard_map/ppermute | solution.py:520
  106.8 0.2 shard_map.136.gap_mine
  107.0 0.0 collective-permute-start.10
  107.0 1.4 %collective-permute-done.10.gap_other = f32[264,128]{1,0:T(8,128)S(1)} collective-permute-done((f32[264,128]{1,0:T(8,128)S(1)}, f32[264,128]{1,0:T(8,128)S(1)}, u32[]{:S(2)}, u32[]{:S(2)}) %collective-permute-start.10) | collective-permute-done | bytes 135200 | tf_op jit(solution)/shard_map/ppermute | solution.py:520
  108.3 0.3 shard_map.137
  108.7 10.9 %all_to_all.47 = f32[8,48,128]{2,1,0:T(8,128)S(1)} all-to-all(f32[8,48,128]{2,1,0:T(8,128)S(1)} %bitcast.21), channel_id=1, replica_groups=mesh['mkt'=8,'grp'=4] {'mkt'}, dimensions={0} | all-to-all | bytes 393216 | tf_op jit(solution)/shard_map/all_to_all | solution.py:517
  119.6 0.7 shard_map.138
  (7 shorter events, 0.1 us)
Async XLA Ops:
  0.6 36.4 %copy-start = (f32[512,1024]{1,0:T(8,128)S(1)}, f32[512,1024]{1,0:T(8,128)}, u32[]{:S(2)}) copy-start(f32[512,1024]{1,0:T(8,128)} %share_h.3) | copy-start | bytes 6291460
  30.1 1.3 %collective-permute-start = (f32[128,128]{1,0:T(8,128)S(1)}, f32[128,128]{1,0:T(8,128)S(1)}, u32[]{:S(2)}, u32[]{:S(2)}) collective-permute-start(f32[128,128]{1,0:T(8,128)S(1)} %get-tuple-element.30.refs_0_), channel_id=1, source_target_pairs={{0,1},{1,0},{2,3},{3,2},{4,5},{5,4},{6,7},{7,6},{8,9},{9,8},{10,11... | collective-permute-start | bytes 196616 | tf_op jit(solution)/shard_map/ppermute | solution.py:520
  31.4 5.6 %collective-permute-start.1 = (f32[256,128]{1,0:T(8,128)S(1)}, f32[256,128]{1,0:T(8,128)S(1)}, u32[]{:S(2)}, u32[]{:S(2)}) collective-permute-start(f32[256,128]{1,0:T(8,128)S(1)} %pad_maximum_fusion), channel_id=1, source_target_pairs={{0,2},{1,3},{2,0},{3,1},{4,6},{5,7},{6,4},{7,5},{8,10},{9,11},{10,... | collective-permute-start | bytes 393224 | tf_op jit(solution)/shard_map/ppermute | solution.py:520
  43.4 1.4 %collective-permute-start.2 = (f32[264,128]{1,0:T(8,128)S(1)}, f32[264,128]{1,0:T(8,128)S(1)}, u32[]{:S(2)}, u32[]{:S(2)}) collective-permute-start(f32[264,128]{1,0:T(8,128)S(1)} %get-tuple-element.41), channel_id=1, source_target_pairs={{0,1},{1,0},{2,3},{3,2},{4,5},{5,4},{6,7},{7,6},{8,9},{9,8},{10,11... | collective-permute-start | bytes 405512 | tf_op jit(solution)/shard_map/ppermute | solution.py:520
  44.9 5.7 %collective-permute-start.3 = (f32[264,128]{1,0:T(8,128)S(1)}, f32[264,128]{1,0:T(8,128)S(1)}, u32[]{:S(2)}, u32[]{:S(2)}) collective-permute-start(f32[264,128]{1,0:T(8,128)S(1)} %shard_map.127.mine), channel_id=1, source_target_pairs={{0,2},{1,3},{2,0},{3,1},{4,6},{5,7},{6,4},{7,5},{8,10},{9,11},{10,... | collective-permute-start | bytes 405512 | tf_op jit(solution)/shard_map/ppermute | solution.py:520
  50.7 1.4 %collective-permute-start.4 = (f32[264,128]{1,0:T(8,128)S(1)}, f32[264,128]{1,0:T(8,128)S(1)}, u32[]{:S(2)}, u32[]{:S(2)}) collective-permute-start(f32[264,128]{1,0:T(8,128)S(1)} %shard_map.128.gap_mine), channel_id=1, source_target_pairs={{0,1},{1,0},{2,3},{3,2},{4,5},{5,4},{6,7},{7,6},{8,9},{9,8},{10,11... | collective-permute-start | bytes 405512 | tf_op jit(solution)/shard_map/ppermute | solution.py:520
  71.9 1.4 %collective-permute-start.5 = (f32[264,128]{1,0:T(8,128)S(1)}, f32[264,128]{1,0:T(8,128)S(1)}, u32[]{:S(2)}, u32[]{:S(2)}) collective-permute-start(f32[264,128]{1,0:T(8,128)S(1)} %get-tuple-element.46), channel_id=1, source_target_pairs={{0,1},{1,0},{2,3},{3,2},{4,5},{5,4},{6,7},{7,6},{8,9},{9,8},{10,11... | collective-permute-start | bytes 405512 | tf_op jit(solution)/shard_map/ppermute | solution.py:520
  73.3 5.7 %collective-permute-start.6 = (f32[264,128]{1,0:T(8,128)S(1)}, f32[264,128]{1,0:T(8,128)S(1)}, u32[]{:S(2)}, u32[]{:S(2)}) collective-permute-start(f32[264,128]{1,0:T(8,128)S(1)} %shard_map.131.mine), channel_id=1, source_target_pairs={{0,2},{1,3},{2,0},{3,1},{4,6},{5,7},{6,4},{7,5},{8,10},{9,11},{10,... | collective-permute-start | bytes 405512 | tf_op jit(solution)/shard_map/ppermute | solution.py:520
  79.2 1.4 %collective-permute-start.7 = (f32[264,128]{1,0:T(8,128)S(1)}, f32[264,128]{1,0:T(8,128)S(1)}, u32[]{:S(2)}, u32[]{:S(2)}) collective-permute-start(f32[264,128]{1,0:T(8,128)S(1)} %shard_map.132.gap_mine), channel_id=1, source_target_pairs={{0,1},{1,0},{2,3},{3,2},{4,5},{5,4},{6,7},{7,6},{8,9},{9,8},{10,11... | collective-permute-start | bytes 405512 | tf_op jit(solution)/shard_map/ppermute | solution.py:520
  99.7 1.4 %collective-permute-start.8 = (f32[264,128]{1,0:T(8,128)S(1)}, f32[264,128]{1,0:T(8,128)S(1)}, u32[]{:S(2)}, u32[]{:S(2)}) collective-permute-start(f32[264,128]{1,0:T(8,128)S(1)} %get-tuple-element.51), channel_id=1, source_target_pairs={{0,1},{1,0},{2,3},{3,2},{4,5},{5,4},{6,7},{7,6},{8,9},{9,8},{10,11... | collective-permute-start | bytes 405512 | tf_op jit(solution)/shard_map/ppermute | solution.py:520
  101.1 5.7 %collective-permute-start.9 = (f32[264,128]{1,0:T(8,128)S(1)}, f32[264,128]{1,0:T(8,128)S(1)}, u32[]{:S(2)}, u32[]{:S(2)}) collective-permute-start(f32[264,128]{1,0:T(8,128)S(1)} %shard_map.135.mine), channel_id=1, source_target_pairs={{0,2},{1,3},{2,0},{3,1},{4,6},{5,7},{6,4},{7,5},{8,10},{9,11},{10,... | collective-permute-start | bytes 405512 | tf_op jit(solution)/shard_map/ppermute | solution.py:520
  107.0 1.4 %collective-permute-start.10 = (f32[264,128]{1,0:T(8,128)S(1)}, f32[264,128]{1,0:T(8,128)S(1)}, u32[]{:S(2)}, u32[]{:S(2)}) collective-permute-start(f32[264,128]{1,0:T(8,128)S(1)} %shard_map.136.gap_mine), channel_id=1, source_target_pairs={{0,1},{1,0},{2,3},{3,2},{4,5},{5,4},{6,7},{7,6},{8,9},{9,8},{10,11... | collective-permute-start | bytes 405512 | tf_op jit(solution)/shard_map/ppermute | solution.py:520

commit v4 on v3

--- a/solution.py
+++ b/solution.py
@@ -46,7 +46,8 @@
         self.s_shift = self.s_mean + self.i8
         self.S = -(-(self.s_shift + self.i8) // 8) * 8
         self.PB = self.hh * products
-        self.S2 = self.PB + 8
+        self.PH = self.PB // 2
+        self.S2 = self.PH + 8
         self.S3 = -(-(self.i8 + 2 * self.oi + 1) // 8) * 8
         self.vmem = 16 if firms * products * self.ML <= 2**22 else 58
 
@@ -303,7 +304,7 @@
     return total
 
 
-def step_body(p, table, mean_of, taste, hot, mass_t, mass_row, pred, keep, give, tab, expu, parts, acc):
+def step_body(p, table, mean_of, taste, hot, mass_t, mass_row, pred, parts, give, tab, expu, acc):
     turned = table[...].T
     for q, piece in enumerate(split2(turned)):
         for t in range(p.F // LANES):
@@ -327,79 +328,128 @@
 
     total = lax.fori_loop(0, p.NS, gather, jnp.zeros((p.RL, p.ML), F32), unroll=min(16, p.NS))
     scale = mass_t[...] / (1.0 + total)
-    acc[...] = jnp.zeros_like(acc)
     if p.NR > 2 * p.RL:
         parts[...] = jnp.zeros_like(parts)
-    per = p.per
-
-    def scatter(n, _):
+
+    def fill(n):
+        for v in range(p.u):
+            j = n * p.u + v
+            x = expu[j] * scale
+            hi, lo = split2(x)
+            for b in range(p.hh):
+                at = slice(b * LANES, (b + 1) * LANES)
+                parts[n, v * p.hh + b, 0 : p.RL, :] = hi[:, at]
+                parts[n, v * p.hh + b, p.RL : 2 * p.RL, :] = lo[:, at]
+            row = jnp.sum(x, axis=0, keepdims=True)
+            for b in range(p.hh):
+                pred[pl.ds(b * p.J + j, 1), :] = row[:, b * LANES : (b + 1) * LANES]
+
+    give[0 : p.HR, :] = totals_of(p, parts, hot, acc, 1, fill)
+    give[p.HR :, :] = mass_row[...]
+
+
+def totals_of(p, parts, hot, acc, other, fill):
+    start = ((lax.axis_index("grp") & 1) ^ other) * p.HR
+    acc[...] = jnp.zeros_like(acc)
+
+    def body(n, _):
         value = None
-        for s in range(per):
+        for s in range(p.per):
+            at = n * p.per + s
+            fill(at)
+            left = []
             for v in range(p.u):
-                j = (n * per + s) * p.u + v
-                x = expu[j] * scale
-                hi, lo = split2(x)
                 for b in range(p.hh):
-                    at = slice(b * LANES, (b + 1) * LANES)
-                    parts[s, v * p.hh + b, 0 : p.RL, :] = hi[:, at]
-                    parts[s, v * p.hh + b, p.RL : 2 * p.RL, :] = lo[:, at]
-                row = jnp.sum(x, axis=0, keepdims=True)
-                for b in range(p.hh):
-                    pred[pl.ds(b * p.J + j, 1), :] = row[:, b * LANES : (b + 1) * LANES]
-            right = jnp.concatenate([parts[s, t] for t in range(p.u * p.hh)], axis=1)
-            term = dot_t(hot_of(n * per + s), right)
+                    rows = [pl.ds(pl.multiple_of(start + fh * p.FP, 8), p.HR) for fh in range(p.hh)]
+                    tall = [hot[at * p.u + v, b, r, :] for r in rows]
+                    left.append(tall[0] if p.hh == 1 else jnp.concatenate(tall, axis=0))
+            right = jnp.concatenate([parts[at, t] for t in range(p.u * p.hh)], axis=1)
+            term = dot_t(jnp.concatenate(left, axis=1), right)
             value = term if value is None else value + term
         acc[...] += value
         return 0
 
-    lax.fori_loop(0, p.NS // per, scatter, 0)
+    lax.fori_loop(0, p.NS // p.per, body, 0)
     full = acc[:, 0:LANES]
     for t in range(1, p.NR // LANES):
         full = full + acc[:, t * LANES : (t + 1) * LANES]
-    if p.hh == 1:
-        acc[:, 0:LANES] = full
-    else:
-        pack_table(p, fold(p, full), acc.at[0 : p.FP, 0:LANES])
-    mine = (lax.axis_index("grp") & 1) * p.HR
-    keep[0 : p.HR, :] = acc[pl.ds(pl.multiple_of(mine, 8), p.HR), 0:LANES]
-    give[0 : p.HR, :] = acc[pl.ds(pl.multiple_of(p.HR - mine, 8), p.HR), 0:LANES]
+    full = fold(p, full)
+    value = full[0 : p.HR, :]
+    for b in range(1, p.hh):
+        value = jnp.where(block_mask(p.RL, p.HR, b), full[b * p.HR : (b + 1) * p.HR, :], value)
+    return value
+
+
+def rest_kernel(p, parts, hot, mass_row, keep, acc):
+    keep[0 : p.HR, :] = totals_of(p, parts, hot, acc, 0, lambda n: None)
     keep[p.HR :, :] = mass_row[...]
-    give[p.HR :, :] = mass_row[...]
 
 
 def step_scratch_of(p):
     return (
         pltpu.VMEM((p.F // LANES, 2 * p.RL, LANES), BF),
         pltpu.VMEM((p.J, p.RL, p.ML), F32),
-        pltpu.VMEM((p.per, p.u * p.hh, p.NR, LANES), BF),
-        pltpu.VMEM((p.F, p.NR), F32),
-    )
-
-
-def first_kernel(p, table, mean_t, taste, hot, mass_t, mass_row, pred, keep, give, *scratch):
-    step_body(p, table, mean_t, taste, hot, mass_t, mass_row, pred, keep, give, *scratch)
-
-
-def next_kernel(
-    p, recv, gap_mine, gap_other, table_in, mean_in, shift_t, taste, hot, mass_t, mass_row,
-    table, mean_t, pred, keep, give, *scratch
+        pltpu.VMEM((p.F // 2, p.NR), F32),
+    )
+
+
+def split_predicted(p, pred, pred_keep, pred_give):
+    mine = (lax.axis_index("mkt") & 1) * p.PH
+    pred_keep[...] = pred[pl.ds(pl.multiple_of(mine, 8), p.PH), :]
+    pred_give[...] = pred[pl.ds(pl.multiple_of(p.PH - mine, 8), p.PH), :]
+
+
+def first_kernel(
+    p, table, mean_t, taste, hot, mass_t, mass_row, pred_keep, pred_give, parts, give, pred, *scratch
 ):
-    clip = clip_of(p, sum_chunks(p, recv, p.S2, p.PB, 1))
+    step_body(p, table, mean_t, taste, hot, mass_t, mass_row, pred, parts, give, *scratch)
+    split_predicted(p, pred, pred_keep, pred_give)
+
+
+def update(p, recv, gap_mine, gap_other, table_in, mean_in, shift_t, table, mean_t):
+    clip = clip_of(p, sum_chunks(p, recv, p.S2, p.PH, 1))
     mine = (lax.axis_index("grp") & 1) * p.HR
     for ref, start in ((gap_mine, mine), (gap_other, p.HR - mine)):
         at = pl.ds(pl.multiple_of(start, 8), p.HR)
         table[at, :] = table_in[at, :] + clip * ref[0 : p.HR, :]
+    halves = []
+    for side in range(2):
+        total = recv[side * p.S2 : side * p.S2 + p.PH, :]
+        for c in range(side + 2, p.C, 2):
+            total = total + recv[c * p.S2 : c * p.S2 + p.PH, :]
+        halves.append(total)
+    total = jnp.log(jnp.concatenate(halves, axis=0))
     for b in range(p.hh):
-        total = sum_chunks(p, recv, p.S2, b * p.J, p.J)
-        mean_t[b] = mean_in[b] + shift_t[b] - jnp.log(total)
-    step_body(p, table, mean_t, taste, hot, mass_t, mass_row, pred, keep, give, *scratch)
-
-
-def add_kernel(p, a, b, out):
-    out[...] = a[...] + b[...]
-
-
-def gap_kernel(p, mine, other, share, gap):
+        mean_t[b] = mean_in[b] + shift_t[b] - total[b * p.J : (b + 1) * p.J, :]
+
+
+def next_kernel(
+    p, recv, gap_mine, gap_other, table_in, mean_in, shift_t, taste, hot, mass_t, mass_row,
+    table, mean_t, pred_keep, pred_give, parts, give, pred, *scratch
+):
+    update(p, recv, gap_mine, gap_other, table_in, mean_in, shift_t, table, mean_t)
+    step_body(p, table, mean_t, taste, hot, mass_t, mass_row, pred, parts, give, *scratch)
+    split_predicted(p, pred, pred_keep, pred_give)
+
+
+def last_kernel(
+    p, recv, gap_mine, gap_other, table_in, mean_in, shift_t, taste, hot, mass_t, mass_row,
+    table, mean_t, pred, parts, give, *scratch
+):
+    update(p, recv, gap_mine, gap_other, table_in, mean_in, shift_t, table, mean_t)
+    step_body(p, table, mean_t, taste, hot, mass_t, mass_row, pred, parts, give, *scratch)
+
+
+def add_kernel(p, a, b, *refs):
+    refs[len(refs) // 2][...] = a[...] + b[...]
+    for n in range(len(refs) // 2):
+        refs[len(refs) // 2 + 1 + n][...] = refs[n][...]
+
+
+def gap_kernel(p, mine, other, share, *refs):
+    gap = refs[-1] if len(refs) == 1 else refs[2]
+    if len(refs) > 1:
+        refs[3][...] = refs[0][...] + refs[1][...]
     total = mine[...] + other[...]
     at = pl.ds(pl.multiple_of((lax.axis_index("grp") & 1) * p.HR, 8), p.HR)
     value = jnp.log(share[at, :]) - jnp.log(total[0 : p.HR, :] / total[p.HR : p.HR + 1, :])
@@ -412,8 +462,8 @@
     squares = gap_mine[p.HR :, :] + gap_other[p.HR :, :]
     value = pred[...]
     for c in range(p.C):
-        send[c * p.S2 : c * p.S2 + p.PB, :] = value
-        send[c * p.S2 + p.PB : (c + 1) * p.S2, :] = squares
+        send[c * p.S2 : c * p.S2 + p.PH, :] = value
+        send[c * p.S2 + p.PH : (c + 1) * p.S2, :] = squares
 
 
 def final_kernel(p, gap_mine, gap_other, table, columns, pred, mean_t, shift_t, send, own, gap, nat, means):
@@ -574,11 +624,7 @@
         (exchange(send),),
         scratch=(pltpu.VMEM((max(LANES, p.PR), LANES), F32),),
     )
-    rows = [loy]
-    bit = 1
-    while bit < p.Q:
-        rows.append(swap(rows[0] if bit == 1 else jnp.concatenate(rows, axis=0), bit))
-        bit *= 2
+    rows = [loy] + [swap(loy, bits) for bits in range(1, p.Q)]
     taste, hot = call(
         p,
         taste_kernel,
@@ -594,35 +640,59 @@
         scratch=(pltpu.VMEM((p.F, LANES), F32), pltpu.SemaphoreType.DMA(())),
     )
     half = sds((p.HR + 8, LANES))
-    step_outs = (sds((p.PB, LANES)), half, half)
+    tables = (sds((p.FP, LANES)), tiles)
+    half_pred = sds((p.PH, LANES))
+    all_parts = sds((p.NS, p.u * p.hh, p.NR, LANES), BF)
     step_scratch = step_scratch_of(p)
+    whole_pred = (pltpu.VMEM((p.PB, LANES), F32),)
     fixed = (taste, hot, mass_t, mass_row)
     for step in range(ITERS):
+        last = step == ITERS - 1
         if step == 0:
-            pred, keep, give = call(
+            pred, pred_give, parts, give = call(
                 p,
                 first_kernel,
-                step_outs,
+                (half_pred, half_pred, all_parts, half),
                 (table, mean_t, *fixed),
-                scratch=step_scratch,
+                scratch=whole_pred + step_scratch,
+            )
+        elif not last:
+            table, mean_t, pred, pred_give, parts, give = call(
+                p,
+                next_kernel,
+                tables + (half_pred, half_pred, all_parts, half),
+                (recv, gap_mine, gap_other, table, mean_t, shift_t, *fixed),
+                scratch=whole_pred + step_scratch,
             )
         else:
-            table, mean_t, pred, keep, give = call(
+            table, mean_t, pred, parts, give = call(
                 p,
-                next_kernel,
-                (sds((p.FP, LANES)), tiles) + step_outs,
+                last_kernel,
+                tables + (sds((p.PB, LANES)), all_parts, half),
                 (recv, gap_mine, gap_other, table, mean_t, shift_t, *fixed),
                 scratch=step_scratch,
             )
-        mine = call(p, add_kernel, half, (keep, swap(give, 1)))
+        given = swap(give, 1)
+        keep = call(p, rest_kernel, half, (parts, hot, mass_row), scratch=step_scratch[-1:])
+        if last:
+            (mine,) = call(p, add_kernel, (half,), (keep, given))
+        else:
+            mine, pred_give = call(p, add_kernel, (half, half_pred), (keep, given, pred_give))
+            pred_other = lax.ppermute(pred_give, "mkt", [(c, c ^ 1) for c in range(p.C)])
         bit = 2
         while 2 * bit < p.Q:
-            mine = call(p, add_kernel, half, (mine, swap(mine, bit)))
+            (mine,) = call(p, add_kernel, (half,), (mine, swap(mine, bit)))
             bit *= 2
-        gap_mine = call(p, gap_kernel, half, (mine, swap(mine, bit), share))
+        sums = (mine, swap(mine, bit), share)
+        if last:
+            gap_mine = call(p, gap_kernel, half, sums)
+        else:
+            gap_mine, pred = call(p, gap_kernel, (half, half_pred), sums + (pred, pred_other))
         gap_other = swap(gap_mine, 1)
-        if step < ITERS - 1:
-            recv = exchange(call(p, send_kernel, sds((p.C * p.S2, LANES)), (gap_mine, gap_other, pred)))
+        if not last:
+            recv = exchange(
+                call(p, send_kernel, sds((p.C * p.S2, LANES)), (gap_mine, gap_other, pred))
+            )
     send, own = call(
         p,
         final_kernel,

time: 121 us -> 112 us (0.926)
  blocking collectives: 64.3 us -> 58.7 us
  waiting for transfers between devices: 22.1 us -> 16.8 us
  Pallas kernels: 25.6 us -> 27 us
  starting transfers between devices: 6.63 us -> 7.87 us
    ppermute x11 -> x12, waiting for transfers between devices: 22.1 us -> 11 us  [swap(): return lax.ppermute(x, 'grp', [(q, q ^ bit) for q in range(p.Q)])]
    ppermute x0 -> x2, waiting for transfers between devices: none -> 5.79 us  [local(): lax.ppermute(pred_give, 'mkt', [(c, c ^ 1) for c in range(p.C)])]
    all_to_all x4, blocking collectives: 64.3 us -> 58.7 us  [exchange(): return lax.all_to_all(x, 'mkt', split_axis=0, concat_axis=0, tiled=True)]
    ppermute x0 -> x2, starting transfers between devices: none -> 1.69 us  [local(): lax.ppermute(pred_give, 'mkt', [(c, c ^ 1) for c in range(p.C)])]
    pallas_call x17 -> x20, Pallas kernels: 25.6 us -> 27 us  [call(): pl.pallas_call(functools.partial(kernel, p), out_shape=outs, in_specs=spe...]
    ppermute x11 -> x12, starting transfers between devices: 6.63 us -> 6.17 us  [swap(): return lax.ppermute(x, 'grp', [(q, q ^ bit) for q in range(p.Q)])]
  transfers between devices with their start and end apart: 11 -> 14, of which waited for: 11 -> 9; matrix products, arithmetic and copies ran while one was open for 1% -> 1% of each run, Pallas kernels for 2% -> 7%
where the time goes in v4:
time: 112 us
  blocking collectives  58.7 us (52%)
  Pallas kernels  27 us (24%)
  waiting for transfers between devices  16.8 us (15%)
  starting transfers between devices  7.87 us (7%)
    all_to_all x4, blocking collectives, exchange(): return lax.all_to_all(x, 'mkt', split_axis=0, concat_axis=0, tiled=True)  58.7 us
    pallas_call x20, Pallas kernels, call(): pl.pallas_call(functools.partial(kernel, p), out_shape=outs, in_specs=spe...  27 us
    ppermute x12, waiting for transfers between devices, swap(): return lax.ppermute(x, 'grp', [(q, q ^ bit) for q in range(p.Q)])  11 us
    ppermute x12, starting transfers between devices, swap(): return lax.ppermute(x, 'grp', [(q, q ^ bit) for q in range(p.Q)])  6.17 us
    ppermute x2, waiting for transfers between devices, local(): lax.ppermute(pred_give, 'mkt', [(c, c ^ 1) for c in range(p.C)])  5.79 us
  transfers between devices with their start and end apart: 14, of which 9 were waited for; matrix products, arithmetic and copies ran while one was open for 1% of the time, Pallas kernels for 7%

profile of v4, /device:TPU:0, one launch (start us, length us, event | category | flops | bytes accessed | tf_op | source)
XLA Modules:
  0.0 112.0 jit_solution(17482554879830172187)
XLA Ops:
  0.6 3.0 %shard_map.122 = f32[1408,128]{1,0:T(8,128)} custom-call(f32[5]{0:T(128)} %scale.1, f32[16]{0:T(128)} %size.1, f32[5,16,1024]{2,1,0:T(8,128)} %bitcast.23, f32[16,1024]{1,0:T(8,128)} %weight_h.1, f32[16,1024]{1,0:T(8,128)} %loyalty_h.1, f32[5,16,64]{2,1,0:T(8,128)} %bitcast.25, s32[16,64]{1,0:T(8,128)} %firms_h.1, f32[16,64]{1,0:T(8,128)} %mean_h.1, ...), custom_call_target="tpu_custom_call" | custom-call | tf_op jit(solution)/shard_map/pallas_call | solution.py:61
  3.6 26.1 %all_to_all.44 = f32[8,176,128]{2,1,0:T(8,128)S(1)} all-to-all(f32[8,176,128]{2,1,0:T(8,128)} %bitcast.22), channel_id=1, replica_groups=mesh['mkt'=8,'grp'=4] {'mkt'}, dimensions={0} | all-to-all | bytes 1441792 | tf_op jit(solution)/shard_map/all_to_all | solution.py:567
  29.7 0.3 shard_map.123
  30.1 0.1 collective-permute-start.2
  30.1 1.6 %collective-permute-start.1 = (f32[128,128]{1,0:T(8,128)S(1)}, f32[128,128]{1,0:T(8,128)S(1)}, u32[]{:S(2)}, u32[]{:S(2)}) collective-permute-start(f32[128,128]{1,0:T(8,128)S(1)} %get-tuple-element.40.refs_0_), channel_id=1, source_target_pairs={{0,2},{1,3},{2,0},{3,1},{4,6},{5,7},{6,4},{7,5},{8,10},{9,11},{10,... | collective-permute-start | bytes 196616 | tf_op jit(solution)/shard_map/ppermute | solution.py:570
  31.7 0.3 collective-permute-start
  32.0 0.8 reshape.20
  32.8 0.1 reshape.21.order
  32.8 2.8 %shard_map.125 = (f32[64,128,128]{2,1,0:T(8,128)S(1)}, bf16[64,1,512,128]{3,2,1,0:T(8,128)(2,1)S(1)}) custom-call(f32[5,128,128]{2,1,0:T(8,128)S(1)} %get-tuple-element.43.draws_t, f32[5,1,64,128]{3,2,1,0:T(8,128)S(1)} %get-tuple-element.44.traits_t, f32[1,64,128]{2,1,0:T(8,128)S(1)} %get-tuple-element.45.firms_t), custom_call_target="tpu_custom_call" | custom-call | tf_op jit(solution)/shard_map/pallas_call | solution.py:61
  35.6 0.0 collective-permute-done.2.refs_3_
  35.6 0.3 collective-permute-done.1.refs_2_
  35.9 0.0 collective-permute-done.refs_1_
  35.9 0.6 shard_map.124
  36.6 4.8 %shard_map.126 = (f32[32,128]{1,0:T(8,128)S(1)}, f32[32,128]{1,0:T(8,128)S(1)}, bf16[32,2,256,128]{3,2,1,0:T(8,128)(2,1)S(1)}, f32[264,128]{1,0:T(8,128)S(1)}) custom-call(f32[512,128]{1,0:T(8,128)S(1)} %get-tuple-element.41.table.table_in, f32[1,64,128]{2,1,0:T(8,128)S(1)} %get-tuple-element.42.mean_t.mean_in, f32[64,128,128]{2,1,0:T(8,128)S(1)} %get-tuple-element.46.taste, ...), custom_call_target="tpu_custom_call" | custom-call | tf_op jit(solution)/shard_map/pallas_call | solution.py:61
  41.3 0.1 collective-permute-start.3
  41.4 1.5 %shard_map.127.a = f32[264,128]{1,0:T(8,128)S(1)} custom-call(bf16[32,2,256,128]{3,2,1,0:T(8,128)(2,1)S(1)} %get-tuple-element.50.parts, bf16[64,1,512,128]{3,2,1,0:T(8,128)(2,1)S(1)} %get-tuple-element.47.hot, f32[8,128]{1,0:T(8,128)S(1)} %get-tuple-element.49.mass_row), custom_call_target="tpu_custom_call" | custom-call | tf_op jit(solution)/shard_map/pallas_call | solution.py:61
  43.0 0.0 collective-permute-done.3.b
  43.0 1.3 %collective-permute-start.4 = (f32[264,128]{1,0:T(8,128)S(1)}, f32[264,128]{1,0:T(8,128)S(1)}, u32[]{:S(2)}, u32[]{:S(2)}) collective-permute-start(f32[264,128]{1,0:T(8,128)S(1)} %get-tuple-element.53.mine), channel_id=1, source_target_pairs={{0,2},{1,3},{2,0},{3,1},{4,6},{5,7},{6,4},{7,5},{8,10},{9,11},{10,... | collective-permute-start | bytes 405512 | tf_op jit(solution)/shard_map/ppermute | solution.py:570
  44.3 1.3 %collective-permute-start.5 = (f32[32,128]{1,0:T(8,128)S(1)}, f32[32,128]{1,0:T(8,128)S(1)}, u32[]{:S(2)}, u32[]{:S(2)}) collective-permute-start(f32[32,128]{1,0:T(8,128)S(1)} %get-tuple-element.56), channel_id=1, source_target_pairs={{0,4},{4,0},{8,12},{12,8},{16,20},{20,16},{24,28},{28,24},{1,5},{5... | collective-permute-start | bytes 49160 | tf_op jit(solution)/shard_map/ppermute | solution.py:681
  45.7 2.4 %collective-permute-done.5.refs_1_ = f32[32,128]{1,0:T(8,128)S(1)} collective-permute-done((f32[32,128]{1,0:T(8,128)S(1)}, f32[32,128]{1,0:T(8,128)S(1)}, u32[]{:S(2)}, u32[]{:S(2)}) %collective-permute-start.5) | collective-permute-done | bytes 16416 | tf_op jit(solution)/shard_map/ppermute | solution.py:681
  48.1 1.0 collective-permute-done.4.other
  49.0 0.2 shard_map.129
  49.2 0.0 collective-permute-start.6
  49.2 1.4 %collective-permute-done.6.gap_other = f32[264,128]{1,0:T(8,128)S(1)} collective-permute-done((f32[264,128]{1,0:T(8,128)S(1)}, f32[264,128]{1,0:T(8,128)S(1)}, u32[]{:S(2)}, u32[]{:S(2)}) %collective-permute-start.6) | collective-permute-done | bytes 135200 | tf_op jit(solution)/shard_map/ppermute | solution.py:570
  50.6 11.1 %all_to_all.45 = f32[8,40,128]{2,1,0:T(8,128)S(1)} all-to-all(f32[8,40,128]{2,1,0:T(8,128)S(1)} %bitcast.17), channel_id=1, replica_groups=mesh['mkt'=8,'grp'=4] {'mkt'}, dimensions={0} | all-to-all | bytes 327680 | tf_op jit(solution)/shard_map/all_to_all | solution.py:567
  61.7 4.7 %shard_map.131 = (f32[512,128]{1,0:T(8,128)S(1)}, f32[1,64,128]{2,1,0:T(8,128)S(1)}, f32[32,128]{1,0:T(8,128)S(1)}, f32[32,128]{1,0:T(8,128)S(1)}, bf16[32,2,256...) custom-call(f32[320,128]{1,0:T(8,128)S(1)} %bitcast.20, f32[264,128]{1,0:T(8,128)S(1)} %get-tuple-element.57.gap_mine, ...), custom_call_target="tpu_custom_call" | custom-call | tf_op jit(solution)/shard_map/pallas_call | solution.py:61
  66.3 0.1 collective-permute-start.7
  66.4 1.5 %shard_map.132.a = f32[264,128]{1,0:T(8,128)S(1)} custom-call(bf16[32,2,256,128]{3,2,1,0:T(8,128)(2,1)S(1)} %get-tuple-element.60.parts, bf16[64,1,512,128]{3,2,1,0:T(8,128)(2,1)S(1)} %get-tuple-element.47.hot, f32[8,128]{1,0:T(8,128)S(1)} %get-tuple-element.49.mass_row), custom_call_target="tpu_custom_call" | custom-call | tf_op jit(solution)/shard_map/pallas_call | solution.py:61
  67.9 0.0 collective-permute-done.7.b
  68.0 1.3 %collective-permute-start.8 = (f32[264,128]{1,0:T(8,128)S(1)}, f32[264,128]{1,0:T(8,128)S(1)}, u32[]{:S(2)}, u32[]{:S(2)}) collective-permute-start(f32[264,128]{1,0:T(8,128)S(1)} %get-tuple-element.63.mine), channel_id=1, source_target_pairs={{0,2},{1,3},{2,0},{3,1},{4,6},{5,7},{6,4},{7,5},{8,10},{9,11},{10,... | collective-permute-start | bytes 405512 | tf_op jit(solution)/shard_map/ppermute | solution.py:570
  69.3 0.3 collective-permute-start.9
  69.6 3.4 %collective-permute-done.9.refs_1_ = f32[32,128]{1,0:T(8,128)S(1)} collective-permute-done((f32[32,128]{1,0:T(8,128)S(1)}, f32[32,128]{1,0:T(8,128)S(1)}, u32[]{:S(2)}, u32[]{:S(2)}) %collective-permute-start.9) | collective-permute-done | bytes 16416 | tf_op jit(solution)/shard_map/ppermute | solution.py:681
  73.0 1.0 collective-permute-done.8.other
  74.0 0.2 shard_map.134
  74.2 0.0 collective-permute-start.10
  74.2 1.4 %collective-permute-done.10.gap_other = f32[264,128]{1,0:T(8,128)S(1)} collective-permute-done((f32[264,128]{1,0:T(8,128)S(1)}, f32[264,128]{1,0:T(8,128)S(1)}, u32[]{:S(2)}, u32[]{:S(2)}) %collective-permute-start.10) | collective-permute-done | bytes 135200 | tf_op jit(solution)/shard_map/ppermute | solution.py:570
  75.5 10.5 %all_to_all.46 = f32[8,40,128]{2,1,0:T(8,128)S(1)} all-to-all(f32[8,40,128]{2,1,0:T(8,128)S(1)} %bitcast.18), channel_id=1, replica_groups=mesh['mkt'=8,'grp'=4] {'mkt'}, dimensions={0} | all-to-all | bytes 327680 | tf_op jit(solution)/shard_map/all_to_all | solution.py:567
  86.1 4.7 %shard_map.136 = (f32[512,128]{1,0:T(8,128)S(1)}, f32[1,64,128]{2,1,0:T(8,128)S(1)}, f32[64,128]{1,0:T(8,128)S(1)}, bf16[32,2,256,128]{3,2,1,0:T(8,128)(2,1)S(1)}, f32[264,128]{1,0:T(8,128)S(1)}) custom-call(f32[320,128]{1,0:T(8,128)S(1)} %bitcast.19, f32[264,128]{1,0:T(8,128)S(1)} %get-tuple-element.66.gap_mine, ...), custom_call_target="tpu_custom_call" | custom-call | tf_op jit(solution)/shard_map/pallas_call | solution.py:61
  90.7 0.1 collective-permute-start.11
  90.8 1.5 %shard_map.137.a = f32[264,128]{1,0:T(8,128)S(1)} custom-call(bf16[32,2,256,128]{3,2,1,0:T(8,128)(2,1)S(1)} %get-tuple-element.70.parts, bf16[64,1,512,128]{3,2,1,0:T(8,128)(2,1)S(1)} %get-tuple-element.47.hot, f32[8,128]{1,0:T(8,128)S(1)} %get-tuple-element.49.mass_row), custom_call_target="tpu_custom_call" | custom-call | tf_op jit(solution)/shard_map/pallas_call | solution.py:61
  92.3 0.0 collective-permute-done.11.b
  92.4 1.3 %collective-permute-start.12 = (f32[264,128]{1,0:T(8,128)S(1)}, f32[264,128]{1,0:T(8,128)S(1)}, u32[]{:S(2)}, u32[]{:S(2)}) collective-permute-start(f32[264,128]{1,0:T(8,128)S(1)} %shard_map.138.mine), channel_id=1, source_target_pairs={{0,2},{1,3},{2,0},{3,1},{4,6},{5,7},{6,4},{7,5},{8,10},{9,11},{10,... | collective-permute-start | bytes 405512 | tf_op jit(solution)/shard_map/ppermute | solution.py:570
  93.7 4.7 %collective-permute-done.12.other = f32[264,128]{1,0:T(8,128)S(1)} collective-permute-done((f32[264,128]{1,0:T(8,128)S(1)}, f32[264,128]{1,0:T(8,128)S(1)}, u32[]{:S(2)}, u32[]{:S(2)}) %collective-permute-start.12) | collective-permute-done | bytes 135200 | tf_op jit(solution)/shard_map/ppermute | solution.py:570
  98.4 0.2 shard_map.139.gap_mine
  98.6 1.4 %collective-permute-done.13.gap_other = f32[264,128]{1,0:T(8,128)S(1)} collective-permute-done((f32[264,128]{1,0:T(8,128)S(1)}, f32[264,128]{1,0:T(8,128)S(1)}, u32[]{:S(2)}, u32[]{:S(2)}) %collective-permute-start.13) | collective-permute-done | bytes 135200 | tf_op jit(solution)/shard_map/ppermute | solution.py:570
  99.9 0.4 shard_map.140
  100.3 11.0 %all_to_all.47 = f32[8,48,128]{2,1,0:T(8,128)S(1)} all-to-all(f32[8,48,128]{2,1,0:T(8,128)S(1)} %bitcast.21), channel_id=1, replica_groups=mesh['mkt'=8,'grp'=4] {'mkt'}, dimensions={0} | all-to-all | bytes 393216 | tf_op jit(solution)/shard_map/all_to_all | solution.py:567
  111.3 0.7 shard_map.141
  (9 shorter events, 0.1 us)
Async XLA Ops:
  0.6 35.3 %copy-start = (f32[512,1024]{1,0:T(8,128)S(1)}, f32[512,1024]{1,0:T(8,128)}, u32[]{:S(2)}) copy-start(f32[512,1024]{1,0:T(8,128)} %share_h.3) | copy-start | bytes 6291460
  30.1 5.6 %collective-permute-start.2 = (f32[128,128]{1,0:T(8,128)S(1)}, f32[128,128]{1,0:T(8,128)S(1)}, u32[]{:S(2)}, u32[]{:S(2)}) collective-permute-start(f32[128,128]{1,0:T(8,128)S(1)} %get-tuple-element.40.refs_0_), channel_id=1, source_target_pairs={{0,3},{1,2},{2,1},{3,0},{4,7},{5,6},{6,5},{7,4},{8,11},{9,10},{10,... | collective-permute-start | bytes 196616 | tf_op jit(solution)/shard_map/ppermute | solution.py:570
  30.1 5.8 %collective-permute-start.1 = (f32[128,128]{1,0:T(8,128)S(1)}, f32[128,128]{1,0:T(8,128)S(1)}, u32[]{:S(2)}, u32[]{:S(2)}) collective-permute-start(f32[128,128]{1,0:T(8,128)S(1)} %get-tuple-element.40.refs_0_), channel_id=1, source_target_pairs={{0,2},{1,3},{2,0},{3,1},{4,6},{5,7},{6,4},{7,5},{8,10},{9,11},{10,... | collective-permute-start | bytes 196616 | tf_op jit(solution)/shard_map/ppermute | solution.py:570
  31.7 4.2 %collective-permute-start = (f32[128,128]{1,0:T(8,128)S(1)}, f32[128,128]{1,0:T(8,128)S(1)}, u32[]{:S(2)}, u32[]{:S(2)}) collective-permute-start(f32[128,128]{1,0:T(8,128)S(1)} %get-tuple-element.40.refs_0_), channel_id=1, source_target_pairs={{0,1},{1,0},{2,3},{3,2},{4,5},{5,4},{6,7},{7,6},{8,9},{9,8},{10,11... | collective-permute-start | bytes 196616 | tf_op jit(solution)/shard_map/ppermute | solution.py:570
  41.3 1.6 %collective-permute-start.3 = (f32[264,128]{1,0:T(8,128)S(1)}, f32[264,128]{1,0:T(8,128)S(1)}, u32[]{:S(2)}, u32[]{:S(2)}) collective-permute-start(f32[264,128]{1,0:T(8,128)S(1)} %get-tuple-element.51), channel_id=1, source_target_pairs={{0,1},{1,0},{2,3},{3,2},{4,5},{5,4},{6,7},{7,6},{8,9},{9,8},{10,11... | collective-permute-start | bytes 405512 | tf_op jit(solution)/shard_map/ppermute | solution.py:570
  43.0 6.0 %collective-permute-start.4 = (f32[264,128]{1,0:T(8,128)S(1)}, f32[264,128]{1,0:T(8,128)S(1)}, u32[]{:S(2)}, u32[]{:S(2)}) collective-permute-start(f32[264,128]{1,0:T(8,128)S(1)} %get-tuple-element.53.mine), channel_id=1, source_target_pairs={{0,2},{1,3},{2,0},{3,1},{4,6},{5,7},{6,4},{7,5},{8,10},{9,11},{10,... | collective-permute-start | bytes 405512 | tf_op jit(solution)/shard_map/ppermute | solution.py:570
  44.3 3.7 %collective-permute-start.5 = (f32[32,128]{1,0:T(8,128)S(1)}, f32[32,128]{1,0:T(8,128)S(1)}, u32[]{:S(2)}, u32[]{:S(2)}) collective-permute-start(f32[32,128]{1,0:T(8,128)S(1)} %get-tuple-element.56), channel_id=1, source_target_pairs={{0,4},{4,0},{8,12},{12,8},{16,20},{20,16},{24,28},{28,24},{1,5},{5... | collective-permute-start | bytes 49160 | tf_op jit(solution)/shard_map/ppermute | solution.py:681
  49.2 1.4 %collective-permute-start.6 = (f32[264,128]{1,0:T(8,128)S(1)}, f32[264,128]{1,0:T(8,128)S(1)}, u32[]{:S(2)}, u32[]{:S(2)}) collective-permute-start(f32[264,128]{1,0:T(8,128)S(1)} %get-tuple-element.57.gap_mine), channel_id=1, source_target_pairs={{0,1},{1,0},{2,3},{3,2},{4,5},{5,4},{6,7},{7,6},{8,9},{9,8},{10,11... | collective-permute-start | bytes 405512 | tf_op jit(solution)/shard_map/ppermute | solution.py:570
  66.3 1.6 %collective-permute-start.7 = (f32[264,128]{1,0:T(8,128)S(1)}, f32[264,128]{1,0:T(8,128)S(1)}, u32[]{:S(2)}, u32[]{:S(2)}) collective-permute-start(f32[264,128]{1,0:T(8,128)S(1)} %get-tuple-element.61), channel_id=1, source_target_pairs={{0,1},{1,0},{2,3},{3,2},{4,5},{5,4},{6,7},{7,6},{8,9},{9,8},{10,11... | collective-permute-start | bytes 405512 | tf_op jit(solution)/shard_map/ppermute | solution.py:570
  68.0 6.0 %collective-permute-start.8 = (f32[264,128]{1,0:T(8,128)S(1)}, f32[264,128]{1,0:T(8,128)S(1)}, u32[]{:S(2)}, u32[]{:S(2)}) collective-permute-start(f32[264,128]{1,0:T(8,128)S(1)} %get-tuple-element.63.mine), channel_id=1, source_target_pairs={{0,2},{1,3},{2,0},{3,1},{4,6},{5,7},{6,4},{7,5},{8,10},{9,11},{10,... | collective-permute-start | bytes 405512 | tf_op jit(solution)/shard_map/ppermute | solution.py:570
  69.3 3.7 %collective-permute-start.9 = (f32[32,128]{1,0:T(8,128)S(1)}, f32[32,128]{1,0:T(8,128)S(1)}, u32[]{:S(2)}, u32[]{:S(2)}) collective-permute-start(f32[32,128]{1,0:T(8,128)S(1)} %get-tuple-element.65), channel_id=1, source_target_pairs={{0,4},{4,0},{8,12},{12,8},{16,20},{20,16},{24,28},{28,24},{1,5},{5... | collective-permute-start | bytes 49160 | tf_op jit(solution)/shard_map/ppermute | solution.py:681
  74.2 1.4 %collective-permute-start.10 = (f32[264,128]{1,0:T(8,128)S(1)}, f32[264,128]{1,0:T(8,128)S(1)}, u32[]{:S(2)}, u32[]{:S(2)}) collective-permute-start(f32[264,128]{1,0:T(8,128)S(1)} %get-tuple-element.66.gap_mine), channel_id=1, source_target_pairs={{0,1},{1,0},{2,3},{3,2},{4,5},{5,4},{6,7},{7,6},{8,9},{9,8},{10,11... | collective-permute-start | bytes 405512 | tf_op jit(solution)/shard_map/ppermute | solution.py:570
  90.7 1.6 %collective-permute-start.11 = (f32[264,128]{1,0:T(8,128)S(1)}, f32[264,128]{1,0:T(8,128)S(1)}, u32[]{:S(2)}, u32[]{:S(2)}) collective-permute-start(f32[264,128]{1,0:T(8,128)S(1)} %get-tuple-element.71), channel_id=1, source_target_pairs={{0,1},{1,0},{2,3},{3,2},{4,5},{5,4},{6,7},{7,6},{8,9},{9,8},{10,11... | collective-permute-start | bytes 405512 | tf_op jit(solution)/shard_map/ppermute | solution.py:570
  92.4 6.0 %collective-permute-start.12 = (f32[264,128]{1,0:T(8,128)S(1)}, f32[264,128]{1,0:T(8,128)S(1)}, u32[]{:S(2)}, u32[]{:S(2)}) collective-permute-start(f32[264,128]{1,0:T(8,128)S(1)} %shard_map.138.mine), channel_id=1, source_target_pairs={{0,2},{1,3},{2,0},{3,1},{4,6},{5,7},{6,4},{7,5},{8,10},{9,11},{10,... | collective-permute-start | bytes 405512 | tf_op jit(solution)/shard_map/ppermute | solution.py:570
  98.6 1.4 %collective-permute-start.13 = (f32[264,128]{1,0:T(8,128)S(1)}, f32[264,128]{1,0:T(8,128)S(1)}, u32[]{:S(2)}, u32[]{:S(2)}) collective-permute-start(f32[264,128]{1,0:T(8,128)S(1)} %shard_map.139.gap_mine), channel_id=1, source_target_pairs={{0,1},{1,0},{2,3},{3,2},{4,5},{5,4},{6,7},{7,6},{8,9},{9,8},{10,11... | collective-permute-start | bytes 405512 | tf_op jit(solution)/shard_map/ppermute | solution.py:570

commit v5 on v4

--- a/solution.py
+++ b/solution.py
@@ -35,7 +35,7 @@
         self.oi = self.ownp // self.hh
         self.u = max(1, 256 // self.ML)
         self.NS = products // self.u
-        self.per = min(16, self.NS)
+        self.per = self.NS if self.NS <= 32 else 16
         self.NR = max(LANES, 2 * self.RL)
         self.s_draws = 0
         self.s_mass = self.s_draws + traits * self.ii
@@ -53,7 +53,6 @@
 
 
 VM = pl.BlockSpec(memory_space=pltpu.VMEM)
-SM = pl.BlockSpec(memory_space=pltpu.SMEM)
 HBM = pl.BlockSpec(memory_space=pltpu.HBM)
 
 
@@ -107,12 +106,12 @@
 
 
 def pack_kernel(
-    p, scale, size, draws_h, weight_h, loyalty_h, traits_h, firms_h, mean_h, share_h, out_h,
-    draws, weight, loyalty, traits, firms, mean, share, out, sems, out_sems,
+    p, scale_h, size_h, draws_h, weight_h, loyalty_h, traits_h, firms_h, mean_h, share_h, out_h,
+    draws, weight, loyalty, traits, firms, mean, share, out, scale, size, sems, out_sems,
 ):
     pairs = (
         (draws_h, draws), (weight_h, weight), (traits_h, traits), (firms_h, firms),
-        (mean_h, mean), (share_h, share), (loyalty_h, loyalty),
+        (mean_h, mean), (share_h, share), (loyalty_h, loyalty), (scale_h, scale), (size_h, size),
     )
     copies = [pltpu.make_async_copy(a, b, sems.at[n]) for n, (a, b) in enumerate(pairs)]
     for copy in copies:
@@ -592,7 +591,7 @@
             market_share,
         ),
         vmem=60,
-        specs=[SM, SM] + [HBM] * 7,
+        specs=[HBM] * 9,
         out_specs=HBM,
         scratch=(
             pltpu.VMEM((p.K, p.M, p.R), F32),
@@ -603,7 +602,9 @@
             pltpu.VMEM((p.M, p.J), F32),
             pltpu.VMEM((p.M, p.J), F32),
             pltpu.VMEM((p.C * p.S, LANES), F32),
-            pltpu.SemaphoreType.DMA((7,)),
+            pltpu.SMEM((p.K,), F32),
+            pltpu.SMEM((p.M,), F32),
+            pltpu.SemaphoreType.DMA((9,)),
             pltpu.SemaphoreType.DMA((p.C,)),
         ),
     )

time: 112 us -> 110 us (0.982)
  Pallas kernels: 27 us -> 25.1 us
    pallas_call x20, Pallas kernels: 27 us -> 25.1 us  [call(): pl.pallas_call(functools.partial(kernel, p), out_shape=outs, in_specs=spe...]
  transfers between devices with their start and end apart: 14 -> 14, of which waited for: 9 -> 11; matrix products, arithmetic and copies ran while one was open for 1% -> 1% of each run, Pallas kernels for 7% -> 6%
where the time goes in v5:
time: 110 us
  blocking collectives  58.7 us (53%)
  Pallas kernels  25.1 us (23%)
  waiting for transfers between devices  16.8 us (15%)
  starting transfers between devices  7.85 us (7%)
    all_to_all x4, blocking collectives, exchange(): return lax.all_to_all(x, 'mkt', split_axis=0, concat_axis=0, tiled=True)  58.7 us
    pallas_call x20, Pallas kernels, call(): pl.pallas_call(functools.partial(kernel, p), out_shape=outs, in_specs=spe...  25.1 us
    ppermute x12, waiting for transfers between devices, swap(): return lax.ppermute(x, 'grp', [(q, q ^ bit) for q in range(p.Q)])  11.1 us
    ppermute x12, starting transfers between devices, swap(): return lax.ppermute(x, 'grp', [(q, q ^ bit) for q in range(p.Q)])  6.16 us
    ppermute x2, waiting for transfers between devices, local(): lax.ppermute(pred_give, 'mkt', [(c, c ^ 1) for c in range(p.C)])  5.78 us
  transfers between devices with their start and end apart: 14, of which 11 were waited for; matrix products, arithmetic and copies ran while one was open for 1% of the time, Pallas kernels for 6%

profile of v5, /device:TPU:0, one launch (start us, length us, event | category | flops | bytes accessed | tf_op | source)
XLA Modules:
  0.0 110.1 jit_solution(880248495088438448)
XLA Ops:
  0.6 2.4 %shard_map.122 = f32[1408,128]{1,0:T(8,128)} custom-call(f32[5]{0:T(128)} %scale_h.1, f32[16]{0:T(128)} %size_h.1, f32[5,16,1024]{2,1,0:T(8,128)} %bitcast.23, f32[16,1024]{1,0:T(8,128)} %weight_h.1, f32[16,1024]{1,0:T(8,128)} %loyalty_h.1, f32[5,16,64]{2,1,0:T(8,128)} %bitcast.25, s32[16,64]{1,0:T(8,128)} %firms_h.1, f32[16,64]{1,0:T(8,128)} %mean_h.1, ...), custom_call_target="tpu_custom_call" | custom-call | tf_op jit(solution)/shard_map/pallas_call | solution.py:60
  3.0 26.1 %all_to_all.44 = f32[8,176,128]{2,1,0:T(8,128)S(1)} all-to-all(f32[8,176,128]{2,1,0:T(8,128)} %bitcast.22), channel_id=1, replica_groups=mesh['mkt'=8,'grp'=4] {'mkt'}, dimensions={0} | all-to-all | bytes 1441792 | tf_op jit(solution)/shard_map/all_to_all | solution.py:566
  29.1 0.3 shard_map.123
  29.4 0.1 collective-permute-start.2
  29.5 1.6 %collective-permute-start.1 = (f32[128,128]{1,0:T(8,128)S(1)}, f32[128,128]{1,0:T(8,128)S(1)}, u32[]{:S(2)}, u32[]{:S(2)}) collective-permute-start(f32[128,128]{1,0:T(8,128)S(1)} %get-tuple-element.40.refs_0_), channel_id=1, source_target_pairs={{0,2},{1,3},{2,0},{3,1},{4,6},{5,7},{6,4},{7,5},{8,10},{9,11},{10,... | collective-permute-start | bytes 196616 | tf_op jit(solution)/shard_map/ppermute | solution.py:569
  31.1 0.3 collective-permute-start
  31.4 0.8 reshape.20
  32.1 0.1 reshape.21.order
  32.2 2.8 %shard_map.125 = (f32[64,128,128]{2,1,0:T(8,128)S(1)}, bf16[64,1,512,128]{3,2,1,0:T(8,128)(2,1)S(1)}) custom-call(f32[5,128,128]{2,1,0:T(8,128)S(1)} %get-tuple-element.43.draws_t, f32[5,1,64,128]{3,2,1,0:T(8,128)S(1)} %get-tuple-element.44.traits_t, f32[1,64,128]{2,1,0:T(8,128)S(1)} %get-tuple-element.45.firms_t), custom_call_target="tpu_custom_call" | custom-call | tf_op jit(solution)/shard_map/pallas_call | solution.py:60
  35.0 0.0 collective-permute-done.2.refs_3_
  35.0 0.3 collective-permute-done.1.refs_2_
  35.3 0.0 collective-permute-done.refs_1_
  35.3 0.6 shard_map.124
  35.9 4.6 %shard_map.126 = (f32[32,128]{1,0:T(8,128)S(1)}, f32[32,128]{1,0:T(8,128)S(1)}, bf16[32,2,256,128]{3,2,1,0:T(8,128)(2,1)S(1)}, f32[264,128]{1,0:T(8,128)S(1)}) custom-call(f32[512,128]{1,0:T(8,128)S(1)} %get-tuple-element.41.table.table_in, f32[1,64,128]{2,1,0:T(8,128)S(1)} %get-tuple-element.42.mean_t.mean_in, f32[64,128,128]{2,1,0:T(8,128)S(1)} %get-tuple-element.46.taste, ...), custom_call_target="tpu_custom_call" | custom-call | tf_op jit(solution)/shard_map/pallas_call | solution.py:60
  40.5 0.1 collective-permute-start.3
  40.7 1.3 %shard_map.127.a = f32[264,128]{1,0:T(8,128)S(1)} custom-call(bf16[32,2,256,128]{3,2,1,0:T(8,128)(2,1)S(1)} %get-tuple-element.50.parts, bf16[64,1,512,128]{3,2,1,0:T(8,128)(2,1)S(1)} %get-tuple-element.47.hot, f32[8,128]{1,0:T(8,128)S(1)} %get-tuple-element.49.mass_row), custom_call_target="tpu_custom_call" | custom-call | tf_op jit(solution)/shard_map/pallas_call | solution.py:60
  41.9 0.0 collective-permute-done.3.b
  42.0 1.3 %collective-permute-start.4 = (f32[264,128]{1,0:T(8,128)S(1)}, f32[264,128]{1,0:T(8,128)S(1)}, u32[]{:S(2)}, u32[]{:S(2)}) collective-permute-start(f32[264,128]{1,0:T(8,128)S(1)} %get-tuple-element.53.mine), channel_id=1, source_target_pairs={{0,2},{1,3},{2,0},{3,1},{4,6},{5,7},{6,4},{7,5},{8,10},{9,11},{10,... | collective-permute-start | bytes 405512 | tf_op jit(solution)/shard_map/ppermute | solution.py:569
  43.3 1.4 %collective-permute-start.5 = (f32[32,128]{1,0:T(8,128)S(1)}, f32[32,128]{1,0:T(8,128)S(1)}, u32[]{:S(2)}, u32[]{:S(2)}) collective-permute-start(f32[32,128]{1,0:T(8,128)S(1)} %get-tuple-element.56), channel_id=1, source_target_pairs={{0,4},{4,0},{8,12},{12,8},{16,20},{20,16},{24,28},{28,24},{1,5},{5... | collective-permute-start | bytes 49160 | tf_op jit(solution)/shard_map/ppermute | solution.py:682
  44.7 2.4 %collective-permute-done.5.refs_1_ = f32[32,128]{1,0:T(8,128)S(1)} collective-permute-done((f32[32,128]{1,0:T(8,128)S(1)}, f32[32,128]{1,0:T(8,128)S(1)}, u32[]{:S(2)}, u32[]{:S(2)}) %collective-permute-start.5) | collective-permute-done | bytes 16416 | tf_op jit(solution)/shard_map/ppermute | solution.py:682
  47.1 0.9 collective-permute-done.4.other
  48.0 0.2 shard_map.129
  48.2 1.4 %collective-permute-done.6.gap_other = f32[264,128]{1,0:T(8,128)S(1)} collective-permute-done((f32[264,128]{1,0:T(8,128)S(1)}, f32[264,128]{1,0:T(8,128)S(1)}, u32[]{:S(2)}, u32[]{:S(2)}) %collective-permute-start.6) | collective-permute-done | bytes 135200 | tf_op jit(solution)/shard_map/ppermute | solution.py:569
  49.5 11.1 %all_to_all.45 = f32[8,40,128]{2,1,0:T(8,128)S(1)} all-to-all(f32[8,40,128]{2,1,0:T(8,128)S(1)} %bitcast.17), channel_id=1, replica_groups=mesh['mkt'=8,'grp'=4] {'mkt'}, dimensions={0} | all-to-all | bytes 327680 | tf_op jit(solution)/shard_map/all_to_all | solution.py:566
  60.6 4.5 %shard_map.131 = (f32[512,128]{1,0:T(8,128)S(1)}, f32[1,64,128]{2,1,0:T(8,128)S(1)}, f32[32,128]{1,0:T(8,128)S(1)}, f32[32,128]{1,0:T(8,128)S(1)}, bf16[32,2,256...) custom-call(f32[320,128]{1,0:T(8,128)S(1)} %bitcast.20, f32[264,128]{1,0:T(8,128)S(1)} %get-tuple-element.57.gap_mine, ...), custom_call_target="tpu_custom_call" | custom-call | tf_op jit(solution)/shard_map/pallas_call | solution.py:60
  65.1 0.1 collective-permute-start.7
  65.2 1.3 %shard_map.132.a = f32[264,128]{1,0:T(8,128)S(1)} custom-call(bf16[32,2,256,128]{3,2,1,0:T(8,128)(2,1)S(1)} %get-tuple-element.60.parts, bf16[64,1,512,128]{3,2,1,0:T(8,128)(2,1)S(1)} %get-tuple-element.47.hot, f32[8,128]{1,0:T(8,128)S(1)} %get-tuple-element.49.mass_row), custom_call_target="tpu_custom_call" | custom-call | tf_op jit(solution)/shard_map/pallas_call | solution.py:60
  66.5 0.1 collective-permute-done.7.b
  66.6 1.3 %collective-permute-start.8 = (f32[264,128]{1,0:T(8,128)S(1)}, f32[264,128]{1,0:T(8,128)S(1)}, u32[]{:S(2)}, u32[]{:S(2)}) collective-permute-start(f32[264,128]{1,0:T(8,128)S(1)} %get-tuple-element.63.mine), channel_id=1, source_target_pairs={{0,2},{1,3},{2,0},{3,1},{4,6},{5,7},{6,4},{7,5},{8,10},{9,11},{10,... | collective-permute-start | bytes 405512 | tf_op jit(solution)/shard_map/ppermute | solution.py:569
  67.9 0.3 collective-permute-start.9
  68.2 3.4 %collective-permute-done.9.refs_1_ = f32[32,128]{1,0:T(8,128)S(1)} collective-permute-done((f32[32,128]{1,0:T(8,128)S(1)}, f32[32,128]{1,0:T(8,128)S(1)}, u32[]{:S(2)}, u32[]{:S(2)}) %collective-permute-start.9) | collective-permute-done | bytes 16416 | tf_op jit(solution)/shard_map/ppermute | solution.py:682
  71.6 1.0 collective-permute-done.8.other
  72.6 0.2 shard_map.134
  72.7 0.0 collective-permute-start.10
  72.7 1.4 %collective-permute-done.10.gap_other = f32[264,128]{1,0:T(8,128)S(1)} collective-permute-done((f32[264,128]{1,0:T(8,128)S(1)}, f32[264,128]{1,0:T(8,128)S(1)}, u32[]{:S(2)}, u32[]{:S(2)}) %collective-permute-start.10) | collective-permute-done | bytes 135200 | tf_op jit(solution)/shard_map/ppermute | solution.py:569
  74.1 10.5 %all_to_all.46 = f32[8,40,128]{2,1,0:T(8,128)S(1)} all-to-all(f32[8,40,128]{2,1,0:T(8,128)S(1)} %bitcast.18), channel_id=1, replica_groups=mesh['mkt'=8,'grp'=4] {'mkt'}, dimensions={0} | all-to-all | bytes 327680 | tf_op jit(solution)/shard_map/all_to_all | solution.py:566
  84.6 4.5 %shard_map.136 = (f32[512,128]{1,0:T(8,128)S(1)}, f32[1,64,128]{2,1,0:T(8,128)S(1)}, f32[64,128]{1,0:T(8,128)S(1)}, bf16[32,2,256,128]{3,2,1,0:T(8,128)(2,1)S(1)}, f32[264,128]{1,0:T(8,128)S(1)}) custom-call(f32[320,128]{1,0:T(8,128)S(1)} %bitcast.19, f32[264,128]{1,0:T(8,128)S(1)} %get-tuple-element.66.gap_mine, ...), custom_call_target="tpu_custom_call" | custom-call | tf_op jit(solution)/shard_map/pallas_call | solution.py:60
  89.1 0.1 collective-permute-start.11
  89.2 1.3 %shard_map.137.a = f32[264,128]{1,0:T(8,128)S(1)} custom-call(bf16[32,2,256,128]{3,2,1,0:T(8,128)(2,1)S(1)} %get-tuple-element.70.parts, bf16[64,1,512,128]{3,2,1,0:T(8,128)(2,1)S(1)} %get-tuple-element.47.hot, f32[8,128]{1,0:T(8,128)S(1)} %get-tuple-element.49.mass_row), custom_call_target="tpu_custom_call" | custom-call | tf_op jit(solution)/shard_map/pallas_call | solution.py:60
  90.5 0.1 collective-permute-done.11.b
  90.5 1.3 %collective-permute-start.12 = (f32[264,128]{1,0:T(8,128)S(1)}, f32[264,128]{1,0:T(8,128)S(1)}, u32[]{:S(2)}, u32[]{:S(2)}) collective-permute-start(f32[264,128]{1,0:T(8,128)S(1)} %shard_map.138.mine), channel_id=1, source_target_pairs={{0,2},{1,3},{2,0},{3,1},{4,6},{5,7},{6,4},{7,5},{8,10},{9,11},{10,... | collective-permute-start | bytes 405512 | tf_op jit(solution)/shard_map/ppermute | solution.py:569
  91.9 4.7 %collective-permute-done.12.other = f32[264,128]{1,0:T(8,128)S(1)} collective-permute-done((f32[264,128]{1,0:T(8,128)S(1)}, f32[264,128]{1,0:T(8,128)S(1)}, u32[]{:S(2)}, u32[]{:S(2)}) %collective-permute-start.12) | collective-permute-done | bytes 135200 | tf_op jit(solution)/shard_map/ppermute | solution.py:569
  96.6 0.2 shard_map.139.gap_mine
  96.7 0.0 collective-permute-start.13
  96.7 1.4 %collective-permute-done.13.gap_other = f32[264,128]{1,0:T(8,128)S(1)} collective-permute-done((f32[264,128]{1,0:T(8,128)S(1)}, f32[264,128]{1,0:T(8,128)S(1)}, u32[]{:S(2)}, u32[]{:S(2)}) %collective-permute-start.13) | collective-permute-done | bytes 135200 | tf_op jit(solution)/shard_map/ppermute | solution.py:569
  98.1 0.4 shard_map.140
  98.4 11.0 %all_to_all.47 = f32[8,48,128]{2,1,0:T(8,128)S(1)} all-to-all(f32[8,48,128]{2,1,0:T(8,128)S(1)} %bitcast.21), channel_id=1, replica_groups=mesh['mkt'=8,'grp'=4] {'mkt'}, dimensions={0} | all-to-all | bytes 393216 | tf_op jit(solution)/shard_map/all_to_all | solution.py:566
  109.4 0.7 shard_map.141
  (9 shorter events, 0.1 us)
Async XLA Ops:
  0.6 34.7 %copy-start = (f32[512,1024]{1,0:T(8,128)S(1)}, f32[512,1024]{1,0:T(8,128)}, u32[]{:S(2)}) copy-start(f32[512,1024]{1,0:T(8,128)} %share_h.3) | copy-start | bytes 6291460
  29.4 5.6 %collective-permute-start.2 = (f32[128,128]{1,0:T(8,128)S(1)}, f32[128,128]{1,0:T(8,128)S(1)}, u32[]{:S(2)}, u32[]{:S(2)}) collective-permute-start(f32[128,128]{1,0:T(8,128)S(1)} %get-tuple-element.40.refs_0_), channel_id=1, source_target_pairs={{0,3},{1,2},{2,1},{3,0},{4,7},{5,6},{6,5},{7,4},{8,11},{9,10},{10,... | collective-permute-start | bytes 196616 | tf_op jit(solution)/shard_map/ppermute | solution.py:569
  29.5 5.8 %collective-permute-start.1 = (f32[128,128]{1,0:T(8,128)S(1)}, f32[128,128]{1,0:T(8,128)S(1)}, u32[]{:S(2)}, u32[]{:S(2)}) collective-permute-start(f32[128,128]{1,0:T(8,128)S(1)} %get-tuple-element.40.refs_0_), channel_id=1, source_target_pairs={{0,2},{1,3},{2,0},{3,1},{4,6},{5,7},{6,4},{7,5},{8,10},{9,11},{10,... | collective-permute-start | bytes 196616 | tf_op jit(solution)/shard_map/ppermute | solution.py:569
  31.1 4.2 %collective-permute-start = (f32[128,128]{1,0:T(8,128)S(1)}, f32[128,128]{1,0:T(8,128)S(1)}, u32[]{:S(2)}, u32[]{:S(2)}) collective-permute-start(f32[128,128]{1,0:T(8,128)S(1)} %get-tuple-element.40.refs_0_), channel_id=1, source_target_pairs={{0,1},{1,0},{2,3},{3,2},{4,5},{5,4},{6,7},{7,6},{8,9},{9,8},{10,11... | collective-permute-start | bytes 196616 | tf_op jit(solution)/shard_map/ppermute | solution.py:569
  40.5 1.4 %collective-permute-start.3 = (f32[264,128]{1,0:T(8,128)S(1)}, f32[264,128]{1,0:T(8,128)S(1)}, u32[]{:S(2)}, u32[]{:S(2)}) collective-permute-start(f32[264,128]{1,0:T(8,128)S(1)} %get-tuple-element.51), channel_id=1, source_target_pairs={{0,1},{1,0},{2,3},{3,2},{4,5},{5,4},{6,7},{7,6},{8,9},{9,8},{10,11... | collective-permute-start | bytes 405512 | tf_op jit(solution)/shard_map/ppermute | solution.py:569
  42.0 6.0 %collective-permute-start.4 = (f32[264,128]{1,0:T(8,128)S(1)}, f32[264,128]{1,0:T(8,128)S(1)}, u32[]{:S(2)}, u32[]{:S(2)}) collective-permute-start(f32[264,128]{1,0:T(8,128)S(1)} %get-tuple-element.53.mine), channel_id=1, source_target_pairs={{0,2},{1,3},{2,0},{3,1},{4,6},{5,7},{6,4},{7,5},{8,10},{9,11},{10,... | collective-permute-start | bytes 405512 | tf_op jit(solution)/shard_map/ppermute | solution.py:569
  43.3 3.7 %collective-permute-start.5 = (f32[32,128]{1,0:T(8,128)S(1)}, f32[32,128]{1,0:T(8,128)S(1)}, u32[]{:S(2)}, u32[]{:S(2)}) collective-permute-start(f32[32,128]{1,0:T(8,128)S(1)} %get-tuple-element.56), channel_id=1, source_target_pairs={{0,4},{4,0},{8,12},{12,8},{16,20},{20,16},{24,28},{28,24},{1,5},{5... | collective-permute-start | bytes 49160 | tf_op jit(solution)/shard_map/ppermute | solution.py:682
  48.2 1.4 %collective-permute-start.6 = (f32[264,128]{1,0:T(8,128)S(1)}, f32[264,128]{1,0:T(8,128)S(1)}, u32[]{:S(2)}, u32[]{:S(2)}) collective-permute-start(f32[264,128]{1,0:T(8,128)S(1)} %get-tuple-element.57.gap_mine), channel_id=1, source_target_pairs={{0,1},{1,0},{2,3},{3,2},{4,5},{5,4},{6,7},{7,6},{8,9},{9,8},{10,11... | collective-permute-start | bytes 405512 | tf_op jit(solution)/shard_map/ppermute | solution.py:569
  65.1 1.4 %collective-permute-start.7 = (f32[264,128]{1,0:T(8,128)S(1)}, f32[264,128]{1,0:T(8,128)S(1)}, u32[]{:S(2)}, u32[]{:S(2)}) collective-permute-start(f32[264,128]{1,0:T(8,128)S(1)} %get-tuple-element.61), channel_id=1, source_target_pairs={{0,1},{1,0},{2,3},{3,2},{4,5},{5,4},{6,7},{7,6},{8,9},{9,8},{10,11... | collective-permute-start | bytes 405512 | tf_op jit(solution)/shard_map/ppermute | solution.py:569
  66.6 6.0 %collective-permute-start.8 = (f32[264,128]{1,0:T(8,128)S(1)}, f32[264,128]{1,0:T(8,128)S(1)}, u32[]{:S(2)}, u32[]{:S(2)}) collective-permute-start(f32[264,128]{1,0:T(8,128)S(1)} %get-tuple-element.63.mine), channel_id=1, source_target_pairs={{0,2},{1,3},{2,0},{3,1},{4,6},{5,7},{6,4},{7,5},{8,10},{9,11},{10,... | collective-permute-start | bytes 405512 | tf_op jit(solution)/shard_map/ppermute | solution.py:569
  67.9 3.7 %collective-permute-start.9 = (f32[32,128]{1,0:T(8,128)S(1)}, f32[32,128]{1,0:T(8,128)S(1)}, u32[]{:S(2)}, u32[]{:S(2)}) collective-permute-start(f32[32,128]{1,0:T(8,128)S(1)} %get-tuple-element.65), channel_id=1, source_target_pairs={{0,4},{4,0},{8,12},{12,8},{16,20},{20,16},{24,28},{28,24},{1,5},{5... | collective-permute-start | bytes 49160 | tf_op jit(solution)/shard_map/ppermute | solution.py:682
  72.7 1.4 %collective-permute-start.10 = (f32[264,128]{1,0:T(8,128)S(1)}, f32[264,128]{1,0:T(8,128)S(1)}, u32[]{:S(2)}, u32[]{:S(2)}) collective-permute-start(f32[264,128]{1,0:T(8,128)S(1)} %get-tuple-element.66.gap_mine), channel_id=1, source_target_pairs={{0,1},{1,0},{2,3},{3,2},{4,5},{5,4},{6,7},{7,6},{8,9},{9,8},{10,11... | collective-permute-start | bytes 405512 | tf_op jit(solution)/shard_map/ppermute | solution.py:569
  89.1 1.4 %collective-permute-start.11 = (f32[264,128]{1,0:T(8,128)S(1)}, f32[264,128]{1,0:T(8,128)S(1)}, u32[]{:S(2)}, u32[]{:S(2)}) collective-permute-start(f32[264,128]{1,0:T(8,128)S(1)} %get-tuple-element.71), channel_id=1, source_target_pairs={{0,1},{1,0},{2,3},{3,2},{4,5},{5,4},{6,7},{7,6},{8,9},{9,8},{10,11... | collective-permute-start | bytes 405512 | tf_op jit(solution)/shard_map/ppermute | solution.py:569
  90.5 6.0 %collective-permute-start.12 = (f32[264,128]{1,0:T(8,128)S(1)}, f32[264,128]{1,0:T(8,128)S(1)}, u32[]{:S(2)}, u32[]{:S(2)}) collective-permute-start(f32[264,128]{1,0:T(8,128)S(1)} %shard_map.138.mine), channel_id=1, source_target_pairs={{0,2},{1,3},{2,0},{3,1},{4,6},{5,7},{6,4},{7,5},{8,10},{9,11},{10,... | collective-permute-start | bytes 405512 | tf_op jit(solution)/shard_map/ppermute | solution.py:569
  96.7 1.4 %collective-permute-start.13 = (f32[264,128]{1,0:T(8,128)S(1)}, f32[264,128]{1,0:T(8,128)S(1)}, u32[]{:S(2)}, u32[]{:S(2)}) collective-permute-start(f32[264,128]{1,0:T(8,128)S(1)} %shard_map.139.gap_mine), channel_id=1, source_target_pairs={{0,1},{1,0},{2,3},{3,2},{4,5},{5,4},{6,7},{7,6},{8,9},{9,8},{10,11... | collective-permute-start | bytes 405512 | tf_op jit(solution)/shard_map/ppermute | solution.py:569

commit v6 on v5

--- a/solution.py
+++ b/solution.py
@@ -36,6 +36,7 @@
         self.u = max(1, 256 // self.ML)
         self.NS = products // self.u
         self.per = self.NS if self.NS <= 32 else 16
+        self.plain = self.hh == 1 and mkt * own_firms == LANES and LANES % (grp * own_firms) == 0
         self.NR = max(LANES, 2 * self.RL)
         self.s_draws = 0
         self.s_mass = self.s_draws + traits * self.ii
@@ -229,7 +230,18 @@
         loy[c * p.oi : (c + 1) * p.oi, :] = recv[c * p.S + p.s_loy : c * p.S + p.s_loy + p.oi, :]
 
 
-def taste_kernel(p, draws_t, traits_t, firms_t, taste, hot):
+def taste_kernel(p, draws_t, traits_t, firms_t, order_in, taste, hot, order):
+    if p.plain:
+        spread = [jnp.broadcast_to(order_in[n : n + 1, :], (8, LANES)) for n in range(p.F // LANES)]
+        for q in range(p.Q):
+            row = None
+            for c in range(p.C):
+                n, at = divmod((c * p.Q + q) * p.own, LANES)
+                piece = moved(spread[n], c * p.own - at)
+                row = piece if row is None else jnp.where(block_mask(p.own, 8, c), piece, row)
+            order[q : q + 1, :] = row[0:1, :]
+    else:
+        order[...] = order_in[...]
     rows = min(p.F, 256)
     firm = lax.broadcasted_iota(jnp.int32, (rows, LANES), 0).astype(F32).astype(BF)
 
@@ -568,10 +580,13 @@
     def swap(x, bit):
         return lax.ppermute(x, "grp", [(q, q ^ bit) for q in range(p.Q)])
 
-    order = firm_order.reshape(p.C, p.Q, p.own)
-    order = jnp.pad(order, ((0, 0), (0, 0), (0, p.ownp - p.own)), constant_values=-1)
-    order = order.reshape(p.C, p.Q, p.hh, p.oi).transpose(1, 2, 0, 3).reshape(p.Q * p.hh, p.C * p.oi)
-    order = jnp.pad(order, ((0, 0), (0, LANES - p.C * p.oi)), constant_values=-1)
+    if p.plain:
+        order = firm_order.reshape(p.F // LANES, LANES)
+    else:
+        order = firm_order.reshape(p.C, p.Q, p.own)
+        order = jnp.pad(order, ((0, 0), (0, 0), (0, p.ownp - p.own)), constant_values=-1)
+        order = order.reshape(p.C, p.Q, p.hh, p.oi).transpose(1, 2, 0, 3).reshape(p.Q * p.hh, p.C * p.oi)
+        order = jnp.pad(order, ((0, 0), (0, LANES - p.C * p.oi)), constant_values=-1)
     if p.ownp > p.own:
         loyalty = jnp.pad(loyalty, ((0, p.ownp - p.own), (0, 0)))
 
@@ -626,11 +641,11 @@
         scratch=(pltpu.VMEM((max(LANES, p.PR), LANES), F32),),
     )
     rows = [loy] + [swap(loy, bits) for bits in range(1, p.Q)]
-    taste, hot = call(
+    taste, hot, order = call(
         p,
         taste_kernel,
-        (sds((p.J, p.RL, p.ML)), sds((p.J, p.hh, p.F, LANES), BF)),
-        (draws_t, traits_t, firms_t),
+        (sds((p.J, p.RL, p.ML)), sds((p.J, p.hh, p.F, LANES), BF), sds((p.Q * p.hh, LANES), jnp.int32)),
+        (draws_t, traits_t, firms_t, order),
     )
     table, share, columns = call(
         p,

time: 110 us -> 110 us (level)
  transfers between devices with their start and end apart: 14 -> 14, of which waited for: 11 -> 11; matrix products, arithmetic and copies ran while one was open for 1% -> 0% of each run, Pallas kernels for 6% -> 6%
where the time goes in v6:
time: 110 us
  blocking collectives  58.7 us (53%)
  Pallas kernels  25.1 us (23%)
  waiting for transfers between devices  17.2 us (16%)
  starting transfers between devices  7.62 us (7%)
    all_to_all x4, blocking collectives, exchange(): return lax.all_to_all(x, 'mkt', split_axis=0, concat_axis=0, tiled=True)  58.7 us
    pallas_call x20, Pallas kernels, call(): pl.pallas_call(functools.partial(kernel, p), out_shape=outs, in_specs=spe...  25.1 us
    ppermute x12, waiting for transfers between devices, swap(): return lax.ppermute(x, 'grp', [(q, q ^ bit) for q in range(p.Q)])  11.4 us
    ppermute x12, starting transfers between devices, swap(): return lax.ppermute(x, 'grp', [(q, q ^ bit) for q in range(p.Q)])  5.92 us
    ppermute x2, waiting for transfers between devices, local(): lax.ppermute(pred_give, 'mkt', [(c, c ^ 1) for c in range(p.C)])  5.78 us
  transfers between devices with their start and end apart: 14, of which 11 were waited for; matrix products, arithmetic and copies ran while one was open for 0% of the time, Pallas kernels for 6%

profile of v6, /device:TPU:0, one launch (start us, length us, event | category | flops | bytes accessed | tf_op | source)
XLA Modules:
  0.0 110.1 jit_solution(1852184122051018153)
XLA Ops:
  0.6 2.4 %shard_map.122 = f32[1408,128]{1,0:T(8,128)} custom-call(f32[5]{0:T(128)} %scale_h.1, f32[16]{0:T(128)} %size_h.1, f32[5,16,1024]{2,1,0:T(8,128)} %bitcast.20, f32[16,1024]{1,0:T(8,128)} %weight_h.1, f32[16,1024]{1,0:T(8,128)} %loyalty_h.1, f32[5,16,64]{2,1,0:T(8,128)} %bitcast.21, s32[16,64]{1,0:T(8,128)} %firms_h.1, f32[16,64]{1,0:T(8,128)} %mean_h.1, ...), custom_call_target="tpu_custom_call" | custom-call | tf_op jit(solution)/shard_map/pallas_call | solution.py:61
  3.0 26.1 %all_to_all.44 = f32[8,176,128]{2,1,0:T(8,128)S(1)} all-to-all(f32[8,176,128]{2,1,0:T(8,128)} %bitcast.19), channel_id=1, replica_groups=mesh['mkt'=8,'grp'=4] {'mkt'}, dimensions={0} | all-to-all | bytes 1441792 | tf_op jit(solution)/shard_map/all_to_all | solution.py:578
  29.1 0.3 shard_map.123
  29.4 0.1 collective-permute-start.2
  29.5 1.6 %collective-permute-start.1 = (f32[128,128]{1,0:T(8,128)S(1)}, f32[128,128]{1,0:T(8,128)S(1)}, u32[]{:S(2)}, u32[]{:S(2)}) collective-permute-start(f32[128,128]{1,0:T(8,128)S(1)} %get-tuple-element.45.refs_0_), channel_id=1, source_target_pairs={{0,2},{1,3},{2,0},{3,1},{4,6},{5,7},{6,4},{7,5},{8,10},{9,11},{10,... | collective-permute-start | bytes 196616 | tf_op jit(solution)/shard_map/ppermute | solution.py:581
  31.1 0.3 collective-permute-start
  31.4 0.7 copy-done.1
  32.1 2.8 %shard_map.124 = (f32[64,128,128]{2,1,0:T(8,128)S(1)}, bf16[64,1,512,128]{3,2,1,0:T(8,128)(2,1)S(1)}, s32[4,128]{1,0:T(4,128)S(1)}) custom-call(f32[5,128,128]{2,1,0:T(8,128)S(1)} %get-tuple-element.41.draws_t, f32[5,1,64,128]{3,2,1,0:T(8,128)S(1)} %get-tuple-element.42.traits_t, f32[1,64,128]{2,1,0:T(8,128)S(1)} %get-tuple-element.43.firms_t, ...), custom_call_target="tpu_custom_call" | custom-call | tf_op jit(solution)/shard_map/pallas_call | solution.py:61
  34.9 0.0 collective-permute-done.2.refs_3_
  34.9 0.4 collective-permute-done.1.refs_2_
  35.3 0.0 collective-permute-done.refs_1_
  35.3 0.6 shard_map.125
  36.0 4.6 %shard_map.126 = (f32[32,128]{1,0:T(8,128)S(1)}, f32[32,128]{1,0:T(8,128)S(1)}, bf16[32,2,256,128]{3,2,1,0:T(8,128)(2,1)S(1)}, f32[264,128]{1,0:T(8,128)S(1)}) custom-call(f32[512,128]{1,0:T(8,128)S(1)} %get-tuple-element.46.table.table_in, f32[1,64,128]{2,1,0:T(8,128)S(1)} %get-tuple-element.47.mean_t.mean_in, f32[64,128,128]{2,1,0:T(8,128)S(1)} %get-tuple-element.48.taste, ...), custom_call_target="tpu_custom_call" | custom-call | tf_op jit(solution)/shard_map/pallas_call | solution.py:61
  40.5 0.1 collective-permute-start.3
  40.6 1.3 %shard_map.127.a = f32[264,128]{1,0:T(8,128)S(1)} custom-call(bf16[32,2,256,128]{3,2,1,0:T(8,128)(2,1)S(1)} %get-tuple-element.52.parts, bf16[64,1,512,128]{3,2,1,0:T(8,128)(2,1)S(1)} %get-tuple-element.49.hot, f32[8,128]{1,0:T(8,128)S(1)} %get-tuple-element.51.mass_row), custom_call_target="tpu_custom_call" | custom-call | tf_op jit(solution)/shard_map/pallas_call | solution.py:61
  41.9 0.0 collective-permute-done.3.b
  42.0 1.3 %collective-permute-start.4 = (f32[264,128]{1,0:T(8,128)S(1)}, f32[264,128]{1,0:T(8,128)S(1)}, u32[]{:S(2)}, u32[]{:S(2)}) collective-permute-start(f32[264,128]{1,0:T(8,128)S(1)} %get-tuple-element.55.mine), channel_id=1, source_target_pairs={{0,2},{1,3},{2,0},{3,1},{4,6},{5,7},{6,4},{7,5},{8,10},{9,11},{10,... | collective-permute-start | bytes 405512 | tf_op jit(solution)/shard_map/ppermute | solution.py:581
  43.2 1.4 %collective-permute-start.5 = (f32[32,128]{1,0:T(8,128)S(1)}, f32[32,128]{1,0:T(8,128)S(1)}, u32[]{:S(2)}, u32[]{:S(2)}) collective-permute-start(f32[32,128]{1,0:T(8,128)S(1)} %get-tuple-element.58), channel_id=1, source_target_pairs={{0,4},{4,0},{8,12},{12,8},{16,20},{20,16},{24,28},{28,24},{1,5},{5... | collective-permute-start | bytes 49160 | tf_op jit(solution)/shard_map/ppermute | solution.py:697
  44.6 2.4 %collective-permute-done.5.refs_1_ = f32[32,128]{1,0:T(8,128)S(1)} collective-permute-done((f32[32,128]{1,0:T(8,128)S(1)}, f32[32,128]{1,0:T(8,128)S(1)}, u32[]{:S(2)}, u32[]{:S(2)}) %collective-permute-start.5) | collective-permute-done | bytes 16416 | tf_op jit(solution)/shard_map/ppermute | solution.py:697
  47.0 1.0 collective-permute-done.4.other
  48.0 0.2 shard_map.129
  48.2 0.0 collective-permute-start.6
  48.2 1.4 %collective-permute-done.6.gap_other = f32[264,128]{1,0:T(8,128)S(1)} collective-permute-done((f32[264,128]{1,0:T(8,128)S(1)}, f32[264,128]{1,0:T(8,128)S(1)}, u32[]{:S(2)}, u32[]{:S(2)}) %collective-permute-start.6) | collective-permute-done | bytes 135200 | tf_op jit(solution)/shard_map/ppermute | solution.py:581
  49.5 11.1 %all_to_all.45 = f32[8,40,128]{2,1,0:T(8,128)S(1)} all-to-all(f32[8,40,128]{2,1,0:T(8,128)S(1)} %bitcast.13), channel_id=1, replica_groups=mesh['mkt'=8,'grp'=4] {'mkt'}, dimensions={0} | all-to-all | bytes 327680 | tf_op jit(solution)/shard_map/all_to_all | solution.py:578
  60.6 4.5 %shard_map.131 = (f32[512,128]{1,0:T(8,128)S(1)}, f32[1,64,128]{2,1,0:T(8,128)S(1)}, f32[32,128]{1,0:T(8,128)S(1)}, f32[32,128]{1,0:T(8,128)S(1)}, bf16[32,2,256...) custom-call(f32[320,128]{1,0:T(8,128)S(1)} %bitcast.16, f32[264,128]{1,0:T(8,128)S(1)} %get-tuple-element.59.gap_mine, ...), custom_call_target="tpu_custom_call" | custom-call | tf_op jit(solution)/shard_map/pallas_call | solution.py:61
  65.1 0.1 collective-permute-start.7
  65.2 1.3 %shard_map.132.a = f32[264,128]{1,0:T(8,128)S(1)} custom-call(bf16[32,2,256,128]{3,2,1,0:T(8,128)(2,1)S(1)} %get-tuple-element.62.parts, bf16[64,1,512,128]{3,2,1,0:T(8,128)(2,1)S(1)} %get-tuple-element.49.hot, f32[8,128]{1,0:T(8,128)S(1)} %get-tuple-element.51.mass_row), custom_call_target="tpu_custom_call" | custom-call | tf_op jit(solution)/shard_map/pallas_call | solution.py:61
  66.5 0.1 collective-permute-done.7.b
  66.6 1.2 %collective-permute-start.8 = (f32[264,128]{1,0:T(8,128)S(1)}, f32[264,128]{1,0:T(8,128)S(1)}, u32[]{:S(2)}, u32[]{:S(2)}) collective-permute-start(f32[264,128]{1,0:T(8,128)S(1)} %get-tuple-element.65.mine), channel_id=1, source_target_pairs={{0,2},{1,3},{2,0},{3,1},{4,6},{5,7},{6,4},{7,5},{8,10},{9,11},{10,... | collective-permute-start | bytes 405512 | tf_op jit(solution)/shard_map/ppermute | solution.py:581
  67.8 0.3 collective-permute-start.9
  68.2 3.4 %collective-permute-done.9.refs_1_ = f32[32,128]{1,0:T(8,128)S(1)} collective-permute-done((f32[32,128]{1,0:T(8,128)S(1)}, f32[32,128]{1,0:T(8,128)S(1)}, u32[]{:S(2)}, u32[]{:S(2)}) %collective-permute-start.9) | collective-permute-done | bytes 16416 | tf_op jit(solution)/shard_map/ppermute | solution.py:697
  71.6 1.0 collective-permute-done.8.other
  72.6 0.2 shard_map.134
  72.7 0.0 collective-permute-start.10
  72.8 1.4 %collective-permute-done.10.gap_other = f32[264,128]{1,0:T(8,128)S(1)} collective-permute-done((f32[264,128]{1,0:T(8,128)S(1)}, f32[264,128]{1,0:T(8,128)S(1)}, u32[]{:S(2)}, u32[]{:S(2)}) %collective-permute-start.10) | collective-permute-done | bytes 135200 | tf_op jit(solution)/shard_map/ppermute | solution.py:581
  74.1 10.5 %all_to_all.46 = f32[8,40,128]{2,1,0:T(8,128)S(1)} all-to-all(f32[8,40,128]{2,1,0:T(8,128)S(1)} %bitcast.14), channel_id=1, replica_groups=mesh['mkt'=8,'grp'=4] {'mkt'}, dimensions={0} | all-to-all | bytes 327680 | tf_op jit(solution)/shard_map/all_to_all | solution.py:578
  84.6 4.5 %shard_map.136 = (f32[512,128]{1,0:T(8,128)S(1)}, f32[1,64,128]{2,1,0:T(8,128)S(1)}, f32[64,128]{1,0:T(8,128)S(1)}, bf16[32,2,256,128]{3,2,1,0:T(8,128)(2,1)S(1)}, f32[264,128]{1,0:T(8,128)S(1)}) custom-call(f32[320,128]{1,0:T(8,128)S(1)} %bitcast.15, f32[264,128]{1,0:T(8,128)S(1)} %get-tuple-element.68.gap_mine, ...), custom_call_target="tpu_custom_call" | custom-call | tf_op jit(solution)/shard_map/pallas_call | solution.py:61
  89.1 0.1 collective-permute-start.11
  89.2 1.3 %shard_map.137.a = f32[264,128]{1,0:T(8,128)S(1)} custom-call(bf16[32,2,256,128]{3,2,1,0:T(8,128)(2,1)S(1)} %get-tuple-element.72.parts, bf16[64,1,512,128]{3,2,1,0:T(8,128)(2,1)S(1)} %get-tuple-element.49.hot, f32[8,128]{1,0:T(8,128)S(1)} %get-tuple-element.51.mass_row), custom_call_target="tpu_custom_call" | custom-call | tf_op jit(solution)/shard_map/pallas_call | solution.py:61
  90.5 0.1 collective-permute-done.11.b
  90.5 1.2 %collective-permute-start.12 = (f32[264,128]{1,0:T(8,128)S(1)}, f32[264,128]{1,0:T(8,128)S(1)}, u32[]{:S(2)}, u32[]{:S(2)}) collective-permute-start(f32[264,128]{1,0:T(8,128)S(1)} %shard_map.138.mine), channel_id=1, source_target_pairs={{0,2},{1,3},{2,0},{3,1},{4,6},{5,7},{6,4},{7,5},{8,10},{9,11},{10,... | collective-permute-start | bytes 405512 | tf_op jit(solution)/shard_map/ppermute | solution.py:581
  91.8 4.8 %collective-permute-done.12.other = f32[264,128]{1,0:T(8,128)S(1)} collective-permute-done((f32[264,128]{1,0:T(8,128)S(1)}, f32[264,128]{1,0:T(8,128)S(1)}, u32[]{:S(2)}, u32[]{:S(2)}) %collective-permute-start.12) | collective-permute-done | bytes 135200 | tf_op jit(solution)/shard_map/ppermute | solution.py:581
  96.6 0.2 shard_map.139.gap_mine
  96.7 0.0 collective-permute-start.13
  96.7 1.4 %collective-permute-done.13.gap_other = f32[264,128]{1,0:T(8,128)S(1)} collective-permute-done((f32[264,128]{1,0:T(8,128)S(1)}, f32[264,128]{1,0:T(8,128)S(1)}, u32[]{:S(2)}, u32[]{:S(2)}) %collective-permute-start.13) | collective-permute-done | bytes 135200 | tf_op jit(solution)/shard_map/ppermute | solution.py:581
  98.1 0.4 shard_map.140
  98.4 11.0 %all_to_all.47 = f32[8,48,128]{2,1,0:T(8,128)S(1)} all-to-all(f32[8,48,128]{2,1,0:T(8,128)S(1)} %bitcast.17), channel_id=1, replica_groups=mesh['mkt'=8,'grp'=4] {'mkt'}, dimensions={0} | all-to-all | bytes 393216 | tf_op jit(solution)/shard_map/all_to_all | solution.py:578
  109.4 0.7 shard_map.141
  (8 shorter events, 0.1 us)
Async XLA Ops:
  0.6 34.7 %copy-start = (f32[512,1024]{1,0:T(8,128)S(1)}, f32[512,1024]{1,0:T(8,128)}, u32[]{:S(2)}) copy-start(f32[512,1024]{1,0:T(8,128)} %share_h.3) | copy-start | bytes 6291460
  29.4 5.5 %collective-permute-start.2 = (f32[128,128]{1,0:T(8,128)S(1)}, f32[128,128]{1,0:T(8,128)S(1)}, u32[]{:S(2)}, u32[]{:S(2)}) collective-permute-start(f32[128,128]{1,0:T(8,128)S(1)} %get-tuple-element.45.refs_0_), channel_id=1, source_target_pairs={{0,3},{1,2},{2,1},{3,0},{4,7},{5,6},{6,5},{7,4},{8,11},{9,10},{10,... | collective-permute-start | bytes 196616 | tf_op jit(solution)/shard_map/ppermute | solution.py:581
  29.5 5.8 %collective-permute-start.1 = (f32[128,128]{1,0:T(8,128)S(1)}, f32[128,128]{1,0:T(8,128)S(1)}, u32[]{:S(2)}, u32[]{:S(2)}) collective-permute-start(f32[128,128]{1,0:T(8,128)S(1)} %get-tuple-element.45.refs_0_), channel_id=1, source_target_pairs={{0,2},{1,3},{2,0},{3,1},{4,6},{5,7},{6,4},{7,5},{8,10},{9,11},{10,... | collective-permute-start | bytes 196616 | tf_op jit(solution)/shard_map/ppermute | solution.py:581
  31.1 4.2 %collective-permute-start = (f32[128,128]{1,0:T(8,128)S(1)}, f32[128,128]{1,0:T(8,128)S(1)}, u32[]{:S(2)}, u32[]{:S(2)}) collective-permute-start(f32[128,128]{1,0:T(8,128)S(1)} %get-tuple-element.45.refs_0_), channel_id=1, source_target_pairs={{0,1},{1,0},{2,3},{3,2},{4,5},{5,4},{6,7},{7,6},{8,9},{9,8},{10,11... | collective-permute-start | bytes 196616 | tf_op jit(solution)/shard_map/ppermute | solution.py:581
  31.4 0.7 copy-start.1
  40.5 1.4 %collective-permute-start.3 = (f32[264,128]{1,0:T(8,128)S(1)}, f32[264,128]{1,0:T(8,128)S(1)}, u32[]{:S(2)}, u32[]{:S(2)}) collective-permute-start(f32[264,128]{1,0:T(8,128)S(1)} %get-tuple-element.53), channel_id=1, source_target_pairs={{0,1},{1,0},{2,3},{3,2},{4,5},{5,4},{6,7},{7,6},{8,9},{9,8},{10,11... | collective-permute-start | bytes 405512 | tf_op jit(solution)/shard_map/ppermute | solution.py:581
  42.0 6.0 %collective-permute-start.4 = (f32[264,128]{1,0:T(8,128)S(1)}, f32[264,128]{1,0:T(8,128)S(1)}, u32[]{:S(2)}, u32[]{:S(2)}) collective-permute-start(f32[264,128]{1,0:T(8,128)S(1)} %get-tuple-element.55.mine), channel_id=1, source_target_pairs={{0,2},{1,3},{2,0},{3,1},{4,6},{5,7},{6,4},{7,5},{8,10},{9,11},{10,... | collective-permute-start | bytes 405512 | tf_op jit(solution)/shard_map/ppermute | solution.py:581
  43.2 3.7 %collective-permute-start.5 = (f32[32,128]{1,0:T(8,128)S(1)}, f32[32,128]{1,0:T(8,128)S(1)}, u32[]{:S(2)}, u32[]{:S(2)}) collective-permute-start(f32[32,128]{1,0:T(8,128)S(1)} %get-tuple-element.58), channel_id=1, source_target_pairs={{0,4},{4,0},{8,12},{12,8},{16,20},{20,16},{24,28},{28,24},{1,5},{5... | collective-permute-start | bytes 49160 | tf_op jit(solution)/shard_map/ppermute | solution.py:697
  48.2 1.4 %collective-permute-start.6 = (f32[264,128]{1,0:T(8,128)S(1)}, f32[264,128]{1,0:T(8,128)S(1)}, u32[]{:S(2)}, u32[]{:S(2)}) collective-permute-start(f32[264,128]{1,0:T(8,128)S(1)} %get-tuple-element.59.gap_mine), channel_id=1, source_target_pairs={{0,1},{1,0},{2,3},{3,2},{4,5},{5,4},{6,7},{7,6},{8,9},{9,8},{10,11... | collective-permute-start | bytes 405512 | tf_op jit(solution)/shard_map/ppermute | solution.py:581
  65.1 1.4 %collective-permute-start.7 = (f32[264,128]{1,0:T(8,128)S(1)}, f32[264,128]{1,0:T(8,128)S(1)}, u32[]{:S(2)}, u32[]{:S(2)}) collective-permute-start(f32[264,128]{1,0:T(8,128)S(1)} %get-tuple-element.63), channel_id=1, source_target_pairs={{0,1},{1,0},{2,3},{3,2},{4,5},{5,4},{6,7},{7,6},{8,9},{9,8},{10,11... | collective-permute-start | bytes 405512 | tf_op jit(solution)/shard_map/ppermute | solution.py:581
  66.6 6.0 %collective-permute-start.8 = (f32[264,128]{1,0:T(8,128)S(1)}, f32[264,128]{1,0:T(8,128)S(1)}, u32[]{:S(2)}, u32[]{:S(2)}) collective-permute-start(f32[264,128]{1,0:T(8,128)S(1)} %get-tuple-element.65.mine), channel_id=1, source_target_pairs={{0,2},{1,3},{2,0},{3,1},{4,6},{5,7},{6,4},{7,5},{8,10},{9,11},{10,... | collective-permute-start | bytes 405512 | tf_op jit(solution)/shard_map/ppermute | solution.py:581
  67.8 3.7 %collective-permute-start.9 = (f32[32,128]{1,0:T(8,128)S(1)}, f32[32,128]{1,0:T(8,128)S(1)}, u32[]{:S(2)}, u32[]{:S(2)}) collective-permute-start(f32[32,128]{1,0:T(8,128)S(1)} %get-tuple-element.67), channel_id=1, source_target_pairs={{0,4},{4,0},{8,12},{12,8},{16,20},{20,16},{24,28},{28,24},{1,5},{5... | collective-permute-start | bytes 49160 | tf_op jit(solution)/shard_map/ppermute | solution.py:697
  72.7 1.4 %collective-permute-start.10 = (f32[264,128]{1,0:T(8,128)S(1)}, f32[264,128]{1,0:T(8,128)S(1)}, u32[]{:S(2)}, u32[]{:S(2)}) collective-permute-start(f32[264,128]{1,0:T(8,128)S(1)} %get-tuple-element.68.gap_mine), channel_id=1, source_target_pairs={{0,1},{1,0},{2,3},{3,2},{4,5},{5,4},{6,7},{7,6},{8,9},{9,8},{10,11... | collective-permute-start | bytes 405512 | tf_op jit(solution)/shard_map/ppermute | solution.py:581
  89.1 1.4 %collective-permute-start.11 = (f32[264,128]{1,0:T(8,128)S(1)}, f32[264,128]{1,0:T(8,128)S(1)}, u32[]{:S(2)}, u32[]{:S(2)}) collective-permute-start(f32[264,128]{1,0:T(8,128)S(1)} %get-tuple-element.73), channel_id=1, source_target_pairs={{0,1},{1,0},{2,3},{3,2},{4,5},{5,4},{6,7},{7,6},{8,9},{9,8},{10,11... | collective-permute-start | bytes 405512 | tf_op jit(solution)/shard_map/ppermute | solution.py:581
  90.5 6.0 %collective-permute-start.12 = (f32[264,128]{1,0:T(8,128)S(1)}, f32[264,128]{1,0:T(8,128)S(1)}, u32[]{:S(2)}, u32[]{:S(2)}) collective-permute-start(f32[264,128]{1,0:T(8,128)S(1)} %shard_map.138.mine), channel_id=1, source_target_pairs={{0,2},{1,3},{2,0},{3,1},{4,6},{5,7},{6,4},{7,5},{8,10},{9,11},{10,... | collective-permute-start | bytes 405512 | tf_op jit(solution)/shard_map/ppermute | solution.py:581
  96.7 1.4 %collective-permute-start.13 = (f32[264,128]{1,0:T(8,128)S(1)}, f32[264,128]{1,0:T(8,128)S(1)}, u32[]{:S(2)}, u32[]{:S(2)}) collective-permute-start(f32[264,128]{1,0:T(8,128)S(1)} %shard_map.139.gap_mine), channel_id=1, source_target_pairs={{0,1},{1,0},{2,3},{3,2},{4,5},{5,4},{6,7},{7,6},{8,9},{9,8},{10,11... | collective-permute-start | bytes 405512 | tf_op jit(solution)/shard_map/ppermute | solution.py:581
